TPU v7x, 128 devices: a whole 4x4x4 slice. The times are simulated.
128 devices in a mesh: train: 16 (over y_lo, z, core), query: 8 (over x, y_hi).
Axes of the slice: x: 4, y: 4 (y_hi: 2, y_lo: 2; y = y_hi * 2 + y_lo), z: 4, core: 2. Of those that a mesh axis runs over, the one named last changes fastest.
Arguments:
- train_losses: float32 [256, 131072], P('train', 'query'), may hold values from 0 to 16
- query_losses: float32 [256, 16384], P('train', 'query'), may hold values from 0 to 16
- chain_slots: int32 [32], replicated, may hold values from 0 to 31, as said below
- doc_lengths: int32 [128], replicated, may hold values from 1 to 4096, 131072 in all
Outputs:
- influence: float32 [128, 16384], P('train', 'query')
Inputs may be any that keep to these rules, and one draw needn't show every extreme that they name: `chain_slots`: every chain appears exactly once. `doc_lengths`: the documents cover all 131072 train tokens in order.
All inputs are finite; a program needn't handle non-finite values.
Results may differ from a plain program's by a relative error of at most 0.00084.
Values may be sent and summed in bfloat16 or wider, within the bound.
No kernel may reach another device: no remote copies, remote signals or barrier semaphores. Data moves between devices by JAX's collectives and lax.ppermute only.
A program may use at most 64 MiB of HBM per device.

v0:
```python
import jax
import jax.numpy as jnp
from jax import lax
from jax.sharding import PartitionSpec as P

DRAWS = 256
CHAINS = 32


epsilon = 1e-06
highest = lax.Precision.HIGHEST


def laid_out(pieces, dim):
    pieces = jnp.moveaxis(pieces, 0, dim)
    shape = pieces.shape
    return pieces.reshape(*shape[:dim], shape[dim] * shape[dim + 1], *shape[dim + 2 :])


def copy_for_each(shard, axis):
    copies = jnp.broadcast_to(shard, (lax.axis_size(axis), *shard.shape))
    return lax.all_to_all(copies, axis, split_axis=0, concat_axis=0, tiled=True)


def gathered_copies(shard, axis, dim):
    return laid_out(copy_for_each(shard, axis), dim)


def split_up(shard, dim, size):
    shape = shard.shape
    pieces = shard.reshape(*shape[:dim], size, shape[dim] // size, *shape[dim + 1 :])
    return jnp.moveaxis(pieces, dim, 0)


def sum_at_owner(shard, axis, dim):
    pieces = split_up(shard, dim, lax.axis_size(axis))
    arrived = lax.all_to_all(pieces, axis, split_axis=0, concat_axis=0, tiled=True)
    return arrived.sum(axis=0)


def row_scale(centered):
    widened = centered.astype(jnp.float32)
    return lax.rsqrt(jnp.sum(widened * widened, axis=0) / (centered.shape[0] - 1) + epsilon)


def deal_columns(block, groups):
    height = block.shape[0]
    width = block.shape[1]
    return block.reshape(height, width // groups, groups).transpose(0, 2, 1).reshape(height, width)


def accumulate(running, centered, positions, query_paired, query_weights, doc_starts, doc_ends):
    row_total = centered.shape[1]
    block_size = min(1024, row_total)
    full_blocks = row_total // block_size

    def add_piece(running_sum, portion, places):
        scales = row_scale(portion)
        covariance = lax.dot_general(
            portion, query_paired, (((0,), (0,)), ((), ())), preferred_element_type=jnp.float32
        )
        correlation = covariance * scales[:, None] * query_weights[None, :] / (DRAWS - 1)
        signed = correlation * jnp.abs(correlation)
        inside = (places[:, None] >= doc_starts[None, :]) & (places[:, None] < doc_ends[None, :])
        member = inside.astype(jnp.float32)
        return running_sum + lax.dot_general(
            member,
            signed,
            (((0,), (0,)), ((), ())),
            precision=highest,
            preferred_element_type=jnp.float32,
        )

    def add_block(block_index, running_sum):
        offset = block_index * block_size
        portion = lax.dynamic_slice_in_dim(centered, offset, block_size, 1)
        places = lax.dynamic_slice_in_dim(positions, offset, block_size, 0)
        return add_piece(running_sum, portion, places)

    running = lax.fori_loop(0, full_blocks, add_block, running)
    return running


def shards(train_losses, query_losses, chain_slots, doc_lengths):
    train_parts = lax.axis_size("train")
    train_rank = lax.axis_index("train")
    tokens_here = train_losses.shape[1]
    piece_rows = tokens_here // train_parts
    query_whole = gathered_copies(query_losses, "train", 0)
    columns_here = query_whole.shape[1]
    query_centered = (query_whole - jnp.sum(query_whole, axis=0)[None, :] / DRAWS).astype(
        jnp.bfloat16
    )
    query_paired = jnp.take(
        query_centered.reshape(CHAINS, DRAWS // CHAINS, columns_here), chain_slots, axis=0
    ).reshape(DRAWS, columns_here)
    query_weights = row_scale(query_paired)
    doc_ends = jnp.cumsum(doc_lengths)
    doc_starts = doc_ends - doc_lengths
    doc_total = doc_lengths.shape[0]
    docs_here = doc_total // train_parts
    running = jnp.zeros((doc_total, columns_here), jnp.float32)
    arrived = lax.all_to_all(
        deal_columns(train_losses, train_parts), "train", split_axis=1, concat_axis=0, tiled=True
    )
    centered_here = (arrived - jnp.sum(arrived, axis=0)[None, :] / DRAWS).astype(jnp.bfloat16)
    portion = lax.all_gather(centered_here, "query", axis=1, tiled=True)
    span_rows = portion.shape[1]
    gathered_index = jnp.arange(span_rows, dtype=jnp.int32)
    places = (
        gathered_index // piece_rows * tokens_here
        + gathered_index % piece_rows * train_parts
        + train_rank
    )
    running = accumulate(
        running, portion, places, query_paired, query_weights, doc_starts, doc_ends
    )
    owned_docs = sum_at_owner(running, "train", 0)
    lengths_here = lax.dynamic_slice_in_dim(
        doc_lengths, train_rank * docs_here, docs_here, 0
    ).astype(jnp.float32)
    return owned_docs / lengths_here[:, None]


def solution(mesh):
    in_specs = (P("train", "query"), P("train", "query"), P(), P())
    out_specs = P("train", "query")
    return jax.shard_map(shards, mesh=mesh, in_specs=in_specs, out_specs=out_specs, check_vma=False)
```

profile of v0, /device:TPU:1, one launch (start us, length us, event | category | flops | bytes accessed | tf_op | source)
XLA Modules:
  0.0 221.5 jit_solution(2497652001487101653)
XLA Ops:
  6.5 5.8 %reshape.82 = f32[16,1024,16]{2,1,0:T(8,128)} reshape(f32[16,16384]{1,0:T(8,128)} %param.6) | data formatting | bytes 2097152 | tf_op jit(solution)/shard_map/reshape | solution.py:49
  12.4 5.3 %copy.13 = f32[16,16,1024]{2,0,1:T(8,128)S(1)} copy(f32[16,16,1024]{1,2,0:T(8,128)} %bitcast.15) | data formatting | bytes 2097152 | tf_op jit(solution)/shard_map/transpose | solution.py:49
  17.7 22.9 %all_to_all.26 = f32[16,16,1024]{2,0,1:T(8,128)S(1)} all-to-all(f32[16,16,1024]{2,0,1:T(8,128)S(1)} %copy.13), channel_id=1, replica_groups=mesh['train'=16,'query'=8] {'train'}, dimensions={1} | all-to-all | bytes 2097152 | tf_op jit(solution)/shard_map/all_to_all | solution.py:103
  41.6 1.6 broadcast_in_dim.49
  43.2 4.8 %all-to-all-start.1 = ((f32[16,16,2048]{2,1,0:T(8,128)}), f32[16,16,2048]{2,1,0:T(8,128)S(1)}, u32[]{:S(2)}, u32[]{:S(2)}) async-start(f32[16,16,2048]{2,1,0:T(8,128)} %broadcast_in_dim.49), calls=%async_computation.1 | async-start | bytes 4194304 | tf_op jit(solution)/shard_map/all_to_all | solution.py:22
  48.6 31.9 %all-to-all-done.1 = f32[16,16,2048]{2,1,0:T(8,128)S(1)} async-done(((f32[16,16,2048]{2,1,0:T(8,128)}), f32[16,16,2048]{2,1,0:T(8,128)S(1)}, u32[]{:S(2)}, u32[]{:S(2)}) %all-to-all-start.1) | async-done | bytes 2097184 | tf_op jit(solution)/shard_map/all_to_all | solution.py:22
  82.0 34.3 %all-gather.2.cloned.1.call-done = bf16[256,8192]{1,0:T(8,128)(2,1)} async-done(((bf16[256,1024]{1,0:T(8,128)(2,1)}), bf16[256,8192]{1,0:T(8,128)(2,1)}) %all-gather.2.cloned.1.call-update) | async-done | bytes 4194320 | tf_op jit(solution)/shard_map/all_gather | solution.py:107
  116.3 76.0 %while.14 = (s32[]{:T(128)}, f32[128,2048]{1,0:T(8,128)}, s32[8192]{0:T(1024)S(1)}, s32[128]{0:T(128)S(1)}, s32[128]{0:T(128)S(1)}, /*index=5*/bf16[256,8192]{1,...) while((s32[]{:T(128)}, f32[128,2048]{1,0:T(8,128)}, ...), condition=%wide.region_6.7_spmd.clone, body=%wide.region_4.6_spmd.clone.sunk | while | flops 4307158016 | bytes 29398264 | solution.py:80
  117.6 2.3 %fusion.39 = f32[1024,2048]{1,0:T(8,128)S(1)} fusion(bf16[256,2048]{1,0:T(8,128)(2,1)S(1)} %get-tuple-element.267, bf16[256,8192]{1,0:T(8,128)(2,1)} %get-tuple-element.266, s32[]{:T(128)S(6)} %select_n.61), kind=kOutput, calls=%fused_computation.14.clone.1 | convolution fusion | flops 1073741824 | bytes 9961476 | tf_op jit(solution)/shard_map/while/body/eval_jaxpr/dot_general | solution.py:59
  120.0 4.9 %fusion.40 = f32[128,2048]{1,0:T(8,128)S(1)} fusion(f32[1024,2048]{1,0:T(8,128)S(1)} %fusion.39, f32[2048]{0:T(1024)S(1)} %get-tuple-element.268, f32[1024]{0:T(1024)S(1)} %add_rsqrt_fusion.3, f32[128,2048]{1,0:T(8,128)S(1)} %copy-done, pred[]{:T(512)S(6)} %compare.6, s32[128]{0:T(128)S(1)} %get-tuple-element.265, s32[128]{0:T(128)S(1)} %get-tuple-element.264, ...), kind=kOutput, calls=%fused_computation.9.clone.1 | convolution fusion | flops 3232628736 | bytes 10503169 | tf_op jit(solution)/shard_map/while/body/eval_jaxpr/dot_general | solution.py:66
  125.8 1.3 multiply_reduce_fusion.3
  127.1 2.3 %fusion.39 = f32[1024,2048]{1,0:T(8,128)S(1)} fusion(bf16[256,2048]{1,0:T(8,128)(2,1)S(1)} %get-tuple-element.267, bf16[256,8192]{1,0:T(8,128)(2,1)} %get-tuple-element.266, s32[]{:T(128)S(6)} %select_n.61), kind=kOutput, calls=%fused_computation.14.clone.1 | convolution fusion | flops 1073741824 | bytes 9961476 | tf_op jit(solution)/shard_map/while/body/eval_jaxpr/dot_general | solution.py:59
  129.5 4.9 %fusion.40 = f32[128,2048]{1,0:T(8,128)S(1)} fusion(f32[1024,2048]{1,0:T(8,128)S(1)} %fusion.39, f32[2048]{0:T(1024)S(1)} %get-tuple-element.268, f32[1024]{0:T(1024)S(1)} %add_rsqrt_fusion.3, f32[128,2048]{1,0:T(8,128)S(1)} %copy-done, pred[]{:T(512)S(6)} %compare.6, s32[128]{0:T(128)S(1)} %get-tuple-element.265, s32[128]{0:T(128)S(1)} %get-tuple-element.264, ...), kind=kOutput, calls=%fused_computation.9.clone.1 | convolution fusion | flops 3232628736 | bytes 10503169 | tf_op jit(solution)/shard_map/while/body/eval_jaxpr/dot_general | solution.py:66
  136.6 2.3 %fusion.39 = f32[1024,2048]{1,0:T(8,128)S(1)} fusion(bf16[256,2048]{1,0:T(8,128)(2,1)S(1)} %get-tuple-element.267, bf16[256,8192]{1,0:T(8,128)(2,1)} %get-tuple-element.266, s32[]{:T(128)S(6)} %select_n.61), kind=kOutput, calls=%fused_computation.14.clone.1 | convolution fusion | flops 1073741824 | bytes 9961476 | tf_op jit(solution)/shard_map/while/body/eval_jaxpr/dot_general | solution.py:59
  139.0 4.9 %fusion.40 = f32[128,2048]{1,0:T(8,128)S(1)} fusion(f32[1024,2048]{1,0:T(8,128)S(1)} %fusion.39, f32[2048]{0:T(1024)S(1)} %get-tuple-element.268, f32[1024]{0:T(1024)S(1)} %add_rsqrt_fusion.3, f32[128,2048]{1,0:T(8,128)S(1)} %copy-done, pred[]{:T(512)S(6)} %compare.6, s32[128]{0:T(128)S(1)} %get-tuple-element.265, s32[128]{0:T(128)S(1)} %get-tuple-element.264, ...), kind=kOutput, calls=%fused_computation.9.clone.1 | convolution fusion | flops 3232628736 | bytes 10503169 | tf_op jit(solution)/shard_map/while/body/eval_jaxpr/dot_general | solution.py:66
  144.8 1.3 multiply_reduce_fusion.3
  146.1 2.3 %fusion.39 = f32[1024,2048]{1,0:T(8,128)S(1)} fusion(bf16[256,2048]{1,0:T(8,128)(2,1)S(1)} %get-tuple-element.267, bf16[256,8192]{1,0:T(8,128)(2,1)} %get-tuple-element.266, s32[]{:T(128)S(6)} %select_n.61), kind=kOutput, calls=%fused_computation.14.clone.1 | convolution fusion | flops 1073741824 | bytes 9961476 | tf_op jit(solution)/shard_map/while/body/eval_jaxpr/dot_general | solution.py:59
  148.5 4.9 %fusion.40 = f32[128,2048]{1,0:T(8,128)S(1)} fusion(f32[1024,2048]{1,0:T(8,128)S(1)} %fusion.39, f32[2048]{0:T(1024)S(1)} %get-tuple-element.268, f32[1024]{0:T(1024)S(1)} %add_rsqrt_fusion.3, f32[128,2048]{1,0:T(8,128)S(1)} %copy-done, pred[]{:T(512)S(6)} %compare.6, s32[128]{0:T(128)S(1)} %get-tuple-element.265, s32[128]{0:T(128)S(1)} %get-tuple-element.264, ...), kind=kOutput, calls=%fused_computation.9.clone.1 | convolution fusion | flops 3232628736 | bytes 10503169 | tf_op jit(solution)/shard_map/while/body/eval_jaxpr/dot_general | solution.py:66
  154.3 1.3 multiply_reduce_fusion.3
  155.6 2.3 %fusion.39 = f32[1024,2048]{1,0:T(8,128)S(1)} fusion(bf16[256,2048]{1,0:T(8,128)(2,1)S(1)} %get-tuple-element.267, bf16[256,8192]{1,0:T(8,128)(2,1)} %get-tuple-element.266, s32[]{:T(128)S(6)} %select_n.61), kind=kOutput, calls=%fused_computation.14.clone.1 | convolution fusion | flops 1073741824 | bytes 9961476 | tf_op jit(solution)/shard_map/while/body/eval_jaxpr/dot_general | solution.py:59
  158.0 4.9 %fusion.40 = f32[128,2048]{1,0:T(8,128)S(1)} fusion(f32[1024,2048]{1,0:T(8,128)S(1)} %fusion.39, f32[2048]{0:T(1024)S(1)} %get-tuple-element.268, f32[1024]{0:T(1024)S(1)} %add_rsqrt_fusion.3, f32[128,2048]{1,0:T(8,128)S(1)} %copy-done, pred[]{:T(512)S(6)} %compare.6, s32[128]{0:T(128)S(1)} %get-tuple-element.265, s32[128]{0:T(128)S(1)} %get-tuple-element.264, ...), kind=kOutput, calls=%fused_computation.9.clone.1 | convolution fusion | flops 3232628736 | bytes 10503169 | tf_op jit(solution)/shard_map/while/body/eval_jaxpr/dot_general | solution.py:66
  163.8 1.3 multiply_reduce_fusion.3
  165.1 2.3 %fusion.39 = f32[1024,2048]{1,0:T(8,128)S(1)} fusion(bf16[256,2048]{1,0:T(8,128)(2,1)S(1)} %get-tuple-element.267, bf16[256,8192]{1,0:T(8,128)(2,1)} %get-tuple-element.266, s32[]{:T(128)S(6)} %select_n.61), kind=kOutput, calls=%fused_computation.14.clone.1 | convolution fusion | flops 1073741824 | bytes 9961476 | tf_op jit(solution)/shard_map/while/body/eval_jaxpr/dot_general | solution.py:59
  167.5 4.9 %fusion.40 = f32[128,2048]{1,0:T(8,128)S(1)} fusion(f32[1024,2048]{1,0:T(8,128)S(1)} %fusion.39, f32[2048]{0:T(1024)S(1)} %get-tuple-element.268, f32[1024]{0:T(1024)S(1)} %add_rsqrt_fusion.3, f32[128,2048]{1,0:T(8,128)S(1)} %copy-done, pred[]{:T(512)S(6)} %compare.6, s32[128]{0:T(128)S(1)} %get-tuple-element.265, s32[128]{0:T(128)S(1)} %get-tuple-element.264, ...), kind=kOutput, calls=%fused_computation.9.clone.1 | convolution fusion | flops 3232628736 | bytes 10503169 | tf_op jit(solution)/shard_map/while/body/eval_jaxpr/dot_general | solution.py:66
  173.3 1.3 multiply_reduce_fusion.3
  174.6 2.3 %fusion.39 = f32[1024,2048]{1,0:T(8,128)S(1)} fusion(bf16[256,2048]{1,0:T(8,128)(2,1)S(1)} %get-tuple-element.267, bf16[256,8192]{1,0:T(8,128)(2,1)} %get-tuple-element.266, s32[]{:T(128)S(6)} %select_n.61), kind=kOutput, calls=%fused_computation.14.clone.1 | convolution fusion | flops 1073741824 | bytes 9961476 | tf_op jit(solution)/shard_map/while/body/eval_jaxpr/dot_general | solution.py:59
  177.0 4.9 %fusion.40 = f32[128,2048]{1,0:T(8,128)S(1)} fusion(f32[1024,2048]{1,0:T(8,128)S(1)} %fusion.39, f32[2048]{0:T(1024)S(1)} %get-tuple-element.268, f32[1024]{0:T(1024)S(1)} %add_rsqrt_fusion.3, f32[128,2048]{1,0:T(8,128)S(1)} %copy-done, pred[]{:T(512)S(6)} %compare.6, s32[128]{0:T(128)S(1)} %get-tuple-element.265, s32[128]{0:T(128)S(1)} %get-tuple-element.264, ...), kind=kOutput, calls=%fused_computation.9.clone.1 | convolution fusion | flops 3232628736 | bytes 10503169 | tf_op jit(solution)/shard_map/while/body/eval_jaxpr/dot_general | solution.py:66
  182.8 1.3 multiply_reduce_fusion.3
  184.1 2.3 %fusion.39 = f32[1024,2048]{1,0:T(8,128)S(1)} fusion(bf16[256,2048]{1,0:T(8,128)(2,1)S(1)} %get-tuple-element.267, bf16[256,8192]{1,0:T(8,128)(2,1)} %get-tuple-element.266, s32[]{:T(128)S(6)} %select_n.61), kind=kOutput, calls=%fused_computation.14.clone.1 | convolution fusion | flops 1073741824 | bytes 9961476 | tf_op jit(solution)/shard_map/while/body/eval_jaxpr/dot_general | solution.py:59
  186.5 4.9 %fusion.40 = f32[128,2048]{1,0:T(8,128)S(1)} fusion(f32[1024,2048]{1,0:T(8,128)S(1)} %fusion.39, f32[2048]{0:T(1024)S(1)} %get-tuple-element.268, f32[1024]{0:T(1024)S(1)} %add_rsqrt_fusion.3, f32[128,2048]{1,0:T(8,128)S(1)} %copy-done, pred[]{:T(512)S(6)} %compare.6, s32[128]{0:T(128)S(1)} %get-tuple-element.265, s32[128]{0:T(128)S(1)} %get-tuple-element.264, ...), kind=kOutput, calls=%fused_computation.9.clone.1 | convolution fusion | flops 3232628736 | bytes 10503169 | tf_op jit(solution)/shard_map/while/body/eval_jaxpr/dot_general | solution.py:66
  192.3 5.9 %all-to-all-start.2 = ((f32[16,8,2048]{2,1,0:T(8,128)}), f32[16,8,2048]{2,1,0:T(8,128)S(1)}, u32[]{:S(2)}, u32[]{:S(2)}) async-start(f32[16,8,2048]{2,1,0:T(8,128)} %bitcast.17), calls=%async_computation.2 | async-start | bytes 2097152 | tf_op jit(solution)/shard_map/all_to_all | solution.py:37
  198.3 15.6 %all-to-all-done.2 = f32[16,8,2048]{2,1,0:T(8,128)S(1)} async-done(((f32[16,8,2048]{2,1,0:T(8,128)}), f32[16,8,2048]{2,1,0:T(8,128)S(1)}, u32[]{:S(2)}, u32[]{:S(2)}) %all-to-all-start.2) | async-done | bytes 1048608 | tf_op jit(solution)/shard_map/all_to_all | solution.py:37
  (82 shorter events, 14.5 us)
Async XLA Ops:
  6.5 109.8 %all-gather.2.cloned.1.call-start = ((), (), s32[]{:S(2)}) async-start(), calls=%async_computation.3 | async-start | bytes 4718592 | tf_op jit(solution)/shard_map/all_gather | solution.py:107
  12.4 29.2 %copy-start.2 = (f32[16,2048]{1,0:T(8,128)S(1)}, f32[16,2048]{1,0:T(8,128)}, u32[]{:S(2)}) copy-start(f32[16,2048]{1,0:T(8,128)} %param.7) | copy-start | bytes 393220
  12.4 35.6 %copy-start.4 = (s32[32]{0:T(128)S(1)}, s32[32]{0:T(128)}, u32[]{:S(2)}) copy-start(s32[32]{0:T(128)} %param.8) | copy-start | bytes 388
  12.4 35.8 %copy-start.3 = (s32[128]{0:T(128)S(1)}, s32[128]{0:T(128)}, u32[]{:S(2)}) copy-start(s32[128]{0:T(128)} %param.9) | copy-start | bytes 1540
  43.2 37.4 %all-to-all-start.1 = ((f32[16,16,2048]{2,1,0:T(8,128)}), f32[16,16,2048]{2,1,0:T(8,128)S(1)}, u32[]{:S(2)}, u32[]{:S(2)}) async-start(f32[16,16,2048]{2,1,0:T(8,128)} %broadcast_in_dim.49), calls=%async_computation.1 | async-start | bytes 4194304 | tf_op jit(solution)/shard_map/all_to_all | solution.py:22
  116.3 3.6 %copy-start = (f32[128,2048]{1,0:T(8,128)S(1)}, f32[128,2048]{1,0:T(8,128)}, u32[]{:S(2)}) copy-start(f32[128,2048]{1,0:T(8,128)} %get-tuple-element.250) | copy-start | bytes 3145732 | tf_op jit(solution)/shard_map/while
  124.8 1.0 copy-start.1
  125.8 3.6 %copy-start = (f32[128,2048]{1,0:T(8,128)S(1)}, f32[128,2048]{1,0:T(8,128)}, u32[]{:S(2)}) copy-start(f32[128,2048]{1,0:T(8,128)} %get-tuple-element.250) | copy-start | bytes 3145732 | tf_op jit(solution)/shard_map/while
  134.3 1.0 copy-start.1
  135.3 3.6 %copy-start = (f32[128,2048]{1,0:T(8,128)S(1)}, f32[128,2048]{1,0:T(8,128)}, u32[]{:S(2)}) copy-start(f32[128,2048]{1,0:T(8,128)} %get-tuple-element.250) | copy-start | bytes 3145732 | tf_op jit(solution)/shard_map/while
  143.8 1.0 copy-start.1
  144.8 3.6 %copy-start = (f32[128,2048]{1,0:T(8,128)S(1)}, f32[128,2048]{1,0:T(8,128)}, u32[]{:S(2)}) copy-start(f32[128,2048]{1,0:T(8,128)} %get-tuple-element.250) | copy-start | bytes 3145732 | tf_op jit(solution)/shard_map/while
  153.3 1.0 copy-start.1
  154.3 3.6 %copy-start = (f32[128,2048]{1,0:T(8,128)S(1)}, f32[128,2048]{1,0:T(8,128)}, u32[]{:S(2)}) copy-start(f32[128,2048]{1,0:T(8,128)} %get-tuple-element.250) | copy-start | bytes 3145732 | tf_op jit(solution)/shard_map/while
  162.8 1.0 copy-start.1
  163.8 3.6 %copy-start = (f32[128,2048]{1,0:T(8,128)S(1)}, f32[128,2048]{1,0:T(8,128)}, u32[]{:S(2)}) copy-start(f32[128,2048]{1,0:T(8,128)} %get-tuple-element.250) | copy-start | bytes 3145732 | tf_op jit(solution)/shard_map/while
  172.3 1.0 copy-start.1
  173.3 3.6 %copy-start = (f32[128,2048]{1,0:T(8,128)S(1)}, f32[128,2048]{1,0:T(8,128)}, u32[]{:S(2)}) copy-start(f32[128,2048]{1,0:T(8,128)} %get-tuple-element.250) | copy-start | bytes 3145732 | tf_op jit(solution)/shard_map/while
  181.8 1.0 copy-start.1
  182.8 3.6 %copy-start = (f32[128,2048]{1,0:T(8,128)S(1)}, f32[128,2048]{1,0:T(8,128)}, u32[]{:S(2)}) copy-start(f32[128,2048]{1,0:T(8,128)} %get-tuple-element.250) | copy-start | bytes 3145732 | tf_op jit(solution)/shard_map/while
  191.3 1.0 copy-start.1
  192.3 21.5 %all-to-all-start.2 = ((f32[16,8,2048]{2,1,0:T(8,128)}), f32[16,8,2048]{2,1,0:T(8,128)S(1)}, u32[]{:S(2)}, u32[]{:S(2)}) async-start(f32[16,8,2048]{2,1,0:T(8,128)} %bitcast.17), calls=%async_computation.2 | async-start | bytes 2097152 | tf_op jit(solution)/shard_map/all_to_all | solution.py:37
Sparse Core Ops, SparseCore 0:
  41.7 74.5 all-gather.1
where the time goes:
time: 222 us; the launch traced here: 221 us
  waiting for transfers between devices  81.9 us (37%)
  matrix products  57.6 us (26%)
  blocking collectives  22.9 us (10%)
  local copies, waits for them, and re-layouts  21.6 us (10%)
  between operations  13.5 us (6%)
  other arithmetic  13 us (6%)
  starting transfers between devices  10.6 us (5%)
    dot_general x8, matrix products, add_piece(): lax.dot_general(member, signed, (((0,), (0,)), ((), ())), precision=highe...  38.9 us
    all_gather x1, waiting for transfers between devices, shards(): portion = lax.all_gather(centered_here, 'query', axis=1, tiled=True)  34.3 us
    all_to_all x1, waiting for transfers between devices, copy_for_each(): return lax.all_to_all(copies, axis, split_axis=0, concat_axis=0, tiled=True)  31.9 us
    all_to_all x1, blocking collectives, shards(): lax.all_to_all(deal_columns(train_losses, train_parts), 'train', split_ax...  22.9 us
    dot_general x8, matrix products, add_piece(): lax.dot_general(portion, query_paired, (((0,), (0,)), ((), ())), preferre...  18.7 us
    all_to_all x1, waiting for transfers between devices, sum_at_owner(): lax.all_to_all(pieces, axis, split_axis=0, concat_axis=0, tiled=True)  15.6 us
    reduce_sum x9, other arithmetic, row_scale(): jnp.sum(widened * widened, axis=0) / (centered.shape[0] - 1) + epsilon  10.4 us
    while x32, local copies, waits for them, and re-layouts  8.01 us
  transfers between devices with their start and end apart: 3, of which 3 were waited for; matrix products, arithmetic and copies ran while one was open for 2% of the time, Pallas kernels for 0%

commit v1 on v0

v1 whole, which is shorter than its diff:
```python
import jax
import jax.numpy as jnp
from jax import lax
from jax.experimental import pallas as pl
from jax.experimental.pallas import tpu as pltpu
from jax.sharding import Mesh
from jax.sharding import PartitionSpec as P

DRAWS = 256
CHAINS = 32
PER_CHAIN = DRAWS // CHAINS
EPS = 1e-06
DOCS = 128
DOC_OWN = 8
RUN = 1024
QPIECE = 128
TILE = 256
NBLK = 256
NTILE = 1024
NQ_HERE = 4096
NT_HERE = 4096

f32 = jnp.float32
bf16 = jnp.bfloat16


def params(mib=48):
    return pltpu.CompilerParams(vmem_limit_bytes=mib * 1024 * 1024)


def pack_body(train_ref, query_ref, out_ref):
    out_ref[0, :, :RUN] = train_ref[...]
    out_ref[0, :, RUN:] = query_ref[...]


def pack(train, query):
    rows = train.shape[0]
    return pl.pallas_call(
        pack_body,
        grid=(16,),
        in_specs=[
            pl.BlockSpec((rows, RUN), lambda i: (0, i)),
            pl.BlockSpec((rows, QPIECE), lambda i: (0, i)),
        ],
        out_specs=pl.BlockSpec((1, rows, RUN + QPIECE), lambda i: (i, 0, 0)),
        out_shape=jax.ShapeDtypeStruct((16, rows, RUN + QPIECE), f32),
        name="pack",
    )(train, query)


def centre_body(slots_ref, arr_ref, lo_ref, hi_ref, q_ref, qc_ref, qp_ref):
    def centred(j):
        block = arr_ref[:, :, j * 128 : (j + 1) * 128].reshape(DRAWS, 128)
        mean = jnp.sum(block, axis=0, keepdims=True) / DRAWS
        return (block - mean).astype(bf16).astype(f32)

    qc_ref[...] = centred(RUN // 128).reshape(CHAINS, PER_CHAIN, 128)
    for s in range(CHAINS):
        qp_ref[s] = qc_ref[slots_ref[s]]
    q_ref[...] = qp_ref[...].reshape(DRAWS, 128).astype(bf16)
    half = RUN // 2
    for j in range(RUN // 128):
        c = centred(j)
        scale = lax.rsqrt(jnp.sum(c * c, axis=0, keepdims=True) / (DRAWS - 1) + EPS)
        u = (c * scale).T.astype(bf16)
        ref = lo_ref if j * 128 < half else hi_ref
        o = j * 128 % half
        ref[o : o + 128, :] = u


def centre(slots, arr):
    half = jax.ShapeDtypeStruct((RUN // 2, DRAWS), bf16)
    return pl.pallas_call(
        centre_body,
        in_specs=[
            pl.BlockSpec(memory_space=pltpu.SMEM),
            pl.BlockSpec(memory_space=pltpu.VMEM),
        ],
        out_shape=(half, half, jax.ShapeDtypeStruct((DRAWS, QPIECE), bf16)),
        out_specs=[pl.BlockSpec(memory_space=pltpu.VMEM)] * 3,
        scratch_shapes=[
            pltpu.VMEM((CHAINS, PER_CHAIN, 128), f32),
            pltpu.VMEM((CHAINS, PER_CHAIN, 128), f32),
        ],
        compiler_params=params(),
        name="centre",
    )(slots, arr)


def pool_body(
    core_ref, bases_ref, starts_ref, ends_ref, first_ref, last_ref,
    t0, t1, t2, t3, t4, t5, t6, t7, qa_ref, qb_ref,
    send_ref, keep_ref,
    tok, qs, acc, tile_s, sem,
):
    core = core_ref[0]
    copies = []
    half = RUN // 2
    for i, t in enumerate((t0, t1, t2, t3, t4, t5, t6, t7)):
        copies.append(pltpu.make_async_copy(t, tok.at[pl.ds(i * half, half), :], sem))
    for i in range(16):
        ylz, yh = i // 2, i % 2
        for ref, c in ((qa_ref, core), (qb_ref, 1 - core)):
            col = pl.multiple_of((yh * 16 + ylz * 2 + c) * QPIECE, QPIECE)
            copies.append(pltpu.make_async_copy(ref.at[i], qs.at[:, pl.ds(col, QPIECE)], sem))
    for copy in copies:
        copy.start()
    acc[...] = jnp.zeros_like(acc)
    for copy in copies:
        copy.wait()

    def row_of(k):
        owner = k // DOC_OWN
        keep = jnp.where(owner % 2 == core, 1, 0)
        return keep * (DOCS // 2) + owner // 2 * DOC_OWN + k % DOC_OWN

    @pl.loop(0, NQ_HERE // NTILE)
    def _(n):
        cols = pl.multiple_of(n * NTILE, NTILE)

        @pl.loop(0, NT_HERE // TILE)
        def _(i):
            rows = pl.multiple_of(i * TILE, TILE)
            first = first_ref[i]
            last = last_ref[i]

            @pl.when(first == last)
            def _():
                lhs = tok[pl.ds(rows, TILE), :]
                row = row_of(first)
                for b in range(NTILE // NBLK):
                    where = pl.ds(cols + b * NBLK, NBLK)
                    s = jnp.dot(lhs, qs[:, where], preferred_element_type=f32)
                    total = jnp.sum(s * jnp.abs(s), axis=0, keepdims=True)
                    acc[pl.ds(row, 1), where] += total

            @pl.when(first != last)
            def _():
                lhs = tok[pl.ds(rows, TILE), :]
                for b in range(NTILE // NBLK):
                    tile_s[:, b * NBLK : (b + 1) * NBLK] = jnp.dot(
                        lhs, qs[:, pl.ds(cols + b * NBLK, NBLK)], preferred_element_type=f32
                    )
                base = bases_ref[i]

                def one_doc(k, _):
                    begin = jnp.maximum(starts_ref[k] - base, 0)
                    end = jnp.minimum(ends_ref[k] - base, TILE)

                    def one_group(g, total):
                        o = pl.multiple_of(g * 8, 8)
                        s = tile_s[pl.ds(o, 8), :]
                        at = lax.broadcasted_iota(jnp.int32, s.shape, 0) + o
                        inside = (at >= begin) & (at < end)
                        return total + jnp.where(inside, s * jnp.abs(s), 0.0)

                    total = lax.fori_loop(
                        begin // 8, (end + 7) // 8, one_group, jnp.zeros((8, NTILE), f32)
                    )
                    acc[pl.ds(row_of(k), 1), pl.ds(cols, NTILE)] += jnp.sum(
                        total, axis=0, keepdims=True
                    )
                    return 0

                lax.fori_loop(first, last + 1, one_doc, 0)

    send_ref[...] = acc[: DOCS // 2, :]
    keep_ref[...] = acc[DOCS // 2 :, :]


def pool(core, bases, starts, ends, first, last, tokens, qa, qb):
    smem = pl.BlockSpec(memory_space=pltpu.SMEM)
    anyspace = pl.BlockSpec(memory_space=pl.ANY)
    out = jax.ShapeDtypeStruct((DOCS // 2, NQ_HERE), f32)
    return pl.pallas_call(
        pool_body,
        in_specs=[smem] * 6 + [anyspace] * 10,
        out_shape=(out, out),
        out_specs=[pl.BlockSpec(memory_space=pltpu.VMEM)] * 2,
        scratch_shapes=[
            pltpu.VMEM((NT_HERE, DRAWS), bf16),
            pltpu.VMEM((DRAWS, NQ_HERE), bf16),
            pltpu.VMEM((DOCS, NQ_HERE), f32),
            pltpu.VMEM((TILE, NTILE), f32),
            pltpu.SemaphoreType.DMA,
        ],
        compiler_params=params(),
        cost_estimate=pl.CostEstimate(
            flops=2 * NT_HERE * NQ_HERE * DRAWS, bytes_accessed=6 << 20, transcendentals=0
        ),
        name="pool",
    )(core, bases, starts, ends, first, last, *tokens, qa, qb)


def finish_body(pieces_ref, q_ref, len_ref, out_ref):
    total = pieces_ref[0]
    for i in range(1, 16):
        total = total + pieces_ref[i]
    q = q_ref[...].astype(f32)
    scale = lax.rsqrt(jnp.sum(q * q, axis=0, keepdims=True) / (DRAWS - 1) + EPS) / (DRAWS - 1)
    out_ref[...] = total * (scale * scale) / len_ref[...]


def shift(value, axis, by):
    size = lax.axis_size(axis)
    return lax.ppermute(value, axis, [(i, (i + by) % size) for i in range(size)])


def shards(train_losses, query_losses, chain_slots, doc_lengths):
    core = lax.axis_index("c")
    yh = lax.axis_index("yh")
    x = lax.axis_index("x")
    t = (lax.axis_index("yl") * 4 + lax.axis_index("z")) * 2 + core

    doc_ends = jnp.cumsum(doc_lengths)
    doc_starts = doc_ends - doc_lengths

    packed = pack(train_losses, query_losses)
    arrived = lax.all_to_all(packed, ("yl", "z", "c"), split_axis=0, concat_axis=0, tiled=True)
    lo, hi, q_own = centre(chain_slots, arrived)

    left_lo = shift(lo, "x", 1)
    right_hi = shift(hi, "x", -1)
    left_hi = shift(hi, "x", 1)
    right_lo = shift(lo, "x", -1)
    far_lo = shift(left_lo, "x", 1)
    far_hi = shift(right_hi, "x", -1)

    qa = lax.all_to_all(
        jnp.broadcast_to(q_own, (16, *q_own.shape)), ("yl", "z", "yh"),
        split_axis=0, concat_axis=0, tiled=True,
    )
    qb = shift(qa, "c", 1)

    xs = jnp.stack([x, (x + 3) % 4, (x + 1) % 4, (x + 2) % 4])
    run_bases = (xs * 2 + yh) * (16 * RUN) + t * RUN
    bases = (run_bases[:, None] + jnp.arange(RUN // TILE, dtype=jnp.int32) * TILE).reshape(-1)
    first = jnp.sum(doc_ends[None, :] <= bases[:, None], axis=1, dtype=jnp.int32)
    last = jnp.sum(doc_ends[None, :] <= bases[:, None] + (TILE - 1), axis=1, dtype=jnp.int32)

    send, keep = pool(
        core.reshape(1), bases, doc_starts, doc_ends, first, last,
        (lo, hi, left_lo, left_hi, right_lo, right_hi, far_lo, far_hi), qa, qb,
    )
    other = shift(send, "c", 1)
    half = (keep + other).reshape(8, DOC_OWN, 2, 2048).transpose(0, 2, 1, 3)
    pieces = lax.all_to_all(
        half.reshape(16, DOC_OWN, 2048), ("yl", "z", "yh"), split_axis=0, concat_axis=0, tiled=True
    )

    mine = lax.dynamic_index_in_dim(qa.reshape(8, 2, DRAWS, QPIECE), yh, 1, keepdims=False)
    theirs = lax.dynamic_index_in_dim(qb.reshape(8, 2, DRAWS, QPIECE), yh, 1, keepdims=False)
    both = jnp.where(core == 0, jnp.stack([mine, theirs], 1), jnp.stack([theirs, mine], 1))
    q_mine = both.transpose(2, 0, 1, 3).reshape(DRAWS, 2048)
    lengths = lax.dynamic_slice_in_dim(doc_lengths, t * DOC_OWN, DOC_OWN, 0).astype(f32)
    return pl.pallas_call(
        finish_body,
        out_shape=jax.ShapeDtypeStruct((DOC_OWN, 2048), f32),
        compiler_params=params(),
        name="finish",
    )(pieces, q_mine, lengths[:, None])


def solution(mesh):
    fine = Mesh(mesh.devices.reshape(2, 4, 2, 4, 2), ("yl", "z", "c", "x", "yh"))
    split = P(("yl", "z", "c"), ("x", "yh"))
    return jax.shard_map(
        shards, mesh=fine, in_specs=(split, split, P(), P()), out_specs=split, check_vma=False
    )
```

time: 222 us -> 139 us (0.63)
  waiting for transfers between devices: 81.9 us -> 19.4 us
  matrix products: 57.6 us -> 0 us
  Pallas kernels: 0 us -> 37.2 us
  blocking collectives: 22.9 us -> 45.1 us
  local copies, waits for them, and re-layouts: 21.6 us -> 5.41 us
  starting transfers between devices: 10.6 us -> 24.2 us
  between operations: 13.5 us -> 0.12 us
  other arithmetic: 13 us -> 7.18 us
    dot_general x16 -> x0, matrix products: 57.6 us -> none  [the longest x8 38.9 us: add_piece(): lax.dot_general(member, signed, (((0,), (0,)), ((), ())), precision=highe...]
    all_to_all x2 -> x1, waiting for transfers between devices: 47.5 us -> 5.75 us  [shards(): lax.all_to_all(half.reshape(16, DOC_OWN, 2048), ('yl', 'z', 'yh'), split_...]
    pallas_call x0 -> x4, Pallas kernels: none -> 37.2 us  [the longest x1 26.6 us: pool(): pl.pallas_call(pool_body, in_specs=[smem] * 6 + [anyspace] * 10, out_shap...]
    all_gather x1 -> x0, waiting for transfers between devices: 34.3 us -> none  [shards(): portion = lax.all_gather(centered_here, 'query', axis=1, tiled=True)]
    all_to_all x1 -> x2, blocking collectives: 22.9 us -> 45.1 us  [the longest x1 25.3 us: shards(): lax.all_to_all(packed, ('yl', 'z', 'c'), split_axis=0, concat_axis=0, til...]
    ppermute x0 -> x8, waiting for transfers between devices: none -> 13.7 us  [shift(): lax.ppermute(value, axis, [(i, (i + by) % size) for i in range(size)])]
    ppermute x0 -> x8, starting transfers between devices: none -> 13.1 us  [shift(): lax.ppermute(value, axis, [(i, (i + by) % size) for i in range(size)])]
    reduce_sum x12 -> x1, other arithmetic: 10.6 us -> 0.18 us  [shards(): jnp.sum(doc_ends[None, :] <= bases[:, None] + (TILE - 1), axis=1, dtype=j...]
  transfers between devices with their start and end apart: 3 -> 9, of which waited for: 3 -> 5; matrix products, arithmetic and copies ran while one was open for 2% -> 7% of each run, Pallas kernels for 0% -> 0%
where the time goes in v1:
time: 139 us
  blocking collectives  45.1 us (32%)
  Pallas kernels  37.2 us (27%)
  starting transfers between devices  24.2 us (17%)
  waiting for transfers between devices  19.4 us (14%)
  other arithmetic  7.18 us (5%)
  local copies, waits for them, and re-layouts  5.41 us (4%)
    pallas_call x1, Pallas kernels, pool(): pl.pallas_call(pool_body, in_specs=[smem] * 6 + [anyspace] * 10, out_shap...  26.6 us
    all_to_all x1, blocking collectives, shards(): lax.all_to_all(packed, ('yl', 'z', 'c'), split_axis=0, concat_axis=0, til...  25.3 us
    all_to_all x1, blocking collectives, shards(): lax.all_to_all(jnp.broadcast_to(q_own, (16, *q_own.shape)), ('yl', 'z', '...  19.8 us
    ppermute x8, waiting for transfers between devices, shift(): lax.ppermute(value, axis, [(i, (i + by) % size) for i in range(size)])  13.7 us
    ppermute x8, starting transfers between devices, shift(): lax.ppermute(value, axis, [(i, (i + by) % size) for i in range(size)])  13.1 us
    all_to_all x1, starting transfers between devices, shards(): lax.all_to_all(half.reshape(16, DOC_OWN, 2048), ('yl', 'z', 'yh'), split_...  11 us
    pallas_call x1, Pallas kernels, pack(): pl.pallas_call(pack_body, grid=(16,), in_specs=[pl.BlockSpec((rows, RUN),...  8.85 us
    all_to_all x1, waiting for transfers between devices, shards(): lax.all_to_all(half.reshape(16, DOC_OWN, 2048), ('yl', 'z', 'yh'), split_...  5.75 us
  transfers between devices with their start and end apart: 9, of which 5 were waited for; matrix products, arithmetic and copies ran while one was open for 7% of the time, Pallas kernels for 0%

profile of v1, /device:TPU:1, one launch (start us, length us, event | category | flops | bytes accessed | tf_op | source)
XLA Modules:
  0.0 138.6 jit_solution(12642665815062927507)
XLA Ops:
  0.0 8.9 %pack.1 = f32[16,16,1152]{2,1,0:T(8,128)} custom-call(f32[16,16384]{1,0:T(8,128)} %train_ref.1, f32[16,2048]{1,0:T(8,128)} %query_ref.1), custom_call_target="tpu_custom_call" | custom-call | tf_op jit(solution)/shard_map/pack/pallas_call | solution.py:38
  8.9 25.3 %all_to_all.15.arr_ref = f32[16,16,1152]{2,1,0:T(8,128)S(1)} all-to-all(f32[16,16,1152]{2,1,0:T(8,128)} %pack.1), channel_id=1, replica_groups=mesh['yl'=2,'z'=4,'c'=2,'x'=4,'yh'=2] {'yl','z','c'}, dimensions={0} | all-to-all | bytes 2359296 | tf_op jit(solution)/shard_map/all_to_all | solution.py:219
  34.2 1.0 centre.1
  35.2 0.2 broadcast_in_dim.4
  35.4 19.8 %all_to_all.16.qa_ref = bf16[16,256,128]{2,1,0:T(8,128)(2,1)S(1)} all-to-all(bf16[16,256,128]{2,1,0:T(8,128)(2,1)S(1)} %broadcast_in_dim.4), channel_id=1, replica_groups=mesh['yl'=2,'z'=4,'c'=2,'x'=4,'yh'=2] {'yl','z','yh'}, dimensions={0} | all-to-all | bytes 2097152 | tf_op jit(solution)/shard_map/all_to_all | solution.py:229
  55.2 2.5 %collective-permute-start.6 = (bf16[16,256,128]{2,1,0:T(8,128)(2,1)S(1)}, bf16[16,256,128]{2,1,0:T(8,128)(2,1)S(1)}, u32[]{:S(2)}, u32[]{:S(2)}) collective-permute-start(bf16[16,256,128]{2,1,0:T(8,128)(2,1)S(1)} %all_to_all.16.qa_ref), channel_id=1, source_target_pairs={{0,8},{8,0},{1,9},{9,1},{2,10},{10,2},{3,11},{11,3},{4,12},{12,4},... | collective-permute-start | bytes 3145736 | tf_op jit(solution)/shard_map/ppermute | solution.py:206
  57.6 1.2 collective-permute-start
  58.9 1.5 %collective-permute-start.3 = (bf16[512,256]{1,0:T(8,128)(2,1)S(1)}, bf16[512,256]{1,0:T(8,128)(2,1)S(1)}, u32[]{:S(2)}, u32[]{:S(2)}) collective-permute-start(bf16[512,256]{1,0:T(8,128)(2,1)S(1)} %get-tuple-element.11.t1), channel_id=1, source_target_pairs={{0,6},{2,0},{4,2},{6,4},{1,7},{3,1},{5,3},{7,5},{8,14},{10,8},{12,... | collective-permute-start | bytes 786440 | tf_op jit(solution)/shard_map/ppermute | solution.py:206
  60.5 0.1 add.104.bases_ref
  60.6 0.1 copy.13
  60.7 0.2 reduce-window.8
  60.9 0.1 reduce.ends_ref
  61.1 2.7 %collective-permute-start.2 = (bf16[512,256]{1,0:T(8,128)(2,1)S(1)}, bf16[512,256]{1,0:T(8,128)(2,1)S(1)}, u32[]{:S(2)}, u32[]{:S(2)}) collective-permute-start(bf16[512,256]{1,0:T(8,128)(2,1)S(1)} %get-tuple-element.10.t0), channel_id=1, source_target_pairs={{0,6},{2,0},{4,2},{6,4},{1,7},{3,1},{5,3},{7,5},{8,14},{10,8},{12,... | collective-permute-start | bytes 786440 | tf_op jit(solution)/shard_map/ppermute | solution.py:206
  63.7 3.0 %collective-permute-done.t2 = bf16[512,256]{1,0:T(8,128)(2,1)S(1)} collective-permute-done((bf16[512,256]{1,0:T(8,128)(2,1)S(1)}, bf16[512,256]{1,0:T(8,128)(2,1)S(1)}, u32[]{:S(2)}, u32[]{:S(2)}) %collective-permute-start) | collective-permute-done | bytes 262176 | tf_op jit(solution)/shard_map/ppermute | solution.py:206
  66.7 2.7 %collective-permute-start.5 = (bf16[512,256]{1,0:T(8,128)(2,1)S(1)}, bf16[512,256]{1,0:T(8,128)(2,1)S(1)}, u32[]{:S(2)}, u32[]{:S(2)}) collective-permute-start(bf16[512,256]{1,0:T(8,128)(2,1)S(1)} %collective-permute-done.3.t5), channel_id=1, source_target_pairs={{0,6},{2,0},{4,2},{6,4},{1,7},{3,1},{5,3},{7,5},{8,14},{10,8},{12,... | collective-permute-start | bytes 786440 | tf_op jit(solution)/shard_map/ppermute | solution.py:206
  69.4 0.2 convert_reduce_fusion
  69.6 2.7 %collective-permute-done.1.t3 = bf16[512,256]{1,0:T(8,128)(2,1)S(1)} collective-permute-done((bf16[512,256]{1,0:T(8,128)(2,1)S(1)}, bf16[512,256]{1,0:T(8,128)(2,1)S(1)}, u32[]{:S(2)}, u32[]{:S(2)}) %collective-permute-start.1) | collective-permute-done | bytes 262176 | tf_op jit(solution)/shard_map/ppermute | solution.py:206
  72.3 5.6 %collective-permute-done.4.t6 = bf16[512,256]{1,0:T(8,128)(2,1)S(1)} collective-permute-done((bf16[512,256]{1,0:T(8,128)(2,1)S(1)}, bf16[512,256]{1,0:T(8,128)(2,1)S(1)}, u32[]{:S(2)}, u32[]{:S(2)}) %collective-permute-start.4) | collective-permute-done | bytes 262176 | tf_op jit(solution)/shard_map/ppermute | solution.py:206
  78.0 1.0 copy-done.1
  79.0 26.6 %pool.1 = (f32[64,4096]{1,0:T(8,128)S(1)}, f32[64,4096]{1,0:T(8,128)S(1)}) custom-call(s32[1]{0:T(128)} %bitcast.core_ref, s32[16]{0:T(128)S(1)} %add.104.bases_ref, s32[128]{0:T(128)S(1)} %sub.3.starts_ref, s32[128]{0:T(128)S(1)} %reduce.ends_ref, s32[16]{0:T(128)S(1)} %get-tuple-element.16.first_ref, s32[16]{0:T(128)S(1)} %get-tuple-element.15.last_ref, ...), custom_call_target="tpu_custom_call" | custom-call | flops 8589934592 | bytes 6291456 | tf_op jit(solution)/shard_map/pool/pallas_call | solution.py:175
  105.6 2.6 %collective-permute-start.7 = (f32[64,4096]{1,0:T(8,128)S(1)}, f32[64,4096]{1,0:T(8,128)S(1)}, u32[]{:S(2)}, u32[]{:S(2)}) collective-permute-start(f32[64,4096]{1,0:T(8,128)S(1)} %get-tuple-element.14), channel_id=1, source_target_pairs={{0,8},{8,0},{1,9},{9,1},{2,10},{10,2},{3,11},{11,3},{4,12},{12,4},... | collective-permute-start | bytes 3145736 | tf_op jit(solution)/shard_map/ppermute | solution.py:206
  108.2 2.3 %collective-permute-done.7 = f32[64,4096]{1,0:T(8,128)S(1)} collective-permute-done((f32[64,4096]{1,0:T(8,128)S(1)}, f32[64,4096]{1,0:T(8,128)S(1)}, u32[]{:S(2)}, u32[]{:S(2)}) %collective-permute-start.7) | collective-permute-done | bytes 1048608 | tf_op jit(solution)/shard_map/ppermute | solution.py:206
  110.4 1.1 add.106
  111.6 11.0 %all-to-all-start.2 = ((f32[16,8,2048]{2,1,0:T(8,128)}), f32[16,8,2048]{2,1,0:T(8,128)S(1)}, u32[]{:S(2)}, u32[]{:S(2)}) async-start(f32[16,8,2048]{2,1,0:T(8,128)} %bitcast.18), calls=%async_computation.2 | async-start | bytes 2097152 | tf_op jit(solution)/shard_map/all_to_all | solution.py:247
  122.7 0.1 copy.16.len_ref
  122.8 0.8 copy.17
  123.7 0.4 copy-done.2
  124.1 0.8 copy.18
  124.9 5.3 %fusion = bf16[256,8,2,128]{3,2,1,0:T(2,128)(2,1)} fusion(pred[]{:T(512)S(6)} %eq.7, bf16[8,1,256,128]{3,1,0,2:T(2,128)(2,1)S(1)} %copy.18, bf16[8,1,256,128]{3,1,0,2:T(2,128)(2,1)S(1)} %copy.17), kind=kLoop, calls=%fused_computation.1 | loop fusion | flops 4718592 | bytes 2097153 | tf_op jit(solution)/shard_map/transpose | solution.py:254
  130.2 1.8 %reshape.116.q_ref = bf16[256,2048]{1,0:T(8,128)(2,1)S(1)} reshape(bf16[256,8,2,128]{3,2,1,0:T(2,128)(2,1)} %fusion) | data formatting | bytes 2097152 | tf_op jit(solution)/shard_map/reshape | solution.py:254
  132.1 5.8 %all-to-all-done.2.pieces_ref = f32[16,8,2048]{2,1,0:T(8,128)S(1)} async-done(((f32[16,8,2048]{2,1,0:T(8,128)}), f32[16,8,2048]{2,1,0:T(8,128)S(1)}, u32[]{:S(2)}, u32[]{:S(2)}) %all-to-all-start.2) | async-done | bytes 1048608 | tf_op jit(solution)/shard_map/all_to_all | solution.py:247
  137.8 0.7 finish.1
  (19 shorter events, 0.4 us)
Async XLA Ops:
  8.9 25.3 %copy-start = (s32[32]{0:T(128)S(1)}, s32[32]{0:T(128)}, u32[]{:S(2)}) copy-start(s32[32]{0:T(128)} %slots_ref.1) | copy-start | bytes 388
  35.4 25.2 %copy-start.3 = (s32[128]{0:T(128)S(1)}, s32[128]{0:T(128)}, u32[]{:S(2)}) copy-start(s32[128]{0:T(128)} %param.7) | copy-start | bytes 1540
  55.2 22.8 %collective-permute-start.6 = (bf16[16,256,128]{2,1,0:T(8,128)(2,1)S(1)}, bf16[16,256,128]{2,1,0:T(8,128)(2,1)S(1)}, u32[]{:S(2)}, u32[]{:S(2)}) collective-permute-start(bf16[16,256,128]{2,1,0:T(8,128)(2,1)S(1)} %all_to_all.16.qa_ref), channel_id=1, source_target_pairs={{0,8},{8,0},{1,9},{9,1},{2,10},{10,2},{3,11},{11,3},{4,12},{12,4},... | collective-permute-start | bytes 3145736 | tf_op jit(solution)/shard_map/ppermute | solution.py:206
  57.6 9.1 %collective-permute-start = (bf16[512,256]{1,0:T(8,128)(2,1)S(1)}, bf16[512,256]{1,0:T(8,128)(2,1)S(1)}, u32[]{:S(2)}, u32[]{:S(2)}) collective-permute-start(bf16[512,256]{1,0:T(8,128)(2,1)S(1)} %get-tuple-element.10.t0), channel_id=1, source_target_pairs={{0,2},{2,4},{4,6},{6,0},{1,3},{3,5},{5,7},{7,1},{8,10},{10,12},{12... | collective-permute-start | bytes 786440 | tf_op jit(solution)/shard_map/ppermute | solution.py:206
  58.9 7.9 %collective-permute-start.3 = (bf16[512,256]{1,0:T(8,128)(2,1)S(1)}, bf16[512,256]{1,0:T(8,128)(2,1)S(1)}, u32[]{:S(2)}, u32[]{:S(2)}) collective-permute-start(bf16[512,256]{1,0:T(8,128)(2,1)S(1)} %get-tuple-element.11.t1), channel_id=1, source_target_pairs={{0,6},{2,0},{4,2},{6,4},{1,7},{3,1},{5,3},{7,5},{8,14},{10,8},{12,... | collective-permute-start | bytes 786440 | tf_op jit(solution)/shard_map/ppermute | solution.py:206
  61.0 11.4 %collective-permute-start.1 = (bf16[512,256]{1,0:T(8,128)(2,1)S(1)}, bf16[512,256]{1,0:T(8,128)(2,1)S(1)}, u32[]{:S(2)}, u32[]{:S(2)}) collective-permute-start(bf16[512,256]{1,0:T(8,128)(2,1)S(1)} %get-tuple-element.11.t1), channel_id=1, source_target_pairs={{0,2},{2,4},{4,6},{6,0},{1,3},{3,5},{5,7},{7,1},{8,10},{10,12},{12... | collective-permute-start | bytes 786440 | tf_op jit(solution)/shard_map/ppermute | solution.py:206
  61.1 11.3 %collective-permute-start.2 = (bf16[512,256]{1,0:T(8,128)(2,1)S(1)}, bf16[512,256]{1,0:T(8,128)(2,1)S(1)}, u32[]{:S(2)}, u32[]{:S(2)}) collective-permute-start(bf16[512,256]{1,0:T(8,128)(2,1)S(1)} %get-tuple-element.10.t0), channel_id=1, source_target_pairs={{0,6},{2,0},{4,2},{6,4},{1,7},{3,1},{5,3},{7,5},{8,14},{10,8},{12,... | collective-permute-start | bytes 786440 | tf_op jit(solution)/shard_map/ppermute | solution.py:206
  66.7 11.2 %collective-permute-start.4 = (bf16[512,256]{1,0:T(8,128)(2,1)S(1)}, bf16[512,256]{1,0:T(8,128)(2,1)S(1)}, u32[]{:S(2)}, u32[]{:S(2)}) collective-permute-start(bf16[512,256]{1,0:T(8,128)(2,1)S(1)} %collective-permute-done.t2), channel_id=1, source_target_pairs={{0,2},{2,4},{4,6},{6,0},{1,3},{3,5},{5,7},{7,1},{8,10},{10,12},{12... | collective-permute-start | bytes 786440 | tf_op jit(solution)/shard_map/ppermute | solution.py:206
  66.7 11.2 %collective-permute-start.5 = (bf16[512,256]{1,0:T(8,128)(2,1)S(1)}, bf16[512,256]{1,0:T(8,128)(2,1)S(1)}, u32[]{:S(2)}, u32[]{:S(2)}) collective-permute-start(bf16[512,256]{1,0:T(8,128)(2,1)S(1)} %collective-permute-done.3.t5), channel_id=1, source_target_pairs={{0,6},{2,0},{4,2},{6,4},{1,7},{3,1},{5,3},{7,5},{8,14},{10,8},{12,... | collective-permute-start | bytes 786440 | tf_op jit(solution)/shard_map/ppermute | solution.py:206
  78.0 1.0 copy-start.1
  105.6 4.9 %collective-permute-start.7 = (f32[64,4096]{1,0:T(8,128)S(1)}, f32[64,4096]{1,0:T(8,128)S(1)}, u32[]{:S(2)}, u32[]{:S(2)}) collective-permute-start(f32[64,4096]{1,0:T(8,128)S(1)} %get-tuple-element.14), channel_id=1, source_target_pairs={{0,8},{8,0},{1,9},{9,1},{2,10},{10,2},{3,11},{11,3},{4,12},{12,4},... | collective-permute-start | bytes 3145736 | tf_op jit(solution)/shard_map/ppermute | solution.py:206
  111.6 26.2 %all-to-all-start.2 = ((f32[16,8,2048]{2,1,0:T(8,128)}), f32[16,8,2048]{2,1,0:T(8,128)S(1)}, u32[]{:S(2)}, u32[]{:S(2)}) async-start(f32[16,8,2048]{2,1,0:T(8,128)} %bitcast.18), calls=%async_computation.2 | async-start | bytes 2097152 | tf_op jit(solution)/shard_map/all_to_all | solution.py:247
  122.8 1.2 copy-start.2

commit v2 on v1

v2 whole, which is shorter than its diff:
```python
import jax
import jax.numpy as jnp
from jax import lax
from jax.experimental import pallas as pl
from jax.experimental.pallas import tpu as pltpu
from jax.sharding import Mesh
from jax.sharding import PartitionSpec as P

DRAWS = 256
CHAINS = 32
PER_CHAIN = DRAWS // CHAINS
EPS = 1e-06
DOCS = 128
DOC_OWN = 8
RUN = 1024
QPIECE = 128
TILE = 256
NBLK = 512
NTILE = 1024
NQ_HERE = 4096
NT_HERE = 4096

f32 = jnp.float32
bf16 = jnp.bfloat16


def params(mib=48):
    return pltpu.CompilerParams(vmem_limit_bytes=mib * 1024 * 1024)


def pack_body(train_ref, query_ref, out_ref):
    for i in range(16):
        out_ref[i, :, :RUN] = train_ref[:, i * RUN : (i + 1) * RUN]
        out_ref[i, :, RUN:] = query_ref[:, i * QPIECE : (i + 1) * QPIECE]


def pack(train, query):
    rows = train.shape[0]
    return pl.pallas_call(
        pack_body,
        in_specs=[pl.BlockSpec(memory_space=pltpu.VMEM)] * 2,
        out_specs=pl.BlockSpec(memory_space=pltpu.VMEM),
        out_shape=jax.ShapeDtypeStruct((16, rows, RUN + QPIECE), f32),
        compiler_params=params(16),
        name="pack",
    )(train, query)


def centre_body(slots_ref, arr_ref, u_ref, q_ref, qc_ref, qp_ref):
    def centred(j):
        block = arr_ref[:, :, j * 128 : (j + 1) * 128].reshape(DRAWS, 128)
        mean = jnp.sum(block, axis=0, keepdims=True) / DRAWS
        return (block - mean).astype(bf16).astype(f32)

    qc_ref[...] = centred(RUN // 128).reshape(CHAINS, PER_CHAIN, 128)
    for s in range(CHAINS):
        qp_ref[s] = qc_ref[slots_ref[s]]
    q_ref[...] = qp_ref[...].reshape(DRAWS, 128).astype(bf16)
    for j in range(RUN // 128):
        c = centred(j)
        scale = lax.rsqrt(jnp.sum(c * c, axis=0, keepdims=True) / (DRAWS - 1) + EPS)
        u_ref[j * 128 : (j + 1) * 128, :] = (c * scale).T.astype(bf16)


def centre(slots, arr):
    return pl.pallas_call(
        centre_body,
        in_specs=[
            pl.BlockSpec(memory_space=pltpu.SMEM),
            pl.BlockSpec(memory_space=pltpu.VMEM),
        ],
        out_shape=(
            jax.ShapeDtypeStruct((RUN, DRAWS), bf16),
            jax.ShapeDtypeStruct((DRAWS, QPIECE), bf16),
        ),
        out_specs=[pl.BlockSpec(memory_space=pltpu.VMEM)] * 2,
        scratch_shapes=[
            pltpu.VMEM((CHAINS, PER_CHAIN, 128), f32),
            pltpu.VMEM((CHAINS, PER_CHAIN, 128), f32),
        ],
        compiler_params=params(16),
        name="centre",
    )(slots, arr)


def pool_body(
    core_ref, bases_ref, starts_ref, ends_ref, first_ref, last_ref,
    own, left, right, far, qa_ref, qb_ref,
    send_ref, keep_ref,
    tok, qs, acc, tile_s,
):
    core = core_ref[0]
    at = 0
    for ref in (own, left, right, far):
        tok[at : at + ref.shape[0], :] = ref[...]
        at += ref.shape[0]
    for i in range(16):
        ylz, yh = i // 2, i % 2
        for ref, c in ((qa_ref, core), (qb_ref, 1 - core)):
            col = pl.multiple_of((yh * 16 + ylz * 2 + c) * QPIECE, QPIECE)
            qs[:, pl.ds(col, QPIECE)] = ref[i]
    acc[...] = jnp.zeros_like(acc)

    def row_of(k):
        owner = k // DOC_OWN
        keep = jnp.where(owner % 2 == core, 1, 0)
        return keep * (DOCS // 2) + owner // 2 * DOC_OWN + k % DOC_OWN

    @pl.loop(0, NT_HERE // TILE)
    def _(i):
        rows = pl.multiple_of(i * TILE, TILE)
        first = first_ref[i]
        last = last_ref[i]
        base = bases_ref[i]

        def products():
            lhs = tok[pl.ds(rows, TILE), :]
            for b in range(NQ_HERE // NBLK):
                where = slice(b * NBLK, (b + 1) * NBLK)
                yield where, jnp.dot(lhs, qs[:, where], preferred_element_type=f32)

        @pl.when(first == last)
        def _():
            row = row_of(first)
            for where, s in products():
                acc[pl.ds(row, 1), where] += jnp.sum(s * jnp.abs(s), axis=0, keepdims=True)

        @pl.when(first + 1 == last)
        def _():
            row = row_of(first)
            row_next = row_of(last)
            border = ends_ref[first] - base
            upper = lax.broadcasted_iota(jnp.int32, (TILE, NBLK), 0) < border
            for where, s in products():
                p = s * jnp.abs(s)
                p_upper = jnp.where(upper, p, 0.0)
                acc[pl.ds(row, 1), where] += jnp.sum(p_upper, axis=0, keepdims=True)
                acc[pl.ds(row_next, 1), where] += jnp.sum(p - p_upper, axis=0, keepdims=True)

        @pl.when(first + 1 < last)
        def _():
            for where, s in products():
                tile_s[:, where] = s

            def one_doc(k, _):
                begin = jnp.maximum(starts_ref[k] - base, 0)
                end = jnp.minimum(ends_ref[k] - base, TILE)
                row = row_of(k)

                @pl.loop(0, NQ_HERE // NTILE)
                def _(n):
                    cols = pl.ds(pl.multiple_of(n * NTILE, NTILE), NTILE)

                    def one_group(g, total):
                        o = pl.multiple_of(g * 8, 8)
                        s = tile_s[pl.ds(o, 8), cols]
                        at = lax.broadcasted_iota(jnp.int32, s.shape, 0) + o
                        inside = (at >= begin) & (at < end)
                        return total + jnp.where(inside, s * jnp.abs(s), 0.0)

                    total = lax.fori_loop(
                        begin // 8, (end + 7) // 8, one_group, jnp.zeros((8, NTILE), f32)
                    )
                    acc[pl.ds(row, 1), cols] += jnp.sum(total, axis=0, keepdims=True)

                return 0

            lax.fori_loop(first, last + 1, one_doc, 0)

    send_ref[...] = acc[: DOCS // 2, :]
    keep_ref[...] = acc[DOCS // 2 :, :]


def pool(core, bases, starts, ends, first, last, tokens, qa, qb):
    smem = pl.BlockSpec(memory_space=pltpu.SMEM)
    vmem = pl.BlockSpec(memory_space=pltpu.VMEM)
    out = jax.ShapeDtypeStruct((DOCS // 2, NQ_HERE), f32)
    return pl.pallas_call(
        pool_body,
        in_specs=[smem] * 6 + [vmem] * 6,
        out_shape=(out, out),
        out_specs=[vmem] * 2,
        scratch_shapes=[
            pltpu.VMEM((NT_HERE, DRAWS), bf16),
            pltpu.VMEM((DRAWS, NQ_HERE), bf16),
            pltpu.VMEM((DOCS, NQ_HERE), f32),
            pltpu.VMEM((TILE, NQ_HERE), f32),
        ],
        compiler_params=params(28),
        cost_estimate=pl.CostEstimate(
            flops=2 * NT_HERE * NQ_HERE * DRAWS, bytes_accessed=6 << 20, transcendentals=0
        ),
        name="pool",
    )(core, bases, starts, ends, first, last, *tokens, qa, qb)


def finish_body(pieces_ref, q_ref, len_ref, out_ref):
    total = pieces_ref[0]
    for i in range(1, 16):
        total = total + pieces_ref[i]
    q = q_ref[...].astype(f32)
    scale = lax.rsqrt(jnp.sum(q * q, axis=0, keepdims=True) / (DRAWS - 1) + EPS) / (DRAWS - 1)
    out_ref[...] = total * (scale * scale) / len_ref[...]


def shift(value, axis, by):
    size = lax.axis_size(axis)
    return lax.ppermute(value, axis, [(i, (i + by) % size) for i in range(size)])


def step(train_losses, query_losses, chain_slots, doc_lengths):
    core = lax.axis_index("c")
    yh = lax.axis_index("yh")
    x = lax.axis_index("x")
    t = (lax.axis_index("yl") * 4 + lax.axis_index("z")) * 2 + core

    doc_ends = jnp.cumsum(doc_lengths)
    doc_starts = doc_ends - doc_lengths

    packed = pack(train_losses, query_losses)
    arrived = lax.all_to_all(packed, ("yl", "z", "c"), split_axis=0, concat_axis=0, tiled=True)
    own, q_own = centre(chain_slots, arrived)

    left = shift(own, "x", 1)
    right = shift(own, "x", -1)
    far_lo = shift(left[: RUN // 2], "x", 1)
    far_hi = shift(right[RUN // 2 :], "x", -1)
    far = jnp.concatenate([far_lo, far_hi])

    copies = jnp.broadcast_to(q_own, (16, *q_own.shape))
    qa = lax.all_to_all(copies, ("yl", "z", "yh"), split_axis=0, concat_axis=0, tiled=True)
    qb = shift(qa, "c", 1)

    xs = jnp.stack([x, (x + 3) % 4, (x + 1) % 4, (x + 2) % 4])
    run_bases = (xs * 2 + yh) * (16 * RUN) + t * RUN
    bases = (run_bases[:, None] + jnp.arange(RUN // TILE, dtype=jnp.int32) * TILE).reshape(-1)
    first = jnp.sum(doc_ends[None, :] <= bases[:, None], axis=1, dtype=jnp.int32)
    last = jnp.sum(doc_ends[None, :] <= bases[:, None] + (TILE - 1), axis=1, dtype=jnp.int32)

    send, keep = pool(
        core.reshape(1), bases, doc_starts, doc_ends, first, last,
        (own, left, right, far), qa, qb,
    )
    other = shift(send, "c", 1)
    half = (keep + other).reshape(8, DOC_OWN, 2, 2048).transpose(0, 2, 1, 3)
    pieces = lax.all_to_all(
        half.reshape(16, DOC_OWN, 2048), ("yl", "z", "yh"), split_axis=0, concat_axis=0, tiled=True
    )

    mine = lax.dynamic_index_in_dim(qa.reshape(8, 2, DRAWS, QPIECE), yh, 1, keepdims=False)
    theirs = lax.dynamic_index_in_dim(qb.reshape(8, 2, DRAWS, QPIECE), yh, 1, keepdims=False)
    both = jnp.where(core == 0, jnp.stack([mine, theirs], 1), jnp.stack([theirs, mine], 1))
    q_mine = both.transpose(2, 0, 1, 3).reshape(DRAWS, 2048)
    lengths = lax.dynamic_slice_in_dim(doc_lengths, t * DOC_OWN, DOC_OWN, 0).astype(f32)
    return pl.pallas_call(
        finish_body,
        out_shape=jax.ShapeDtypeStruct((DOC_OWN, 2048), f32),
        compiler_params=params(16),
        name="finish",
    )(pieces, q_mine, lengths[:, None])


def solution(mesh):
    fine = Mesh(mesh.devices.reshape(2, 4, 2, 4, 2), ("yl", "z", "c", "x", "yh"))
    split = P(("yl", "z", "c"), ("x", "yh"))
    return jax.shard_map(
        step, mesh=fine, in_specs=(split, split, P(), P()), out_specs=split, check_vma=False
    )
```

time: 139 us -> 119 us (0.86)
  Pallas kernels: 37.2 us -> 18.6 us
  starting transfers between devices: 24.2 us -> 15.3 us
  waiting for transfers between devices: 19.4 us -> 25.4 us
    pallas_call x3, Pallas kernels: 36.2 us -> 16.8 us  [the longest x1 16 us: pool(): pl.pallas_call(pool_body, in_specs=[smem] * 6 + [vmem] * 6, out_shape=(ou...]
    ppermute x8 -> x6, waiting for transfers between devices: 13.7 us -> 19.3 us  [shift(): lax.ppermute(value, axis, [(i, (i + by) % size) for i in range(size)])]
    ppermute x8 -> x6, starting transfers between devices: 13.1 us -> 8.2 us  [shift(): lax.ppermute(value, axis, [(i, (i + by) % size) for i in range(size)])]
    all_to_all x1, starting transfers between devices: 11 us -> 7.13 us  [step(): lax.all_to_all(half.reshape(16, DOC_OWN, 2048), ('yl', 'z', 'yh'), split_...]
  transfers between devices with their start and end apart: 9 -> 7, of which waited for: 5 -> 4; matrix products, arithmetic and copies ran while one was open for 7% -> 8% of each run, Pallas kernels for 0% -> 0%
where the time goes in v2:
time: 119 us; the launch traced here: 118 us
  blocking collectives  44.8 us (38%)
  waiting for transfers between devices  25.4 us (21%)
  Pallas kernels  18.6 us (16%)
  starting transfers between devices  15.3 us (13%)
  other arithmetic  7.19 us (6%)
  local copies, waits for them, and re-layouts  6.18 us (5%)
    all_to_all x1, blocking collectives, step(): lax.all_to_all(packed, ('yl', 'z', 'c'), split_axis=0, concat_axis=0, til...  25 us
    all_to_all x1, blocking collectives, step(): lax.all_to_all(copies, ('yl', 'z', 'yh'), split_axis=0, concat_axis=0, ti...  19.8 us
    ppermute x6, waiting for transfers between devices, shift(): lax.ppermute(value, axis, [(i, (i + by) % size) for i in range(size)])  19.3 us
    pallas_call x1, Pallas kernels, pool(): pl.pallas_call(pool_body, in_specs=[smem] * 6 + [vmem] * 6, out_shape=(ou...  16 us
    ppermute x6, starting transfers between devices, shift(): lax.ppermute(value, axis, [(i, (i + by) % size) for i in range(size)])  8.2 us
    all_to_all x1, starting transfers between devices, step(): lax.all_to_all(half.reshape(16, DOC_OWN, 2048), ('yl', 'z', 'yh'), split_...  7.13 us
    all_to_all x1, waiting for transfers between devices, step(): lax.all_to_all(half.reshape(16, DOC_OWN, 2048), ('yl', 'z', 'yh'), split_...  6.11 us
    transpose x1, other arithmetic, step(): q_mine = both.transpose(2, 0, 1, 3).reshape(DRAWS, 2048)  5.33 us
  transfers between devices with their start and end apart: 7, of which 4 were waited for; matrix products, arithmetic and copies ran while one was open for 8% of the time, Pallas kernels for 0%

profile of v2, /device:TPU:1, one launch (start us, length us, event | category | flops | bytes accessed | tf_op | source)
XLA Modules:
  0.0 117.7 jit_solution(15006935898613190570)
XLA Ops:
  0.0 1.2 %copy-done = f32[16,16384]{1,0:T(8,128)S(1)} copy-done((f32[16,16384]{1,0:T(8,128)S(1)}, f32[16,16384]{1,0:T(8,128)}, u32[]{:S(2)}) %copy-start) | copy-done | bytes 1048600
  1.2 0.9 copy-done.1
  2.1 0.1 pack.1
  2.2 25.0 %all_to_all.15.arr_ref = f32[16,16,1152]{2,1,0:T(8,128)S(1)} all-to-all(f32[16,16,1152]{2,1,0:T(8,128)S(1)} %pack.1), channel_id=1, replica_groups=mesh['yl'=2,'z'=4,'c'=2,'x'=4,'yh'=2] {'yl','z','c'}, dimensions={0} | all-to-all | bytes 2359296 | tf_op jit(solution)/shard_map/all_to_all | solution.py:221
  27.2 1.8 %centre.1 = (bf16[1024,256]{1,0:T(8,128)(2,1)}, bf16[256,128]{1,0:T(8,128)(2,1)S(1)}) custom-call(s32[32]{0:T(128)S(1)} %copy-done.2, f32[16,16,1152]{2,1,0:T(8,128)S(1)} %all_to_all.15.arr_ref), custom_call_target="tpu_custom_call" | custom-call | tf_op jit(solution)/shard_map/centre/pallas_call | solution.py:66
  29.0 0.2 broadcast_in_dim.4
  29.2 19.8 %all_to_all.16.qa_ref = bf16[16,256,128]{2,1,0:T(8,128)(2,1)S(1)} all-to-all(bf16[16,256,128]{2,1,0:T(8,128)(2,1)S(1)} %broadcast_in_dim.4), channel_id=1, replica_groups=mesh['yl'=2,'z'=4,'c'=2,'x'=4,'yh'=2] {'yl','z','yh'}, dimensions={0} | all-to-all | bytes 2097152 | tf_op jit(solution)/shard_map/all_to_all | solution.py:231
  49.0 2.5 %collective-permute-start.4 = (bf16[16,256,128]{2,1,0:T(8,128)(2,1)S(1)}, bf16[16,256,128]{2,1,0:T(8,128)(2,1)S(1)}, u32[]{:S(2)}, u32[]{:S(2)}) collective-permute-start(bf16[16,256,128]{2,1,0:T(8,128)(2,1)S(1)} %all_to_all.16.qa_ref), channel_id=1, source_target_pairs={{0,8},{8,0},{1,9},{9,1},{2,10},{10,2},{3,11},{11,3},{4,12},{12,4},... | collective-permute-start | bytes 3145736 | tf_op jit(solution)/shard_map/ppermute | solution.py:208
  51.5 1.2 %collective-permute-start = (bf16[1024,256]{1,0:T(8,128)(2,1)}, bf16[1024,256]{1,0:T(8,128)(2,1)S(1)}, u32[]{:S(2)}, u32[]{:S(2)}) collective-permute-start(bf16[1024,256]{1,0:T(8,128)(2,1)} %get-tuple-element.9.own), channel_id=1, source_target_pairs={{0,2},{2,4},{4,6},{6,0},{1,3},{3,5},{5,7},{7,1},{8,10},{10,12},{12... | collective-permute-start | bytes 1572872 | tf_op jit(solution)/shard_map/ppermute | solution.py:208
  52.7 1.5 %collective-permute-start.1 = (bf16[1024,256]{1,0:T(8,128)(2,1)}, bf16[1024,256]{1,0:T(8,128)(2,1)S(1)}, u32[]{:S(2)}, u32[]{:S(2)}) collective-permute-start(bf16[1024,256]{1,0:T(8,128)(2,1)} %get-tuple-element.9.own), channel_id=1, source_target_pairs={{0,6},{2,0},{4,2},{6,4},{1,7},{3,1},{5,3},{7,5},{8,14},{10,8},{12,... | collective-permute-start | bytes 1572872 | tf_op jit(solution)/shard_map/ppermute | solution.py:208
  54.2 0.1 iota_multiply_fusion
  54.3 0.1 add.104.bases_ref
  54.4 0.1 copy.13
  54.5 0.2 reduce-window.8
  54.7 0.1 reduce.ends_ref
  54.8 11.6 %collective-permute-done.left = bf16[1024,256]{1,0:T(8,128)(2,1)S(1)} collective-permute-done((bf16[1024,256]{1,0:T(8,128)(2,1)}, bf16[1024,256]{1,0:T(8,128)(2,1)S(1)}, u32[]{:S(2)}, u32[]{:S(2)}) %collective-permute-start) | collective-permute-done | bytes 524320 | tf_op jit(solution)/shard_map/ppermute | solution.py:208
  66.5 2.7 %collective-permute-start.3 = (bf16[512,256]{1,0:T(8,128)(2,1)S(1)}, bf16[512,256]{1,0:T(8,128)(2,1)S(1)}, u32[]{:S(2)}, u32[]{:S(2)}) collective-permute-start(bf16[512,256]{1,0:T(8,128)(2,1)S(1)} %slice.9), channel_id=1, source_target_pairs={{0,6},{2,0},{4,2},{6,4},{1,7},{3,1},{5,3},{7,5},{8,14},{10,8},{12,... | collective-permute-start | bytes 786440 | tf_op jit(solution)/shard_map/ppermute | solution.py:208
  69.2 0.2 convert_reduce_fusion
  69.4 5.3 %collective-permute-done.2 = bf16[512,256]{1,0:T(8,128)(2,1)S(1)} collective-permute-done((bf16[512,256]{1,0:T(8,128)(2,1)S(1)}, bf16[512,256]{1,0:T(8,128)(2,1)S(1)}, u32[]{:S(2)}, u32[]{:S(2)}) %collective-permute-start.2) | collective-permute-done | bytes 262176 | tf_op jit(solution)/shard_map/ppermute | solution.py:208
  74.7 16.0 %pool.1 = (f32[64,4096]{1,0:T(8,128)S(1)}, f32[64,4096]{1,0:T(8,128)S(1)}) custom-call(s32[1]{0:T(128)} %bitcast.core_ref, s32[16]{0:T(128)S(1)} %add.104.bases_ref, s32[128]{0:T(128)S(1)} %sub.3.starts_ref, s32[128]{0:T(128)S(1)} %reduce.ends_ref, s32[16]{0:T(128)S(1)} %get-tuple-element.14.first_ref, s32[16]{0:T(128)S(1)} %get-tuple-element.13.last_ref, ...), custom_call_target="tpu_custom_call" | custom-call | flops 8589934592 | bytes 6291456 | tf_op jit(solution)/shard_map/pool/pallas_call | solution.py:178
  90.8 0.3 collective-permute-start.5
  91.0 2.5 %collective-permute-done.5 = f32[64,4096]{1,0:T(8,128)S(1)} collective-permute-done((f32[64,4096]{1,0:T(8,128)S(1)}, f32[64,4096]{1,0:T(8,128)S(1)}, u32[]{:S(2)}, u32[]{:S(2)}) %collective-permute-start.5) | collective-permute-done | bytes 1048608 | tf_op jit(solution)/shard_map/ppermute | solution.py:208
  93.5 1.1 add.106
  94.6 7.1 %all-to-all-start.2 = ((f32[16,8,2048]{2,1,0:T(8,128)}), f32[16,8,2048]{2,1,0:T(8,128)S(1)}, u32[]{:S(2)}, u32[]{:S(2)}) async-start(f32[16,8,2048]{2,1,0:T(8,128)} %bitcast.19), calls=%async_computation.2 | async-start | bytes 2097152 | tf_op jit(solution)/shard_map/all_to_all | solution.py:246
  101.8 0.1 convert_bitcast_fusion
  101.9 0.1 copy.16.len_ref
  102.0 0.8 copy.17
  102.8 0.8 copy.18
  103.7 5.3 %fusion = bf16[256,8,2,128]{3,2,1,0:T(2,128)(2,1)} fusion(pred[]{:T(512)S(6)} %eq.7, bf16[8,1,256,128]{3,1,0,2:T(2,128)(2,1)S(1)} %copy.18, bf16[8,1,256,128]{3,1,0,2:T(2,128)(2,1)S(1)} %copy.17), kind=kLoop, calls=%fused_computation.1 | loop fusion | flops 4718592 | bytes 2097153 | tf_op jit(solution)/shard_map/transpose | solution.py:253
  109.0 1.8 %reshape.116.q_ref = bf16[256,2048]{1,0:T(8,128)(2,1)S(1)} reshape(bf16[256,8,2,128]{3,2,1,0:T(2,128)(2,1)} %fusion) | data formatting | bytes 2097152 | tf_op jit(solution)/shard_map/reshape | solution.py:253
  110.8 6.1 %all-to-all-done.2.pieces_ref = f32[16,8,2048]{2,1,0:T(8,128)S(1)} async-done(((f32[16,8,2048]{2,1,0:T(8,128)}), f32[16,8,2048]{2,1,0:T(8,128)S(1)}, u32[]{:S(2)}, u32[]{:S(2)}) %all-to-all-start.2) | async-done | bytes 1048608 | tf_op jit(solution)/shard_map/all_to_all | solution.py:246
  116.9 0.7 finish.1
  (18 shorter events, 0.3 us)
Async XLA Ops:
  0.0 1.2 %copy-start = (f32[16,16384]{1,0:T(8,128)S(1)}, f32[16,16384]{1,0:T(8,128)}, u32[]{:S(2)}) copy-start(f32[16,16384]{1,0:T(8,128)} %train_ref.1) | copy-start | bytes 3145732
  1.2 0.9 copy-start.1
  2.2 25.0 %copy-start.2 = (s32[32]{0:T(128)S(1)}, s32[32]{0:T(128)}, u32[]{:S(2)}) copy-start(s32[32]{0:T(128)} %slots_ref.1) | copy-start | bytes 388
  29.2 25.2 %copy-start.3 = (s32[128]{0:T(128)S(1)}, s32[128]{0:T(128)}, u32[]{:S(2)}) copy-start(s32[128]{0:T(128)} %param.7) | copy-start | bytes 1540
  49.0 25.7 %collective-permute-start.4 = (bf16[16,256,128]{2,1,0:T(8,128)(2,1)S(1)}, bf16[16,256,128]{2,1,0:T(8,128)(2,1)S(1)}, u32[]{:S(2)}, u32[]{:S(2)}) collective-permute-start(bf16[16,256,128]{2,1,0:T(8,128)(2,1)S(1)} %all_to_all.16.qa_ref), channel_id=1, source_target_pairs={{0,8},{8,0},{1,9},{9,1},{2,10},{10,2},{3,11},{11,3},{4,12},{12,4},... | collective-permute-start | bytes 3145736 | tf_op jit(solution)/shard_map/ppermute | solution.py:208
  51.5 14.9 %collective-permute-start = (bf16[1024,256]{1,0:T(8,128)(2,1)}, bf16[1024,256]{1,0:T(8,128)(2,1)S(1)}, u32[]{:S(2)}, u32[]{:S(2)}) collective-permute-start(bf16[1024,256]{1,0:T(8,128)(2,1)} %get-tuple-element.9.own), channel_id=1, source_target_pairs={{0,2},{2,4},{4,6},{6,0},{1,3},{3,5},{5,7},{7,1},{8,10},{10,12},{12... | collective-permute-start | bytes 1572872 | tf_op jit(solution)/shard_map/ppermute | solution.py:208
  52.7 13.8 %collective-permute-start.1 = (bf16[1024,256]{1,0:T(8,128)(2,1)}, bf16[1024,256]{1,0:T(8,128)(2,1)S(1)}, u32[]{:S(2)}, u32[]{:S(2)}) collective-permute-start(bf16[1024,256]{1,0:T(8,128)(2,1)} %get-tuple-element.9.own), channel_id=1, source_target_pairs={{0,6},{2,0},{4,2},{6,4},{1,7},{3,1},{5,3},{7,5},{8,14},{10,8},{12,... | collective-permute-start | bytes 1572872 | tf_op jit(solution)/shard_map/ppermute | solution.py:208
  66.4 8.3 %collective-permute-start.2 = (bf16[512,256]{1,0:T(8,128)(2,1)S(1)}, bf16[512,256]{1,0:T(8,128)(2,1)S(1)}, u32[]{:S(2)}, u32[]{:S(2)}) collective-permute-start(bf16[512,256]{1,0:T(8,128)(2,1)S(1)} %slice.8), channel_id=1, source_target_pairs={{0,2},{2,4},{4,6},{6,0},{1,3},{3,5},{5,7},{7,1},{8,10},{10,12},{12... | collective-permute-start | bytes 786440 | tf_op jit(solution)/shard_map/ppermute | solution.py:208
  66.5 8.2 %collective-permute-start.3 = (bf16[512,256]{1,0:T(8,128)(2,1)S(1)}, bf16[512,256]{1,0:T(8,128)(2,1)S(1)}, u32[]{:S(2)}, u32[]{:S(2)}) collective-permute-start(bf16[512,256]{1,0:T(8,128)(2,1)S(1)} %slice.9), channel_id=1, source_target_pairs={{0,6},{2,0},{4,2},{6,4},{1,7},{3,1},{5,3},{7,5},{8,14},{10,8},{12,... | collective-permute-start | bytes 786440 | tf_op jit(solution)/shard_map/ppermute | solution.py:208
  90.8 2.7 %collective-permute-start.5 = (f32[64,4096]{1,0:T(8,128)S(1)}, f32[64,4096]{1,0:T(8,128)S(1)}, u32[]{:S(2)}, u32[]{:S(2)}) collective-permute-start(f32[64,4096]{1,0:T(8,128)S(1)} %get-tuple-element.12), channel_id=1, source_target_pairs={{0,8},{8,0},{1,9},{9,1},{2,10},{10,2},{3,11},{11,3},{4,12},{12,4},... | collective-permute-start | bytes 3145736 | tf_op jit(solution)/shard_map/ppermute | solution.py:208
  94.6 22.3 %all-to-all-start.2 = ((f32[16,8,2048]{2,1,0:T(8,128)}), f32[16,8,2048]{2,1,0:T(8,128)S(1)}, u32[]{:S(2)}, u32[]{:S(2)}) async-start(f32[16,8,2048]{2,1,0:T(8,128)} %bitcast.19), calls=%async_computation.2 | async-start | bytes 2097152 | tf_op jit(solution)/shard_map/all_to_all | solution.py:246

commit v3 on v2

v3 whole, which is shorter than its diff:
```python
import jax
import jax.numpy as jnp
from jax import lax
from jax.experimental import pallas as pl
from jax.experimental.pallas import tpu as pltpu
from jax.sharding import Mesh
from jax.sharding import PartitionSpec as P

DRAWS = 256
CHAINS = 32
PER_CHAIN = DRAWS // CHAINS
EPS = 1e-06
DOCS = 128
DOC_OWN = 8
RUN = 1024
QPIECE = 128
TILE = 256
NBLK = 512
NTILE = 1024
NQ_HALF = 2048
PIECE = RUN + 256 + 3 * QPIECE
NT_HERE = 4096

f32 = jnp.float32
bf16 = jnp.bfloat16


def params(mib=48):
    return pltpu.CompilerParams(vmem_limit_bytes=mib * 1024 * 1024)


def terms(value):
    hi = value.astype(bf16).astype(f32)
    rest = value - hi
    mid = rest.astype(bf16).astype(f32)
    return hi, mid, rest - mid


def pack_body(train_ref, query_ref, out_ref):
    rows = train_ref.shape[0]
    for i in range(16):
        block = train_ref[:, i * RUN : (i + 1) * RUN]
        mean = jnp.sum(block, axis=0, keepdims=True) / rows
        out_ref[i, :, :RUN] = (block - mean).astype(bf16)
        stacked = jnp.concatenate([mean[:, j * 128 : (j + 1) * 128] for j in range(8)], axis=0)
        hi, mid, lo = terms(stacked)
        out_ref[i, :, RUN : RUN + 128] = jnp.concatenate([hi, mid], axis=0).astype(bf16)
        out_ref[i, :, RUN + 128 : RUN + 256] = jnp.concatenate([lo, lo], axis=0).astype(bf16)
        for k, term in enumerate(terms(query_ref[:, i * QPIECE : (i + 1) * QPIECE])):
            o = RUN + 256 + k * QPIECE
            out_ref[i, :, o : o + QPIECE] = term.astype(bf16)


def pack(train, query):
    return pl.pallas_call(
        pack_body,
        in_specs=[pl.BlockSpec(memory_space=pltpu.VMEM)] * 2,
        out_specs=pl.BlockSpec(memory_space=pltpu.VMEM),
        out_shape=jax.ShapeDtypeStruct((16, train.shape[0], PIECE), bf16),
        compiler_params=params(16),
        name="pack",
    )(train, query)


def centre_body(slots_ref, arr_ref, u_ref, q_ref, qc_ref, qp_ref, mean_ref):
    def part(o):
        return arr_ref[:, :, o : o + 128].astype(f32)

    o = RUN + 256
    query = ((part(o + 2 * QPIECE) + part(o + QPIECE)) + part(o)).reshape(DRAWS, QPIECE)
    mean = jnp.sum(query, axis=0, keepdims=True) / DRAWS
    qc = (query - mean).astype(bf16).astype(f32)
    qc_ref[...] = qc.reshape(CHAINS, PER_CHAIN, QPIECE)
    for s in range(CHAINS):
        qp_ref[s] = qc_ref[slots_ref[s]]
    q_ref[...] = qp_ref[...].reshape(DRAWS, QPIECE).astype(bf16)

    upper = part(RUN)
    mean_ref[...] = (part(RUN + 128)[:, :8] + upper[:, 8:]) + upper[:, :8]
    for j in range(RUN // 128):
        local = mean_ref[:, j : j + 1, :]
        offset = local - jnp.sum(local, axis=0, keepdims=True) / 16
        c = (part(j * 128) + offset).reshape(DRAWS, 128).astype(bf16).astype(f32)
        scale = lax.rsqrt(jnp.sum(c * c, axis=0, keepdims=True) / (DRAWS - 1) + EPS)
        u_ref[j * 128 : (j + 1) * 128, :] = (c * scale).T.astype(bf16)


def centre(slots, arr):
    return pl.pallas_call(
        centre_body,
        in_specs=[
            pl.BlockSpec(memory_space=pltpu.SMEM),
            pl.BlockSpec(memory_space=pltpu.VMEM),
        ],
        out_shape=(
            jax.ShapeDtypeStruct((RUN, DRAWS), bf16),
            jax.ShapeDtypeStruct((DRAWS, QPIECE), bf16),
        ),
        out_specs=[pl.BlockSpec(memory_space=pltpu.VMEM)] * 2,
        scratch_shapes=[
            pltpu.VMEM((CHAINS, PER_CHAIN, QPIECE), f32),
            pltpu.VMEM((CHAINS, PER_CHAIN, QPIECE), f32),
            pltpu.VMEM((16, 8, 128), f32),
        ],
        compiler_params=params(16),
        name="centre",
    )(slots, arr)


def pool_body(
    core_ref, bases_ref, starts_ref, ends_ref, first_ref, last_ref,
    own, left, right, far, q_ref,
    send_ref, keep_ref, weight_ref,
    tok, qs, acc, tile_s,
):
    core = core_ref[0]
    at = 0
    for ref in (own, left, right, far):
        tok[at : at + ref.shape[0], :] = ref[...]
        at += ref.shape[0]
    for i in range(16):
        o = (i % 2 * 8 + i // 2) * QPIECE
        block = q_ref[i]
        qs[:, o : o + QPIECE] = block
        wide = block.astype(f32)
        scale = lax.rsqrt(jnp.sum(wide * wide, axis=0, keepdims=True) / (DRAWS - 1) + EPS)
        weight_ref[:, o : o + QPIECE] = (scale / (DRAWS - 1)) * (scale / (DRAWS - 1))
    acc[...] = jnp.zeros_like(acc)

    def row_of(k):
        owner = k // DOC_OWN
        keep = jnp.where(owner % 2 == core, 1, 0)
        return keep * (DOCS // 2) + owner // 2 * DOC_OWN + k % DOC_OWN

    def products(rows):
        lhs = tok[pl.ds(rows, TILE), :]
        for b in range(NQ_HALF // NBLK):
            where = slice(b * NBLK, (b + 1) * NBLK)
            yield where, jnp.dot(lhs, qs[:, where], preferred_element_type=f32)

    def many(i, rows):
        for where, s in products(rows):
            tile_s[:, where] = s
        base = bases_ref[i]

        def one_doc(k, _):
            begin = jnp.maximum(starts_ref[k] - base, 0)
            end = jnp.minimum(ends_ref[k] - base, TILE)
            row = row_of(k)

            @pl.loop(0, NQ_HALF // NTILE)
            def _(n):
                cols = pl.ds(pl.multiple_of(n * NTILE, NTILE), NTILE)

                def one_group(g, total):
                    o = pl.multiple_of(g * 8, 8)
                    s = tile_s[pl.ds(o, 8), cols]
                    at = lax.broadcasted_iota(jnp.int32, s.shape, 0) + o
                    inside = (at >= begin) & (at < end)
                    return total + jnp.where(inside, s * jnp.abs(s), 0.0)

                total = lax.fori_loop(
                    begin // 8, (end + 7) // 8, one_group, jnp.zeros((8, NTILE), f32)
                )
                acc[pl.ds(row, 1), cols] += jnp.sum(total, axis=0, keepdims=True)

            return 0

        lax.fori_loop(first_ref[i], last_ref[i] + 1, one_doc, 0)

    @pl.loop(0, NT_HERE // TILE // 2)
    def _(pair):
        tiles = (2 * pair, 2 * pair + 1)
        rows = [pl.multiple_of(i * TILE, TILE) for i in tiles]
        extra = [last_ref[i] - first_ref[i] for i in tiles]
        most = jnp.maximum(extra[0], extra[1])

        @pl.when(most == 0)
        def _():
            for i, r in zip(tiles, rows):
                row = row_of(first_ref[i])
                for where, s in products(r):
                    acc[pl.ds(row, 1), where] += jnp.sum(s * jnp.abs(s), axis=0, keepdims=True)

        @pl.when(most == 1)
        def _():
            for i, r in zip(tiles, rows):
                row = row_of(first_ref[i])
                row_next = row_of(last_ref[i])
                border = ends_ref[first_ref[i]] - bases_ref[i]
                upper = lax.broadcasted_iota(jnp.int32, (TILE, NBLK), 0) < border
                for where, s in products(r):
                    p = s * jnp.abs(s)
                    p_upper = jnp.where(upper, p, 0.0)
                    acc[pl.ds(row, 1), where] += jnp.sum(p_upper, axis=0, keepdims=True)
                    acc[pl.ds(row_next, 1), where] += jnp.sum(p - p_upper, axis=0, keepdims=True)

        @pl.when(most > 1)
        def _():
            @pl.loop(2 * pair, 2 * pair + 2)
            def _(i):
                many(i, pl.multiple_of(i * TILE, TILE))

    send_ref[...] = acc[: DOCS // 2, :]
    keep_ref[...] = acc[DOCS // 2 :, :]


def pool(core, bases, starts, ends, first, last, tokens, q):
    smem = pl.BlockSpec(memory_space=pltpu.SMEM)
    vmem = pl.BlockSpec(memory_space=pltpu.VMEM)
    out = jax.ShapeDtypeStruct((DOCS // 2, NQ_HALF), f32)
    return pl.pallas_call(
        pool_body,
        in_specs=[smem] * 6 + [vmem] * 5,
        out_shape=(out, out, jax.ShapeDtypeStruct((1, NQ_HALF), f32)),
        out_specs=[vmem] * 3,
        scratch_shapes=[
            pltpu.VMEM((NT_HERE, DRAWS), bf16),
            pltpu.VMEM((DRAWS, NQ_HALF), bf16),
            pltpu.VMEM((DOCS, NQ_HALF), f32),
            pltpu.VMEM((TILE, NQ_HALF), f32),
        ],
        compiler_params=params(20),
        cost_estimate=pl.CostEstimate(
            flops=2 * NT_HERE * NQ_HALF * DRAWS, bytes_accessed=5 << 20, transcendentals=0
        ),
        name="pool",
    )(core, bases, starts, ends, first, last, *tokens, q)


def combine_body(keep_a, got_a, keep_b, got_b, out_ref):
    half = NQ_HALF // 2
    for d in range(16):
        ylz, yh = d // 2, d % 2
        r = slice(ylz * DOC_OWN, (ylz + 1) * DOC_OWN)
        c = slice(yh * half, (yh + 1) * half)
        out_ref[d, :, :half] = keep_a[r, c] + got_a[r, c]
        out_ref[d, :, half:] = keep_b[r, c] + got_b[r, c]


def combine(*arrays):
    return pl.pallas_call(
        combine_body,
        in_specs=[pl.BlockSpec(memory_space=pltpu.VMEM)] * 4,
        out_specs=pl.BlockSpec(memory_space=pltpu.VMEM),
        out_shape=jax.ShapeDtypeStruct((16, DOC_OWN, NQ_HALF), f32),
        compiler_params=params(16),
        name="combine",
    )(*arrays)


def finish_body(place_ref, pieces_ref, weight_a, weight_b, len_ref, out_ref):
    core = place_ref[0]
    yh = place_ref[1]
    total = pieces_ref[0]
    for i in range(1, 16):
        total = total + pieces_ref[i]
    total = total / len_ref[...]
    half = NQ_HALF // 2
    cols = pl.ds(pl.multiple_of(yh * half, half), half)
    for k, (weight, c) in enumerate(((weight_a, core), (weight_b, 1 - core))):
        part = total[:, k * half : (k + 1) * half] * weight[:, cols]
        for ylz in range(8):
            o = pl.multiple_of((ylz * 2 + c) * QPIECE, QPIECE)
            out_ref[:, pl.ds(o, QPIECE)] = part[:, ylz * QPIECE : (ylz + 1) * QPIECE]


def finish(place, pieces, weight_a, weight_b, lengths):
    vmem = pl.BlockSpec(memory_space=pltpu.VMEM)
    return pl.pallas_call(
        finish_body,
        in_specs=[pl.BlockSpec(memory_space=pltpu.SMEM)] + [vmem] * 4,
        out_specs=vmem,
        out_shape=jax.ShapeDtypeStruct((DOC_OWN, NQ_HALF), f32),
        compiler_params=params(16),
        name="finish",
    )(place, pieces, weight_a, weight_b, lengths)


def shift(value, axis, by):
    size = lax.axis_size(axis)
    return lax.ppermute(value, axis, [(i, (i + by) % size) for i in range(size)])


def step(train_losses, query_losses, chain_slots, doc_lengths):
    core = lax.axis_index("c")
    yh = lax.axis_index("yh")
    x = lax.axis_index("x")
    t = (lax.axis_index("yl") * 4 + lax.axis_index("z")) * 2 + core

    doc_ends = jnp.cumsum(doc_lengths)
    doc_starts = doc_ends - doc_lengths

    packed = pack(train_losses, query_losses)
    arrived = lax.all_to_all(packed, ("yl", "z", "c"), split_axis=0, concat_axis=0, tiled=True)
    own, q_own = centre(chain_slots, arrived)

    left = shift(own, "x", 1)
    right = shift(own, "x", -1)
    far_lo = shift(left[: RUN // 2], "x", 1)
    far_hi = shift(right[RUN // 2 :], "x", -1)
    far = jnp.concatenate([far_lo, far_hi])

    copies = jnp.broadcast_to(q_own, (16, *q_own.shape))
    qa = lax.all_to_all(copies, ("yl", "z", "yh"), split_axis=0, concat_axis=0, tiled=True)
    qb = shift(qa, "c", 1)

    xs = jnp.stack([x, (x + 3) % 4, (x + 1) % 4, (x + 2) % 4])
    run_bases = (xs * 2 + yh) * (16 * RUN) + t * RUN
    bases = (run_bases[:, None] + jnp.arange(RUN // TILE, dtype=jnp.int32) * TILE).reshape(-1)
    first = jnp.sum(doc_ends[None, :] <= bases[:, None], axis=1, dtype=jnp.int32)
    last = jnp.sum(doc_ends[None, :] <= bases[:, None] + (TILE - 1), axis=1, dtype=jnp.int32)

    where = (core.reshape(1), bases, doc_starts, doc_ends, first, last)
    tokens = (own, left, right, far)
    send_a, keep_a, weight_a = pool(*where, tokens, qa)
    cross_a = shift(send_a, "c", 1)
    send_b, keep_b, weight_b = pool(*where, tokens, qb)
    cross_b = shift(send_b, "c", 1)
    pieces = lax.all_to_all(
        combine(keep_a, cross_b, keep_b, cross_a), ("yl", "z", "yh"),
        split_axis=0, concat_axis=0, tiled=True,
    )
    lengths = lax.dynamic_slice_in_dim(doc_lengths, t * DOC_OWN, DOC_OWN, 0).astype(f32)
    return finish(jnp.stack([core, yh]), pieces, weight_a, weight_b, lengths[:, None])


def solution(mesh):
    fine = Mesh(mesh.devices.reshape(2, 4, 2, 4, 2), ("yl", "z", "c", "x", "yh"))
    split = P(("yl", "z", "c"), ("x", "yh"))
    return jax.shard_map(
        step, mesh=fine, in_specs=(split, split, P(), P()), out_specs=split, check_vma=False
    )
```

time: 119 us -> 111 us (0.933)
  blocking collectives: 44.8 us -> 20.9 us
  waiting for transfers between devices: 25.4 us -> 34.1 us
  starting transfers between devices: 15.3 us -> 22.9 us
  other arithmetic: 7.19 us -> 0.76 us
  Pallas kernels: 18.6 us -> 23.1 us
    all_to_all x1 -> x2, waiting for transfers between devices: 6.11 us -> 27 us  [the longest x1 14.3 us: step(): lax.all_to_all(combine(keep_a, cross_b, keep_b, cross_a), ('yl', 'z', 'yh...]
    all_to_all x1 -> x0, blocking collectives: 19.8 us -> none  [step(): lax.all_to_all(copies, ('yl', 'z', 'yh'), split_axis=0, concat_axis=0, ti...]
    ppermute x6 -> x7, waiting for transfers between devices: 19.3 us -> 7.06 us  [shift(): lax.ppermute(value, axis, [(i, (i + by) % size) for i in range(size)])]
    all_to_all x1 -> x2, starting transfers between devices: 7.13 us -> 15.9 us  [the longest x1 10.5 us: step(): lax.all_to_all(combine(keep_a, cross_b, keep_b, cross_a), ('yl', 'z', 'yh...]
    transpose x1 -> x0, other arithmetic: 5.33 us -> none  [step(): q_mine = both.transpose(2, 0, 1, 3).reshape(DRAWS, 2048)]
    pallas_call x2 -> x4, Pallas kernels: 16.8 us -> 20.9 us  [the longest x2 18.6 us: pool(): pl.pallas_call(pool_body, in_specs=[smem] * 6 + [vmem] * 5, out_shape=(ou...]
    all_to_all x1, blocking collectives: 25 us -> 20.9 us  [step(): lax.all_to_all(packed, ('yl', 'z', 'c'), split_axis=0, concat_axis=0, til...]
    reshape x1 -> x0, local copies, waits for them, and re-layouts: 1.83 us -> none  [step(): q_mine = both.transpose(2, 0, 1, 3).reshape(DRAWS, 2048)]
  transfers between devices with their start and end apart: 7 -> 9, of which waited for: 4 -> 5; matrix products, arithmetic and copies ran while one was open for 8% -> 3% of each run, Pallas kernels for 0% -> 17%
where the time goes in v3:
time: 111 us; the launch traced here: 109 us
  waiting for transfers between devices  34.1 us (31%)
  Pallas kernels  23.1 us (21%)
  starting transfers between devices  22.9 us (21%)
  blocking collectives  20.9 us (19%)
  local copies, waits for them, and re-layouts  7.31 us (7%)
    all_to_all x1, blocking collectives, step(): lax.all_to_all(packed, ('yl', 'z', 'c'), split_axis=0, concat_axis=0, til...  20.9 us
    pallas_call x2, Pallas kernels, pool(): pl.pallas_call(pool_body, in_specs=[smem] * 6 + [vmem] * 5, out_shape=(ou...  18.6 us
    all_to_all x1, waiting for transfers between devices, step(): lax.all_to_all(combine(keep_a, cross_b, keep_b, cross_a), ('yl', 'z', 'yh...  14.3 us
    all_to_all x1, waiting for transfers between devices, step(): lax.all_to_all(copies, ('yl', 'z', 'yh'), split_axis=0, concat_axis=0, ti...  12.8 us
    all_to_all x1, starting transfers between devices, step(): lax.all_to_all(combine(keep_a, cross_b, keep_b, cross_a), ('yl', 'z', 'yh...  10.5 us
    ppermute x7, waiting for transfers between devices, shift(): lax.ppermute(value, axis, [(i, (i + by) % size) for i in range(size)])  7.06 us
    ppermute x7, starting transfers between devices, shift(): lax.ppermute(value, axis, [(i, (i + by) % size) for i in range(size)])  7.04 us
    all_to_all x1, starting transfers between devices, step(): lax.all_to_all(copies, ('yl', 'z', 'yh'), split_axis=0, concat_axis=0, ti...  5.35 us
  transfers between devices with their start and end apart: 9, of which 5 were waited for; matrix products, arithmetic and copies ran while one was open for 3% of the time, Pallas kernels for 17%

profile of v3, /device:TPU:1, one launch (start us, length us, event | category | flops | bytes accessed | tf_op | source)
XLA Modules:
  0.0 109.2 jit_solution(8727355432293791770)
XLA Ops:
  0.0 1.2 %copy-done = f32[16,16384]{1,0:T(8,128)S(1)} copy-done((f32[16,16384]{1,0:T(8,128)S(1)}, f32[16,16384]{1,0:T(8,128)}, u32[]{:S(2)}) %copy-start) | copy-done | bytes 1048600
  1.2 0.9 copy-done.1
  2.1 0.3 pack.1
  2.4 20.9 %all_to_all.15.arr_ref = bf16[16,16,1664]{2,1,0:T(8,128)(2,1)S(1)} all-to-all(bf16[16,16,1664]{2,1,0:T(8,128)(2,1)S(1)} %pack.1), channel_id=1, replica_groups=mesh['yl'=2,'z'=4,'c'=2,'x'=4,'yh'=2] {'yl','z','c'}, dimensions={0} | all-to-all | bytes 1703936 | tf_op jit(solution)/shard_map/all_to_all | solution.py:295
  23.3 1.9 %centre.1 = (bf16[1024,256]{1,0:T(8,128)(2,1)}, bf16[256,128]{1,0:T(8,128)(2,1)S(1)}) custom-call(s32[32]{0:T(128)S(1)} %copy-done.2, bf16[16,16,1664]{2,1,0:T(8,128)(2,1)S(1)} %all_to_all.15.arr_ref), custom_call_target="tpu_custom_call" | custom-call | tf_op jit(solution)/shard_map/centre/pallas_call | solution.py:89
  25.2 1.2 %broadcast_in_dim.4 = bf16[16,256,128]{2,1,0:T(8,128)(2,1)} broadcast(bf16[256,128]{1,0:T(8,128)(2,1)S(1)} %get-tuple-element.14), dimensions={1,2} | broadcast | bytes 1114112 | tf_op jit(solution)/shard_map/broadcast_in_dim | solution.py:304
  26.4 5.4 %all-to-all-start.1 = ((bf16[16,256,128]{2,1,0:T(8,128)(2,1)}), bf16[16,256,128]{2,1,0:T(8,128)(2,1)S(1)}, u32[]{:S(2)}, u32[]{:S(2)}) async-start(bf16[16,256,128]{2,1,0:T(8,128)(2,1)} %broadcast_in_dim.4), calls=%async_computation.1 | async-start | bytes 2097152 | tf_op jit(solution)/shard_map/all_to_all | solution.py:305
  31.7 1.3 %collective-permute-start = (bf16[1024,256]{1,0:T(8,128)(2,1)}, bf16[1024,256]{1,0:T(8,128)(2,1)S(1)}, u32[]{:S(2)}, u32[]{:S(2)}) collective-permute-start(bf16[1024,256]{1,0:T(8,128)(2,1)} %get-tuple-element.13.own), channel_id=1, source_target_pairs={{0,2},{2,4},{4,6},{6,0},{1,3},{3,5},{5,7},{7,1},{8,10},{10,12},{12... | collective-permute-start | bytes 1572872 | tf_op jit(solution)/shard_map/ppermute | solution.py:282
  33.0 1.5 %collective-permute-start.1 = (bf16[1024,256]{1,0:T(8,128)(2,1)}, bf16[1024,256]{1,0:T(8,128)(2,1)S(1)}, u32[]{:S(2)}, u32[]{:S(2)}) collective-permute-start(bf16[1024,256]{1,0:T(8,128)(2,1)} %get-tuple-element.13.own), channel_id=1, source_target_pairs={{0,6},{2,0},{4,2},{6,4},{1,7},{3,1},{5,3},{7,5},{8,14},{10,8},{12,... | collective-permute-start | bytes 1572872 | tf_op jit(solution)/shard_map/ppermute | solution.py:282
  34.6 12.8 %all-to-all-done.1.q_ref = bf16[16,256,128]{2,1,0:T(8,128)(2,1)S(1)} async-done(((bf16[16,256,128]{2,1,0:T(8,128)(2,1)}), bf16[16,256,128]{2,1,0:T(8,128)(2,1)S(1)}, u32[]{:S(2)}, u32[]{:S(2)}) %all-to-all-start.1) | async-done | bytes 1048608 | tf_op jit(solution)/shard_map/all_to_all | solution.py:305
  47.3 1.4 %collective-permute-start.4 = (bf16[16,256,128]{2,1,0:T(8,128)(2,1)S(1)}, bf16[16,256,128]{2,1,0:T(8,128)(2,1)S(1)}, u32[]{:S(2)}, u32[]{:S(2)}) collective-permute-start(bf16[16,256,128]{2,1,0:T(8,128)(2,1)S(1)} %all-to-all-done.1.q_ref), channel_id=1, source_target_pairs={{0,8},{8,0},{1,9},{9,1},{2,10},{10,2},{3,11},{11,3},{4,12},{12,4},... | collective-permute-start | bytes 3145736 | tf_op jit(solution)/shard_map/ppermute | solution.py:282
  48.8 0.7 slice.8
  49.6 1.2 %collective-permute-start.2 = (bf16[512,256]{1,0:T(8,128)(2,1)}, bf16[512,256]{1,0:T(8,128)(2,1)S(1)}, u32[]{:S(2)}, u32[]{:S(2)}) collective-permute-start(bf16[512,256]{1,0:T(8,128)(2,1)} %slice.8), channel_id=1, source_target_pairs={{0,2},{2,4},{4,6},{6,0},{1,3},{3,5},{5,7},{7,1},{8,10},{10,12},{12... | collective-permute-start | bytes 786440 | tf_op jit(solution)/shard_map/ppermute | solution.py:282
  50.8 0.7 slice.9
  51.5 1.5 %collective-permute-start.3 = (bf16[512,256]{1,0:T(8,128)(2,1)}, bf16[512,256]{1,0:T(8,128)(2,1)}, u32[]{:S(2)}, u32[]{:S(2)}) collective-permute-start(bf16[512,256]{1,0:T(8,128)(2,1)} %slice.9), channel_id=1, source_target_pairs={{0,6},{2,0},{4,2},{6,4},{1,7},{3,1},{5,3},{7,5},{8,14},{10,8},{12,... | collective-permute-start | bytes 786440 | tf_op jit(solution)/shard_map/ppermute | solution.py:282
  53.0 0.7 copy-done.3
  53.6 0.1 copy.9
  53.7 0.2 reduce-window.8
  53.9 0.1 reduce.ends_ref
  54.0 0.2 convert_reduce_fusion
  54.2 4.6 %collective-permute-done.2 = bf16[512,256]{1,0:T(8,128)(2,1)S(1)} collective-permute-done((bf16[512,256]{1,0:T(8,128)(2,1)}, bf16[512,256]{1,0:T(8,128)(2,1)S(1)}, u32[]{:S(2)}, u32[]{:S(2)}) %collective-permute-start.2) | collective-permute-done | bytes 262176 | tf_op jit(solution)/shard_map/ppermute | solution.py:282
  58.9 0.5 collective-permute-done.3
  59.4 1.0 constant_dynamic-update-slice_fusion.far
  60.4 9.3 %pool.2 = (f32[64,2048]{1,0:T(8,128)S(1)}, f32[64,2048]{1,0:T(8,128)S(1)}, f32[1,2048]{1,0:T(1,128)S(1)}) custom-call(s32[1]{0:T(128)} %bitcast.core_ref, s32[16]{0:T(128)S(1)} %add.96.bases_ref, s32[128]{0:T(128)S(1)} %sub.3.starts_ref, s32[128]{0:T(128)S(1)} %reduce.ends_ref, s32[16]{0:T(128)S(1)} %get-tuple-element.22.first_ref, ...), custom_call_target="tpu_custom_call" | custom-call | flops 4294967296 | bytes 5242880 | tf_op jit(solution)/shard_map/pool/pallas_call | solution.py:212
  69.7 0.2 collective-permute-start.6
  69.8 9.3 %pool.3 = (f32[64,2048]{1,0:T(8,128)S(1)}, f32[64,2048]{1,0:T(8,128)S(1)}, f32[1,2048]{1,0:T(1,128)S(1)}) custom-call(s32[1]{0:T(128)} %bitcast.core_ref, s32[16]{0:T(128)S(1)} %add.96.bases_ref, s32[128]{0:T(128)S(1)} %sub.3.starts_ref, s32[128]{0:T(128)S(1)} %reduce.ends_ref, s32[16]{0:T(128)S(1)} %get-tuple-element.22.first_ref, ...), custom_call_target="tpu_custom_call" | custom-call | flops 4294967296 | bytes 5242880 | tf_op jit(solution)/shard_map/pool/pallas_call | solution.py:212
  79.2 1.9 %collective-permute-done.5.got_a = f32[64,2048]{1,0:T(8,128)S(1)} collective-permute-done((f32[64,2048]{1,0:T(8,128)S(1)}, f32[64,2048]{1,0:T(8,128)S(1)}, u32[]{:S(2)}, u32[]{:S(2)}) %collective-permute-start.5) | collective-permute-done | bytes 524320 | tf_op jit(solution)/shard_map/ppermute | solution.py:282
  81.1 1.1 %combine.1 = f32[16,8,2048]{2,1,0:T(8,128)} custom-call(f32[64,2048]{1,0:T(8,128)S(1)} %get-tuple-element.15.keep_a, f32[64,2048]{1,0:T(8,128)S(1)} %collective-permute-done.5.got_a, f32[64,2048]{1,0:T(8,128)S(1)} %get-tuple-element.17.keep_b, f32[64,2048]{1,0:T(8,128)S(1)} %collective-permute-done.6.got_b), custom_call_target="tpu_custom_call" | custom-call | tf_op jit(solution)/shard_map/combine/pallas_call | solution.py:242
  82.2 10.5 %all-to-all-start.2 = ((f32[16,8,2048]{2,1,0:T(8,128)}), f32[16,8,2048]{2,1,0:T(8,128)S(1)}, u32[]{:S(2)}, u32[]{:S(2)}) async-start(f32[16,8,2048]{2,1,0:T(8,128)} %combine.1), calls=%async_computation.2 | async-start | bytes 2097152 | tf_op jit(solution)/shard_map/all_to_all | solution.py:320
  92.7 0.6 copy-done.4
  93.6 14.3 %all-to-all-done.2.pieces_ref = f32[16,8,2048]{2,1,0:T(8,128)S(1)} async-done(((f32[16,8,2048]{2,1,0:T(8,128)}), f32[16,8,2048]{2,1,0:T(8,128)S(1)}, u32[]{:S(2)}, u32[]{:S(2)}) %all-to-all-start.2) | async-done | bytes 1048608 | tf_op jit(solution)/shard_map/all_to_all | solution.py:320
  107.9 1.3 %finish.1 = f32[8,2048]{1,0:T(8,128)} custom-call(s32[2]{0:T(128)S(1)} %pad_add_fusion.place_ref, f32[16,8,2048]{2,1,0:T(8,128)S(1)} %all-to-all-done.2.pieces_ref, f32[1,2048]{1,0:T(1,128)S(1)} %get-tuple-element.19.weight_a, f32[1,2048]{1,0:T(1,128)S(1)} %get-tuple-element.20.weight_b, f32[8,1]{1,0:T(8,128)S(1)} %copy.10.len_ref), custom_call_target="tpu_custom_call" | custom-call | tf_op jit(solution)/shard_map/finish/pallas_call | solution.py:270
  (20 shorter events, 0.6 us)
Async XLA Ops:
  0.0 1.2 %copy-start = (f32[16,16384]{1,0:T(8,128)S(1)}, f32[16,16384]{1,0:T(8,128)}, u32[]{:S(2)}) copy-start(f32[16,16384]{1,0:T(8,128)} %train_ref.1) | copy-start | bytes 3145732
  1.2 0.9 copy-start.1
  2.4 20.9 %copy-start.2 = (s32[32]{0:T(128)S(1)}, s32[32]{0:T(128)}, u32[]{:S(2)}) copy-start(s32[32]{0:T(128)} %slots_ref.1) | copy-start | bytes 388
  26.4 20.9 %all-to-all-start.1 = ((bf16[16,256,128]{2,1,0:T(8,128)(2,1)}), bf16[16,256,128]{2,1,0:T(8,128)(2,1)S(1)}, u32[]{:S(2)}, u32[]{:S(2)}) async-start(bf16[16,256,128]{2,1,0:T(8,128)(2,1)} %broadcast_in_dim.4), calls=%async_computation.1 | async-start | bytes 2097152 | tf_op jit(solution)/shard_map/all_to_all | solution.py:305
  31.7 17.1 %collective-permute-start = (bf16[1024,256]{1,0:T(8,128)(2,1)}, bf16[1024,256]{1,0:T(8,128)(2,1)S(1)}, u32[]{:S(2)}, u32[]{:S(2)}) collective-permute-start(bf16[1024,256]{1,0:T(8,128)(2,1)} %get-tuple-element.13.own), channel_id=1, source_target_pairs={{0,2},{2,4},{4,6},{6,0},{1,3},{3,5},{5,7},{7,1},{8,10},{10,12},{12... | collective-permute-start | bytes 1572872 | tf_op jit(solution)/shard_map/ppermute | solution.py:282
  33.0 17.8 %collective-permute-start.1 = (bf16[1024,256]{1,0:T(8,128)(2,1)}, bf16[1024,256]{1,0:T(8,128)(2,1)S(1)}, u32[]{:S(2)}, u32[]{:S(2)}) collective-permute-start(bf16[1024,256]{1,0:T(8,128)(2,1)} %get-tuple-element.13.own), channel_id=1, source_target_pairs={{0,6},{2,0},{4,2},{6,4},{1,7},{3,1},{5,3},{7,5},{8,14},{10,8},{12,... | collective-permute-start | bytes 1572872 | tf_op jit(solution)/shard_map/ppermute | solution.py:282
  47.3 22.5 %collective-permute-start.4 = (bf16[16,256,128]{2,1,0:T(8,128)(2,1)S(1)}, bf16[16,256,128]{2,1,0:T(8,128)(2,1)S(1)}, u32[]{:S(2)}, u32[]{:S(2)}) collective-permute-start(bf16[16,256,128]{2,1,0:T(8,128)(2,1)S(1)} %all-to-all-done.1.q_ref), channel_id=1, source_target_pairs={{0,8},{8,0},{1,9},{9,1},{2,10},{10,2},{3,11},{11,3},{4,12},{12,4},... | collective-permute-start | bytes 3145736 | tf_op jit(solution)/shard_map/ppermute | solution.py:282
  49.6 9.3 %collective-permute-start.2 = (bf16[512,256]{1,0:T(8,128)(2,1)}, bf16[512,256]{1,0:T(8,128)(2,1)S(1)}, u32[]{:S(2)}, u32[]{:S(2)}) collective-permute-start(bf16[512,256]{1,0:T(8,128)(2,1)} %slice.8), channel_id=1, source_target_pairs={{0,2},{2,4},{4,6},{6,0},{1,3},{3,5},{5,7},{7,1},{8,10},{10,12},{12... | collective-permute-start | bytes 786440 | tf_op jit(solution)/shard_map/ppermute | solution.py:282
  51.5 7.9 %collective-permute-start.3 = (bf16[512,256]{1,0:T(8,128)(2,1)}, bf16[512,256]{1,0:T(8,128)(2,1)}, u32[]{:S(2)}, u32[]{:S(2)}) collective-permute-start(bf16[512,256]{1,0:T(8,128)(2,1)} %slice.9), channel_id=1, source_target_pairs={{0,6},{2,0},{4,2},{6,4},{1,7},{3,1},{5,3},{7,5},{8,14},{10,8},{12,... | collective-permute-start | bytes 786440 | tf_op jit(solution)/shard_map/ppermute | solution.py:282
  53.0 0.7 copy-start.3
  69.7 9.6 %collective-permute-start.6 = (f32[64,2048]{1,0:T(8,128)S(1)}, f32[64,2048]{1,0:T(8,128)S(1)}, u32[]{:S(2)}, u32[]{:S(2)}) collective-permute-start(f32[64,2048]{1,0:T(8,128)S(1)} %get-tuple-element.18), channel_id=1, source_target_pairs={{0,8},{8,0},{1,9},{9,1},{2,10},{10,2},{3,11},{11,3},{4,12},{12,4},... | collective-permute-start | bytes 1572872 | tf_op jit(solution)/shard_map/ppermute | solution.py:282
  79.1 2.0 %collective-permute-start.5 = (f32[64,2048]{1,0:T(8,128)S(1)}, f32[64,2048]{1,0:T(8,128)S(1)}, u32[]{:S(2)}, u32[]{:S(2)}) collective-permute-start(f32[64,2048]{1,0:T(8,128)S(1)} %get-tuple-element.16), channel_id=1, source_target_pairs={{0,8},{8,0},{1,9},{9,1},{2,10},{10,2},{3,11},{11,3},{4,12},{12,4},... | collective-permute-start | bytes 1572872 | tf_op jit(solution)/shard_map/ppermute | solution.py:282
  82.2 25.7 %all-to-all-start.2 = ((f32[16,8,2048]{2,1,0:T(8,128)}), f32[16,8,2048]{2,1,0:T(8,128)S(1)}, u32[]{:S(2)}, u32[]{:S(2)}) async-start(f32[16,8,2048]{2,1,0:T(8,128)} %combine.1), calls=%async_computation.2 | async-start | bytes 2097152 | tf_op jit(solution)/shard_map/all_to_all | solution.py:320
  92.7 0.7 copy-start.4

commit v4 on v3

--- a/solution.py
+++ b/solution.py
@@ -16,7 +16,7 @@
 QPIECE = 128
 TILE = 256
 NBLK = 512
-NTILE = 1024
+BODY = 1024
 NQ_HALF = 2048
 PIECE = RUN + 256 + 3 * QPIECE
 NT_HERE = 4096
@@ -73,7 +73,9 @@
     qc_ref[...] = qc.reshape(CHAINS, PER_CHAIN, QPIECE)
     for s in range(CHAINS):
         qp_ref[s] = qc_ref[slots_ref[s]]
-    q_ref[...] = qp_ref[...].reshape(DRAWS, QPIECE).astype(bf16)
+    paired = qp_ref[...].reshape(DRAWS, QPIECE).astype(bf16)
+    for i in range(16):
+        q_ref[i] = paired
 
     upper = part(RUN)
     mean_ref[...] = (part(RUN + 128)[:, :8] + upper[:, 8:]) + upper[:, :8]
@@ -94,7 +96,7 @@
         ],
         out_shape=(
             jax.ShapeDtypeStruct((RUN, DRAWS), bf16),
-            jax.ShapeDtypeStruct((DRAWS, QPIECE), bf16),
+            jax.ShapeDtypeStruct((16, DRAWS, QPIECE), bf16),
         ),
         out_specs=[pl.BlockSpec(memory_space=pltpu.VMEM)] * 2,
         scratch_shapes=[
@@ -107,17 +109,32 @@
     )(slots, arr)
 
 
-def pool_body(
-    core_ref, bases_ref, starts_ref, ends_ref, first_ref, last_ref,
-    own, left, right, far, q_ref,
-    send_ref, keep_ref, weight_ref,
-    tok, qs, acc, tile_s,
-):
+def rows_kept(block, begin, end):
+    at = lax.broadcasted_iota(jnp.int32, block.shape, 0)
+    inside = (at >= begin) & (at < end)
+    return jnp.where(inside, block.astype(f32), 0.0).astype(bf16)
+
+
+def pool_first_body(core_ref, bases_ref, starts_ref, ends_ref, first_ref, main_ref, last_ref,
+                    own, left, right, far, q_ref,
+                    send_ref, keep_ref, weight_ref, tok, main_tok, qs, acc):
+    i = 0
+    for ref in (own, left, right, far):
+        for r in range(0, RUN, TILE):
+            block = ref[r : r + TILE, :]
+            k = main_ref[i]
+            tok[i * TILE : (i + 1) * TILE, :] = block
+            main_tok[i * TILE : (i + 1) * TILE, :] = rows_kept(
+                block, starts_ref[k] - bases_ref[i], ends_ref[k] - bases_ref[i]
+            )
+            i += 1
+    pool_columns(core_ref, bases_ref, starts_ref, ends_ref, first_ref, main_ref, last_ref,
+                 tok, main_tok, q_ref, send_ref, keep_ref, weight_ref, qs, acc)
+
+
+def pool_columns(core_ref, bases_ref, starts_ref, ends_ref, first_ref, main_ref, last_ref,
+                 tok, main_tok, q_ref, send_ref, keep_ref, weight_ref, qs, acc):
     core = core_ref[0]
-    at = 0
-    for ref in (own, left, right, far):
-        tok[at : at + ref.shape[0], :] = ref[...]
-        at += ref.shape[0]
     for i in range(16):
         o = (i % 2 * 8 + i // 2) * QPIECE
         block = q_ref[i]
@@ -132,100 +149,70 @@
         keep = jnp.where(owner % 2 == core, 1, 0)
         return keep * (DOCS // 2) + owner // 2 * DOC_OWN + k % DOC_OWN
 
-    def products(rows):
-        lhs = tok[pl.ds(rows, TILE), :]
+    def add_sums(lhs, k):
+        row = row_of(k)
         for b in range(NQ_HALF // NBLK):
             where = slice(b * NBLK, (b + 1) * NBLK)
-            yield where, jnp.dot(lhs, qs[:, where], preferred_element_type=f32)
-
-    def many(i, rows):
-        for where, s in products(rows):
-            tile_s[:, where] = s
-        base = bases_ref[i]
-
-        def one_doc(k, _):
-            begin = jnp.maximum(starts_ref[k] - base, 0)
-            end = jnp.minimum(ends_ref[k] - base, TILE)
-            row = row_of(k)
-
-            @pl.loop(0, NQ_HALF // NTILE)
-            def _(n):
-                cols = pl.ds(pl.multiple_of(n * NTILE, NTILE), NTILE)
-
-                def one_group(g, total):
-                    o = pl.multiple_of(g * 8, 8)
-                    s = tile_s[pl.ds(o, 8), cols]
-                    at = lax.broadcasted_iota(jnp.int32, s.shape, 0) + o
-                    inside = (at >= begin) & (at < end)
-                    return total + jnp.where(inside, s * jnp.abs(s), 0.0)
-
-                total = lax.fori_loop(
-                    begin // 8, (end + 7) // 8, one_group, jnp.zeros((8, NTILE), f32)
-                )
-                acc[pl.ds(row, 1), cols] += jnp.sum(total, axis=0, keepdims=True)
-
-            return 0
-
-        lax.fori_loop(first_ref[i], last_ref[i] + 1, one_doc, 0)
-
-    @pl.loop(0, NT_HERE // TILE // 2)
-    def _(pair):
-        tiles = (2 * pair, 2 * pair + 1)
-        rows = [pl.multiple_of(i * TILE, TILE) for i in tiles]
-        extra = [last_ref[i] - first_ref[i] for i in tiles]
-        most = jnp.maximum(extra[0], extra[1])
-
-        @pl.when(most == 0)
+            s = jnp.dot(lhs, qs[:, where], preferred_element_type=f32)
+            acc[pl.ds(row, 1), where] += jnp.sum(s * jnp.abs(s), axis=0, keepdims=True)
+
+    tiles = BODY // TILE
+
+    @pl.loop(0, NT_HERE // BODY)
+    def _(block):
+        for j in range(tiles):
+            i = block * tiles + j
+            add_sums(main_tok[pl.ds(pl.multiple_of(i * TILE, TILE), TILE), :], main_ref[i])
+
+    @pl.loop(0, NT_HERE // TILE)
+    def _(i):
+        @pl.when(first_ref[i] != last_ref[i])
         def _():
-            for i, r in zip(tiles, rows):
-                row = row_of(first_ref[i])
-                for where, s in products(r):
-                    acc[pl.ds(row, 1), where] += jnp.sum(s * jnp.abs(s), axis=0, keepdims=True)
-
-        @pl.when(most == 1)
-        def _():
-            for i, r in zip(tiles, rows):
-                row = row_of(first_ref[i])
-                row_next = row_of(last_ref[i])
-                border = ends_ref[first_ref[i]] - bases_ref[i]
-                upper = lax.broadcasted_iota(jnp.int32, (TILE, NBLK), 0) < border
-                for where, s in products(r):
-                    p = s * jnp.abs(s)
-                    p_upper = jnp.where(upper, p, 0.0)
-                    acc[pl.ds(row, 1), where] += jnp.sum(p_upper, axis=0, keepdims=True)
-                    acc[pl.ds(row_next, 1), where] += jnp.sum(p - p_upper, axis=0, keepdims=True)
-
-        @pl.when(most > 1)
-        def _():
-            @pl.loop(2 * pair, 2 * pair + 2)
-            def _(i):
-                many(i, pl.multiple_of(i * TILE, TILE))
+            base = bases_ref[i]
+            main = main_ref[i]
+
+            def one_doc(k, _):
+                @pl.when(k != main)
+                def _():
+                    half = TILE // 2
+                    o = jnp.where(k > main, half, 0)
+                    rows = pl.multiple_of(i * TILE + o, half)
+                    lhs = rows_kept(
+                        tok[pl.ds(rows, half), :], starts_ref[k] - base - o, ends_ref[k] - base - o
+                    )
+                    add_sums(lhs, k)
+
+                return 0
+
+            lax.fori_loop(first_ref[i], last_ref[i] + 1, one_doc, 0)
 
     send_ref[...] = acc[: DOCS // 2, :]
     keep_ref[...] = acc[DOCS // 2 :, :]
 
 
-def pool(core, bases, starts, ends, first, last, tokens, q):
+def pool(where, tokens, q):
     smem = pl.BlockSpec(memory_space=pltpu.SMEM)
     vmem = pl.BlockSpec(memory_space=pltpu.VMEM)
-    out = jax.ShapeDtypeStruct((DOCS // 2, NQ_HALF), f32)
-    return pl.pallas_call(
-        pool_body,
-        in_specs=[smem] * 6 + [vmem] * 5,
-        out_shape=(out, out, jax.ShapeDtypeStruct((1, NQ_HALF), f32)),
-        out_specs=[vmem] * 3,
+    sums = jax.ShapeDtypeStruct((DOCS // 2, NQ_HALF), f32)
+    shapes = [sums, sums, jax.ShapeDtypeStruct((1, NQ_HALF), f32)]
+    is_first = len(tokens) == 4
+    if is_first:
+        shapes += [jax.ShapeDtypeStruct((NT_HERE, DRAWS), bf16)] * 2
+    return pl.pallas_call(
+        pool_first_body if is_first else pool_columns,
+        in_specs=[smem] * len(where) + [vmem] * (len(tokens) + 1),
+        out_shape=shapes,
+        out_specs=[vmem] * len(shapes),
         scratch_shapes=[
-            pltpu.VMEM((NT_HERE, DRAWS), bf16),
             pltpu.VMEM((DRAWS, NQ_HALF), bf16),
             pltpu.VMEM((DOCS, NQ_HALF), f32),
-            pltpu.VMEM((TILE, NQ_HALF), f32),
         ],
         compiler_params=params(20),
         cost_estimate=pl.CostEstimate(
             flops=2 * NT_HERE * NQ_HALF * DRAWS, bytes_accessed=5 << 20, transcendentals=0
         ),
         name="pool",
-    )(core, bases, starts, ends, first, last, *tokens, q)
+    )(*where, *tokens, q)
 
 
 def combine_body(keep_a, got_a, keep_b, got_b, out_ref):
@@ -288,12 +275,9 @@
     x = lax.axis_index("x")
     t = (lax.axis_index("yl") * 4 + lax.axis_index("z")) * 2 + core
 
-    doc_ends = jnp.cumsum(doc_lengths)
-    doc_starts = doc_ends - doc_lengths
-
     packed = pack(train_losses, query_losses)
     arrived = lax.all_to_all(packed, ("yl", "z", "c"), split_axis=0, concat_axis=0, tiled=True)
-    own, q_own = centre(chain_slots, arrived)
+    own, copies = centre(chain_slots, arrived)
 
     left = shift(own, "x", 1)
     right = shift(own, "x", -1)
@@ -301,21 +285,23 @@
     far_hi = shift(right[RUN // 2 :], "x", -1)
     far = jnp.concatenate([far_lo, far_hi])
 
-    copies = jnp.broadcast_to(q_own, (16, *q_own.shape))
     qa = lax.all_to_all(copies, ("yl", "z", "yh"), split_axis=0, concat_axis=0, tiled=True)
     qb = shift(qa, "c", 1)
 
+    doc_ends = jnp.cumsum(doc_lengths)
+    doc_starts = doc_ends - doc_lengths
     xs = jnp.stack([x, (x + 3) % 4, (x + 1) % 4, (x + 2) % 4])
     run_bases = (xs * 2 + yh) * (16 * RUN) + t * RUN
     bases = (run_bases[:, None] + jnp.arange(RUN // TILE, dtype=jnp.int32) * TILE).reshape(-1)
-    first = jnp.sum(doc_ends[None, :] <= bases[:, None], axis=1, dtype=jnp.int32)
-    last = jnp.sum(doc_ends[None, :] <= bases[:, None] + (TILE - 1), axis=1, dtype=jnp.int32)
-
-    where = (core.reshape(1), bases, doc_starts, doc_ends, first, last)
-    tokens = (own, left, right, far)
-    send_a, keep_a, weight_a = pool(*where, tokens, qa)
+    spots = jnp.stack([bases, bases + TILE // 2, bases + (TILE - 1)])
+    first, main, last = jnp.sum(
+        doc_ends[None, None, :] <= spots[:, :, None], axis=2, dtype=jnp.int32
+    )
+
+    where = (core.reshape(1), bases, doc_starts, doc_ends, first, main, last)
+    send_a, keep_a, weight_a, tok, main_tok = pool(where, (own, left, right, far), qa)
     cross_a = shift(send_a, "c", 1)
-    send_b, keep_b, weight_b = pool(*where, tokens, qb)
+    send_b, keep_b, weight_b = pool(where, (tok, main_tok), qb)
     cross_b = shift(send_b, "c", 1)
     pieces = lax.all_to_all(
         combine(keep_a, cross_b, keep_b, cross_a), ("yl", "z", "yh"),

time: 111 us -> 105 us (0.946)
  local copies, waits for them, and re-layouts: 7.31 us -> 3.23 us
  starting transfers between devices: 22.9 us -> 20.1 us
  waiting for transfers between devices: 34.1 us -> 35.6 us
  Pallas kernels: 23.1 us -> 21.7 us
  other arithmetic: 0.76 us -> 1.87 us
    all_to_all x1, starting transfers between devices: 10.5 us -> 7.65 us  [step(): lax.all_to_all(combine(keep_a, cross_b, keep_b, cross_a), ('yl', 'z', 'yh...]
    pallas_call x2, Pallas kernels: 18.6 us -> 16.7 us  [pool(): pl.pallas_call(pool_first_body if is_first else pool_columns, in_specs=[s...]
    unnamed x11 -> x8, local copies, waits for them, and re-layouts: 3.46 us -> 2.14 us
    broadcast_in_dim x1 -> x0, local copies, waits for them, and re-layouts: 1.17 us -> none  [step(): copies = jnp.broadcast_to(q_own, (16, *q_own.shape))]
  transfers between devices with their start and end apart: 9 -> 9, of which waited for: 5 -> 5; matrix products, arithmetic and copies ran while one was open for 3% -> 3% of each run, Pallas kernels for 17% -> 16%
where the time goes in v4:
time: 105 us; the launch traced here: 104 us
  waiting for transfers between devices  35.6 us (34%)
  Pallas kernels  21.7 us (21%)
  blocking collectives  20.9 us (20%)
  starting transfers between devices  20.1 us (19%)
  local copies, waits for them, and re-layouts  3.23 us (3%)
  other arithmetic  1.87 us (2%)
    all_to_all x1, blocking collectives, step(): lax.all_to_all(packed, ('yl', 'z', 'c'), split_axis=0, concat_axis=0, til...  20.9 us
    pallas_call x2, Pallas kernels, pool(): pl.pallas_call(pool_first_body if is_first else pool_columns, in_specs=[s...  16.7 us
    all_to_all x1, waiting for transfers between devices, step(): lax.all_to_all(combine(keep_a, cross_b, keep_b, cross_a), ('yl', 'z', 'yh...  14.9 us
    all_to_all x1, waiting for transfers between devices, step(): lax.all_to_all(copies, ('yl', 'z', 'yh'), split_axis=0, concat_axis=0, ti...  12.6 us
    ppermute x7, waiting for transfers between devices, shift(): lax.ppermute(value, axis, [(i, (i + by) % size) for i in range(size)])  8.02 us
    all_to_all x1, starting transfers between devices, step(): lax.all_to_all(combine(keep_a, cross_b, keep_b, cross_a), ('yl', 'z', 'yh...  7.65 us
    ppermute x7, starting transfers between devices, shift(): lax.ppermute(value, axis, [(i, (i + by) % size) for i in range(size)])  7.08 us
    all_to_all x1, starting transfers between devices, step(): lax.all_to_all(copies, ('yl', 'z', 'yh'), split_axis=0, concat_axis=0, ti...  5.35 us
  transfers between devices with their start and end apart: 9, of which 5 were waited for; matrix products, arithmetic and copies ran while one was open for 3% of the time, Pallas kernels for 16%

profile of v4, /device:TPU:1, one launch (start us, length us, event | category | flops | bytes accessed | tf_op | source)
XLA Modules:
  0.0 103.5 jit_solution(15372052244133479374)
XLA Ops:
  0.0 1.2 %copy-done = f32[16,16384]{1,0:T(8,128)S(1)} copy-done((f32[16,16384]{1,0:T(8,128)S(1)}, f32[16,16384]{1,0:T(8,128)}, u32[]{:S(2)}) %copy-start) | copy-done | bytes 1048600
  1.2 0.9 copy-done.1
  2.1 0.3 pack.1
  2.4 20.9 %all_to_all.15.arr_ref = bf16[16,16,1664]{2,1,0:T(8,128)(2,1)S(1)} all-to-all(bf16[16,16,1664]{2,1,0:T(8,128)(2,1)S(1)} %pack.1), channel_id=1, replica_groups=mesh['yl'=2,'z'=4,'c'=2,'x'=4,'yh'=2] {'yl','z','c'}, dimensions={0} | all-to-all | bytes 1703936 | tf_op jit(solution)/shard_map/all_to_all | solution.py:279
  23.3 2.3 %centre.1 = (bf16[1024,256]{1,0:T(8,128)(2,1)}, bf16[16,256,128]{2,1,0:T(8,128)(2,1)}) custom-call(s32[32]{0:T(128)S(1)} %copy-done.2, bf16[16,16,1664]{2,1,0:T(8,128)(2,1)S(1)} %all_to_all.15.arr_ref), custom_call_target="tpu_custom_call" | custom-call | tf_op jit(solution)/shard_map/centre/pallas_call | solution.py:91
  25.6 5.4 %all-to-all-start.1 = ((bf16[16,256,128]{2,1,0:T(8,128)(2,1)}), bf16[16,256,128]{2,1,0:T(8,128)(2,1)S(1)}, u32[]{:S(2)}, u32[]{:S(2)}) async-start(bf16[16,256,128]{2,1,0:T(8,128)(2,1)} %get-tuple-element.16), calls=%async_computation.1 | async-start | bytes 2097152 | tf_op jit(solution)/shard_map/all_to_all | solution.py:288
  31.0 0.1 iota_multiply_fusion
  31.1 1.2 %collective-permute-start = (bf16[1024,256]{1,0:T(8,128)(2,1)}, bf16[1024,256]{1,0:T(8,128)(2,1)S(1)}, u32[]{:S(2)}, u32[]{:S(2)}) collective-permute-start(bf16[1024,256]{1,0:T(8,128)(2,1)} %get-tuple-element.15.own), channel_id=1, source_target_pairs={{0,2},{2,4},{4,6},{6,0},{1,3},{3,5},{5,7},{7,1},{8,10},{10,12},{12... | collective-permute-start | bytes 1572872 | tf_op jit(solution)/shard_map/ppermute | solution.py:269
  32.3 1.5 %collective-permute-start.1 = (bf16[1024,256]{1,0:T(8,128)(2,1)}, bf16[1024,256]{1,0:T(8,128)(2,1)S(1)}, u32[]{:S(2)}, u32[]{:S(2)}) collective-permute-start(bf16[1024,256]{1,0:T(8,128)(2,1)} %get-tuple-element.15.own), channel_id=1, source_target_pairs={{0,6},{2,0},{4,2},{6,4},{1,7},{3,1},{5,3},{7,5},{8,14},{10,8},{12,... | collective-permute-start | bytes 1572872 | tf_op jit(solution)/shard_map/ppermute | solution.py:269
  33.9 0.1 add.119
  34.0 12.6 %all-to-all-done.1.q_ref = bf16[16,256,128]{2,1,0:T(8,128)(2,1)S(1)} async-done(((bf16[16,256,128]{2,1,0:T(8,128)(2,1)}), bf16[16,256,128]{2,1,0:T(8,128)(2,1)S(1)}, u32[]{:S(2)}, u32[]{:S(2)}) %all-to-all-start.1) | async-done | bytes 1048608 | tf_op jit(solution)/shard_map/all_to_all | solution.py:288
  46.6 1.4 %collective-permute-start.4 = (bf16[16,256,128]{2,1,0:T(8,128)(2,1)S(1)}, bf16[16,256,128]{2,1,0:T(8,128)(2,1)S(1)}, u32[]{:S(2)}, u32[]{:S(2)}) collective-permute-start(bf16[16,256,128]{2,1,0:T(8,128)(2,1)S(1)} %all-to-all-done.1.q_ref), channel_id=1, source_target_pairs={{0,8},{8,0},{1,9},{9,1},{2,10},{10,2},{3,11},{11,3},{4,12},{12,4},... | collective-permute-start | bytes 3145736 | tf_op jit(solution)/shard_map/ppermute | solution.py:269
  48.0 0.1 copy.9
  48.1 0.2 reduce-window.8
  48.2 0.1 reduce.ends_ref
  48.4 1.3 %collective-permute-start.2 = (bf16[512,256]{1,0:T(8,128)(2,1)S(1)}, bf16[512,256]{1,0:T(8,128)(2,1)}, u32[]{:S(2)}, u32[]{:S(2)}) collective-permute-start(bf16[512,256]{1,0:T(8,128)(2,1)S(1)} %slice.8), channel_id=1, source_target_pairs={{0,2},{2,4},{4,6},{6,0},{1,3},{3,5},{5,7},{7,1},{8,10},{10,12},{12... | collective-permute-start | bytes 786440 | tf_op jit(solution)/shard_map/ppermute | solution.py:269
  49.7 0.7 slice.9
  50.4 1.5 %collective-permute-start.3 = (bf16[512,256]{1,0:T(8,128)(2,1)}, bf16[512,256]{1,0:T(8,128)(2,1)}, u32[]{:S(2)}, u32[]{:S(2)}) collective-permute-start(bf16[512,256]{1,0:T(8,128)(2,1)} %slice.9), channel_id=1, source_target_pairs={{0,6},{2,0},{4,2},{6,4},{1,7},{3,1},{5,3},{7,5},{8,14},{10,8},{12,... | collective-permute-start | bytes 786440 | tf_op jit(solution)/shard_map/ppermute | solution.py:269
  51.9 0.2 convert_reduce_fusion
  52.2 5.5 %collective-permute-done.2 = bf16[512,256]{1,0:T(8,128)(2,1)} collective-permute-done((bf16[512,256]{1,0:T(8,128)(2,1)S(1)}, bf16[512,256]{1,0:T(8,128)(2,1)}, u32[]{:S(2)}, u32[]{:S(2)}) %collective-permute-start.2) | collective-permute-done | bytes 262176 | tf_op jit(solution)/shard_map/ppermute | solution.py:269
  57.6 0.6 collective-permute-done.3
  58.3 1.1 %pad_maximum_fusion.far = bf16[1024,256]{1,0:T(8,128)(2,1)S(1)} fusion(bf16[512,256]{1,0:T(8,128)(2,1)} %collective-permute-done.3, bf16[512,256]{1,0:T(8,128)(2,1)} %collective-permute-done.2), kind=kLoop, calls=%fused_computation | loop fusion | flops 1048576 | bytes 1048576 | tf_op jit(solution)/shard_map/concatenate | solution.py:286
  59.4 8.8 %pool.2 = (f32[64,2048]{1,0:T(8,128)S(1)}, f32[64,2048]{1,0:T(8,128)S(1)}, f32[1,2048]{1,0:T(1,128)S(1)}, bf16[4096,256]{1,0:T(8,128)(2,1)S(1)}, bf16[4096,256]{1,0:T(8,128)(2,1)S(1)}) custom-call(s32[1]{0:T(128)} %bitcast.core_ref, s32[16]{0:T(128)S(1)} %add.118.bases_ref, s32[128]{0:T(128)S(1)} %sub.3.starts_ref, s32[128]{0:T(128)S(1)} %reduce.ends_ref, ...), custom_call_target="tpu_custom_call" | custom-call | flops 4294967296 | bytes 5242880 | tf_op jit(solution)/shard_map/pool/pallas_call | solution.py:201
  68.2 0.2 collective-permute-start.6
  68.4 7.9 %pool.3 = (f32[64,2048]{1,0:T(8,128)S(1)}, f32[64,2048]{1,0:T(8,128)S(1)}, f32[1,2048]{1,0:T(1,128)S(1)}) custom-call(s32[1]{0:T(128)} %bitcast.core_ref, s32[16]{0:T(128)S(1)} %add.118.bases_ref, s32[128]{0:T(128)S(1)} %sub.3.starts_ref, s32[128]{0:T(128)S(1)} %reduce.ends_ref, s32[16]{0:T(128)S(1)} %get-tuple-element.27.first_ref, ...), custom_call_target="tpu_custom_call" | custom-call | flops 4294967296 | bytes 5242880 | tf_op jit(solution)/shard_map/pool/pallas_call | solution.py:201
  76.3 0.1 collective-permute-start.5
  76.4 1.9 %collective-permute-done.5.got_a = f32[64,2048]{1,0:T(8,128)S(1)} collective-permute-done((f32[64,2048]{1,0:T(8,128)S(1)}, f32[64,2048]{1,0:T(8,128)S(1)}, u32[]{:S(2)}, u32[]{:S(2)}) %collective-permute-start.5) | collective-permute-done | bytes 524320 | tf_op jit(solution)/shard_map/ppermute | solution.py:269
  78.3 1.1 %combine.1 = f32[16,8,2048]{2,1,0:T(8,128)} custom-call(f32[64,2048]{1,0:T(8,128)S(1)} %get-tuple-element.17.keep_a, f32[64,2048]{1,0:T(8,128)S(1)} %collective-permute-done.5.got_a, f32[64,2048]{1,0:T(8,128)S(1)} %get-tuple-element.21.keep_b, f32[64,2048]{1,0:T(8,128)S(1)} %collective-permute-done.6.got_b), custom_call_target="tpu_custom_call" | custom-call | tf_op jit(solution)/shard_map/combine/pallas_call | solution.py:229
  79.4 7.6 %all-to-all-start.2 = ((f32[16,8,2048]{2,1,0:T(8,128)}), f32[16,8,2048]{2,1,0:T(8,128)S(1)}, u32[]{:S(2)}, u32[]{:S(2)}) async-start(f32[16,8,2048]{2,1,0:T(8,128)} %combine.1), calls=%async_computation.2 | async-start | bytes 2097152 | tf_op jit(solution)/shard_map/all_to_all | solution.py:306
  87.1 0.1 copy.10.len_ref
  87.3 14.9 %all-to-all-done.2.pieces_ref = f32[16,8,2048]{2,1,0:T(8,128)S(1)} async-done(((f32[16,8,2048]{2,1,0:T(8,128)}), f32[16,8,2048]{2,1,0:T(8,128)S(1)}, u32[]{:S(2)}, u32[]{:S(2)}) %all-to-all-start.2) | async-done | bytes 1048608 | tf_op jit(solution)/shard_map/all_to_all | solution.py:306
  102.2 1.3 %finish.1 = f32[8,2048]{1,0:T(8,128)} custom-call(s32[2]{0:T(128)S(1)} %pad_add_fusion.1.place_ref, f32[16,8,2048]{2,1,0:T(8,128)S(1)} %all-to-all-done.2.pieces_ref, f32[1,2048]{1,0:T(1,128)S(1)} %get-tuple-element.23.weight_a, f32[1,2048]{1,0:T(1,128)S(1)} %get-tuple-element.24.weight_b, f32[8,1]{1,0:T(8,128)S(1)} %copy.10.len_ref), custom_call_target="tpu_custom_call" | custom-call | tf_op jit(solution)/shard_map/finish/pallas_call | solution.py:257
  (19 shorter events, 0.4 us)
Async XLA Ops:
  0.0 1.2 %copy-start = (f32[16,16384]{1,0:T(8,128)S(1)}, f32[16,16384]{1,0:T(8,128)}, u32[]{:S(2)}) copy-start(f32[16,16384]{1,0:T(8,128)} %train_ref.1) | copy-start | bytes 3145732
  1.2 0.9 copy-start.1
  2.1 21.2 %copy-start.2 = (s32[32]{0:T(128)S(1)}, s32[32]{0:T(128)}, u32[]{:S(2)}) copy-start(s32[32]{0:T(128)} %slots_ref.1) | copy-start | bytes 388
  2.4 45.6 %copy-start.3 = (s32[128]{0:T(128)S(1)}, s32[128]{0:T(128)}, u32[]{:S(2)}) copy-start(s32[128]{0:T(128)} %param.7) | copy-start | bytes 1540
  25.6 20.9 %all-to-all-start.1 = ((bf16[16,256,128]{2,1,0:T(8,128)(2,1)}), bf16[16,256,128]{2,1,0:T(8,128)(2,1)S(1)}, u32[]{:S(2)}, u32[]{:S(2)}) async-start(bf16[16,256,128]{2,1,0:T(8,128)(2,1)} %get-tuple-element.16), calls=%async_computation.1 | async-start | bytes 2097152 | tf_op jit(solution)/shard_map/all_to_all | solution.py:288
  31.1 17.2 %collective-permute-start = (bf16[1024,256]{1,0:T(8,128)(2,1)}, bf16[1024,256]{1,0:T(8,128)(2,1)S(1)}, u32[]{:S(2)}, u32[]{:S(2)}) collective-permute-start(bf16[1024,256]{1,0:T(8,128)(2,1)} %get-tuple-element.15.own), channel_id=1, source_target_pairs={{0,2},{2,4},{4,6},{6,0},{1,3},{3,5},{5,7},{7,1},{8,10},{10,12},{12... | collective-permute-start | bytes 1572872 | tf_op jit(solution)/shard_map/ppermute | solution.py:269
  32.3 17.3 %collective-permute-start.1 = (bf16[1024,256]{1,0:T(8,128)(2,1)}, bf16[1024,256]{1,0:T(8,128)(2,1)S(1)}, u32[]{:S(2)}, u32[]{:S(2)}) collective-permute-start(bf16[1024,256]{1,0:T(8,128)(2,1)} %get-tuple-element.15.own), channel_id=1, source_target_pairs={{0,6},{2,0},{4,2},{6,4},{1,7},{3,1},{5,3},{7,5},{8,14},{10,8},{12,... | collective-permute-start | bytes 1572872 | tf_op jit(solution)/shard_map/ppermute | solution.py:269
  46.6 21.8 %collective-permute-start.4 = (bf16[16,256,128]{2,1,0:T(8,128)(2,1)S(1)}, bf16[16,256,128]{2,1,0:T(8,128)(2,1)S(1)}, u32[]{:S(2)}, u32[]{:S(2)}) collective-permute-start(bf16[16,256,128]{2,1,0:T(8,128)(2,1)S(1)} %all-to-all-done.1.q_ref), channel_id=1, source_target_pairs={{0,8},{8,0},{1,9},{9,1},{2,10},{10,2},{3,11},{11,3},{4,12},{12,4},... | collective-permute-start | bytes 3145736 | tf_op jit(solution)/shard_map/ppermute | solution.py:269
  48.4 9.2 %collective-permute-start.2 = (bf16[512,256]{1,0:T(8,128)(2,1)S(1)}, bf16[512,256]{1,0:T(8,128)(2,1)}, u32[]{:S(2)}, u32[]{:S(2)}) collective-permute-start(bf16[512,256]{1,0:T(8,128)(2,1)S(1)} %slice.8), channel_id=1, source_target_pairs={{0,2},{2,4},{4,6},{6,0},{1,3},{3,5},{5,7},{7,1},{8,10},{10,12},{12... | collective-permute-start | bytes 786440 | tf_op jit(solution)/shard_map/ppermute | solution.py:269
  50.4 7.9 %collective-permute-start.3 = (bf16[512,256]{1,0:T(8,128)(2,1)}, bf16[512,256]{1,0:T(8,128)(2,1)}, u32[]{:S(2)}, u32[]{:S(2)}) collective-permute-start(bf16[512,256]{1,0:T(8,128)(2,1)} %slice.9), channel_id=1, source_target_pairs={{0,6},{2,0},{4,2},{6,4},{1,7},{3,1},{5,3},{7,5},{8,14},{10,8},{12,... | collective-permute-start | bytes 786440 | tf_op jit(solution)/shard_map/ppermute | solution.py:269
  68.2 8.2 %collective-permute-start.6 = (f32[64,2048]{1,0:T(8,128)S(1)}, f32[64,2048]{1,0:T(8,128)S(1)}, u32[]{:S(2)}, u32[]{:S(2)}) collective-permute-start(f32[64,2048]{1,0:T(8,128)S(1)} %get-tuple-element.22), channel_id=1, source_target_pairs={{0,8},{8,0},{1,9},{9,1},{2,10},{10,2},{3,11},{11,3},{4,12},{12,4},... | collective-permute-start | bytes 1572872 | tf_op jit(solution)/shard_map/ppermute | solution.py:269
  76.3 2.0 %collective-permute-start.5 = (f32[64,2048]{1,0:T(8,128)S(1)}, f32[64,2048]{1,0:T(8,128)S(1)}, u32[]{:S(2)}, u32[]{:S(2)}) collective-permute-start(f32[64,2048]{1,0:T(8,128)S(1)} %get-tuple-element.20), channel_id=1, source_target_pairs={{0,8},{8,0},{1,9},{9,1},{2,10},{10,2},{3,11},{11,3},{4,12},{12,4},... | collective-permute-start | bytes 1572872 | tf_op jit(solution)/shard_map/ppermute | solution.py:269
  79.4 22.8 %all-to-all-start.2 = ((f32[16,8,2048]{2,1,0:T(8,128)}), f32[16,8,2048]{2,1,0:T(8,128)S(1)}, u32[]{:S(2)}, u32[]{:S(2)}) async-start(f32[16,8,2048]{2,1,0:T(8,128)} %combine.1), calls=%async_computation.2 | async-start | bytes 2097152 | tf_op jit(solution)/shard_map/all_to_all | solution.py:306

commit v5 on v4

--- a/solution.py
+++ b/solution.py
@@ -17,8 +17,9 @@
 TILE = 256
 NBLK = 512
 BODY = 1024
+PACK_MIB = 62
 NQ_HALF = 2048
-PIECE = RUN + 256 + 3 * QPIECE
+PIECE = RUN + 256 + 2 * QPIECE
 NT_HERE = 4096
 
 f32 = jnp.float32
@@ -36,7 +37,15 @@
     return hi, mid, rest - mid
 
 
-def pack_body(train_ref, query_ref, out_ref):
+def pack_body(train_hbm, query_hbm, out_ref, train_ref, query_ref, sem):
+    copies = [
+        pltpu.make_async_copy(query_hbm, query_ref, sem.at[0]),
+        pltpu.make_async_copy(train_hbm, train_ref, sem.at[1]),
+    ]
+    for copy in copies:
+        copy.start()
+    for copy in copies:
+        copy.wait()
     rows = train_ref.shape[0]
     for i in range(16):
         block = train_ref[:, i * RUN : (i + 1) * RUN]
@@ -44,20 +53,30 @@
         out_ref[i, :, :RUN] = (block - mean).astype(bf16)
         stacked = jnp.concatenate([mean[:, j * 128 : (j + 1) * 128] for j in range(8)], axis=0)
         hi, mid, lo = terms(stacked)
-        out_ref[i, :, RUN : RUN + 128] = jnp.concatenate([hi, mid], axis=0).astype(bf16)
-        out_ref[i, :, RUN + 128 : RUN + 256] = jnp.concatenate([lo, lo], axis=0).astype(bf16)
-        for k, term in enumerate(terms(query_ref[:, i * QPIECE : (i + 1) * QPIECE])):
-            o = RUN + 256 + k * QPIECE
-            out_ref[i, :, o : o + QPIECE] = term.astype(bf16)
+        block = query_ref[:, i * QPIECE : (i + 1) * QPIECE]
+        mean = jnp.sum(block, axis=0, keepdims=True) / rows
+        means = terms(mean)
+        low = jnp.concatenate([lo, *means, jnp.zeros((5, 128), f32)], axis=0)
+        o = RUN
+        out_ref[i, :, o : o + 128] = jnp.concatenate([hi, mid], axis=0).astype(bf16)
+        out_ref[i, :, o + 128 : o + 256] = low.astype(bf16)
+        hi, mid, _ = terms(block - mean)
+        out_ref[i, :, o + 256 : o + 384] = hi.astype(bf16)
+        out_ref[i, :, o + 384 : o + 512] = mid.astype(bf16)
 
 
 def pack(train, query):
     return pl.pallas_call(
         pack_body,
-        in_specs=[pl.BlockSpec(memory_space=pltpu.VMEM)] * 2,
+        in_specs=[pl.BlockSpec(memory_space=pltpu.HBM)] * 2,
         out_specs=pl.BlockSpec(memory_space=pltpu.VMEM),
         out_shape=jax.ShapeDtypeStruct((16, train.shape[0], PIECE), bf16),
-        compiler_params=params(16),
+        scratch_shapes=[
+            pltpu.VMEM(train.shape, f32),
+            pltpu.VMEM(query.shape, f32),
+            pltpu.SemaphoreType.DMA((2,)),
+        ],
+        compiler_params=params(PACK_MIB),
         name="pack",
     )(train, query)
 
@@ -66,10 +85,11 @@
     def part(o):
         return arr_ref[:, :, o : o + 128].astype(f32)
 
-    o = RUN + 256
-    query = ((part(o + 2 * QPIECE) + part(o + QPIECE)) + part(o)).reshape(DRAWS, QPIECE)
-    mean = jnp.sum(query, axis=0, keepdims=True) / DRAWS
-    qc = (query - mean).astype(bf16).astype(f32)
+    low = part(RUN + 128)
+    local = (low[:, 10:11] + low[:, 9:10]) + low[:, 8:9]
+    offset = local - jnp.sum(local, axis=0, keepdims=True) / 16
+    query = (part(RUN + 384) + part(RUN + 256)) + offset
+    qc = query.reshape(DRAWS, QPIECE).astype(bf16).astype(f32)
     qc_ref[...] = qc.reshape(CHAINS, PER_CHAIN, QPIECE)
     for s in range(CHAINS):
         qp_ref[s] = qc_ref[slots_ref[s]]
@@ -78,7 +98,7 @@
         q_ref[i] = paired
 
     upper = part(RUN)
-    mean_ref[...] = (part(RUN + 128)[:, :8] + upper[:, 8:]) + upper[:, :8]
+    mean_ref[...] = (low[:, :8] + upper[:, 8:]) + upper[:, :8]
     for j in range(RUN // 128):
         local = mean_ref[:, j : j + 1, :]
         offset = local - jnp.sum(local, axis=0, keepdims=True) / 16
@@ -215,20 +235,20 @@
     )(*where, *tokens, q)
 
 
-def combine_body(keep_a, got_a, keep_b, got_b, out_ref):
+def combine_body(keep_a, got_a, weight_a, keep_b, got_b, weight_b, out_ref):
     half = NQ_HALF // 2
     for d in range(16):
         ylz, yh = d // 2, d % 2
         r = slice(ylz * DOC_OWN, (ylz + 1) * DOC_OWN)
         c = slice(yh * half, (yh + 1) * half)
-        out_ref[d, :, :half] = keep_a[r, c] + got_a[r, c]
-        out_ref[d, :, half:] = keep_b[r, c] + got_b[r, c]
+        out_ref[d, :, :half] = (keep_a[r, c] + got_a[r, c]) * weight_a[:, c]
+        out_ref[d, :, half:] = (keep_b[r, c] + got_b[r, c]) * weight_b[:, c]
 
 
 def combine(*arrays):
     return pl.pallas_call(
         combine_body,
-        in_specs=[pl.BlockSpec(memory_space=pltpu.VMEM)] * 4,
+        in_specs=[pl.BlockSpec(memory_space=pltpu.VMEM)] * 6,
         out_specs=pl.BlockSpec(memory_space=pltpu.VMEM),
         out_shape=jax.ShapeDtypeStruct((16, DOC_OWN, NQ_HALF), f32),
         compiler_params=params(16),
@@ -236,32 +256,26 @@
     )(*arrays)
 
 
-def finish_body(place_ref, pieces_ref, weight_a, weight_b, len_ref, out_ref):
-    core = place_ref[0]
-    yh = place_ref[1]
-    total = pieces_ref[0]
-    for i in range(1, 16):
-        total = total + pieces_ref[i]
-    total = total / len_ref[...]
-    half = NQ_HALF // 2
-    cols = pl.ds(pl.multiple_of(yh * half, half), half)
-    for k, (weight, c) in enumerate(((weight_a, core), (weight_b, 1 - core))):
-        part = total[:, k * half : (k + 1) * half] * weight[:, cols]
+def finish_body(core_ref, total_ref, len_ref, out_ref):
+    core = core_ref[0]
+    total = total_ref[...] / len_ref[...]
+    for k, c in enumerate((core, 1 - core)):
         for ylz in range(8):
             o = pl.multiple_of((ylz * 2 + c) * QPIECE, QPIECE)
-            out_ref[:, pl.ds(o, QPIECE)] = part[:, ylz * QPIECE : (ylz + 1) * QPIECE]
-
-
-def finish(place, pieces, weight_a, weight_b, lengths):
+            i = (k * 8 + ylz) * QPIECE
+            out_ref[:, pl.ds(o, QPIECE)] = total[:, i : i + QPIECE]
+
+
+def finish(core, total, lengths):
     vmem = pl.BlockSpec(memory_space=pltpu.VMEM)
     return pl.pallas_call(
         finish_body,
-        in_specs=[pl.BlockSpec(memory_space=pltpu.SMEM)] + [vmem] * 4,
+        in_specs=[pl.BlockSpec(memory_space=pltpu.SMEM)] + [vmem] * 2,
         out_specs=vmem,
         out_shape=jax.ShapeDtypeStruct((DOC_OWN, NQ_HALF), f32),
         compiler_params=params(16),
         name="finish",
-    )(place, pieces, weight_a, weight_b, lengths)
+    )(core, total, lengths)
 
 
 def shift(value, axis, by):
@@ -303,12 +317,13 @@
     cross_a = shift(send_a, "c", 1)
     send_b, keep_b, weight_b = pool(where, (tok, main_tok), qb)
     cross_b = shift(send_b, "c", 1)
+    sums = combine(keep_a, cross_b, weight_a, keep_b, cross_a, weight_b)
     pieces = lax.all_to_all(
-        combine(keep_a, cross_b, keep_b, cross_a), ("yl", "z", "yh"),
-        split_axis=0, concat_axis=0, tiled=True,
+        sums.astype(jnp.float16), ("yl", "z", "yh"), split_axis=0, concat_axis=0, tiled=True
     )
+    total = jnp.sum(pieces.astype(f32), axis=0)
     lengths = lax.dynamic_slice_in_dim(doc_lengths, t * DOC_OWN, DOC_OWN, 0).astype(f32)
-    return finish(jnp.stack([core, yh]), pieces, weight_a, weight_b, lengths[:, None])
+    return finish(core.reshape(1), total, lengths[:, None])
 
 
 def solution(mesh):

time: 105 us -> 98.7 us (0.940)
  waiting for transfers between devices: 35.6 us -> 30 us
  local copies, waits for them, and re-layouts: 3.23 us -> 1.11 us
    all_to_all x1, waiting for transfers between devices: 14.9 us -> 9.36 us  [step(): lax.all_to_all(sums.astype(jnp.float16), ('yl', 'z', 'yh'), split_axis=0,...]
    pallas_call x1, Pallas kernels: 0.26 us -> 2.49 us  [pack(): pl.pallas_call(pack_body, in_specs=[pl.BlockSpec(memory_space=pltpu.HBM)]...]
    unnamed x8 -> x4, local copies, waits for them, and re-layouts: 2.14 us -> 0.01 us
  transfers between devices with their start and end apart: 9 -> 9, of which waited for: 5 -> 5; matrix products, arithmetic and copies ran while one was open for 3% -> 3% of each run, Pallas kernels for 16% -> 17%
where the time goes in v5:
time: 98.7 us; the launch traced here: 97.1 us
  waiting for transfers between devices  30 us (30%)
  Pallas kernels  22.5 us (23%)
  blocking collectives  20.6 us (21%)
  starting transfers between devices  19.9 us (20%)
  other arithmetic  2.72 us (3%)
  local copies, waits for them, and re-layouts  1.11 us (1%)
    all_to_all x1, blocking collectives, step(): lax.all_to_all(packed, ('yl', 'z', 'c'), split_axis=0, concat_axis=0, til...  20.6 us
    pallas_call x2, Pallas kernels, pool(): pl.pallas_call(pool_first_body if is_first else pool_columns, in_specs=[s...  16.9 us
    all_to_all x1, waiting for transfers between devices, step(): lax.all_to_all(copies, ('yl', 'z', 'yh'), split_axis=0, concat_axis=0, ti...  12.6 us
    all_to_all x1, waiting for transfers between devices, step(): lax.all_to_all(sums.astype(jnp.float16), ('yl', 'z', 'yh'), split_axis=0,...  9.36 us
    ppermute x7, waiting for transfers between devices, shift(): lax.ppermute(value, axis, [(i, (i + by) % size) for i in range(size)])  8.02 us
    all_to_all x1, starting transfers between devices, step(): lax.all_to_all(sums.astype(jnp.float16), ('yl', 'z', 'yh'), split_axis=0,...  7.63 us
    ppermute x7, starting transfers between devices, shift(): lax.ppermute(value, axis, [(i, (i + by) % size) for i in range(size)])  7.12 us
    all_to_all x1, starting transfers between devices, step(): lax.all_to_all(copies, ('yl', 'z', 'yh'), split_axis=0, concat_axis=0, ti...  5.13 us
  transfers between devices with their start and end apart: 9, of which 5 were waited for; matrix products, arithmetic and copies ran while one was open for 3% of the time, Pallas kernels for 17%

profile of v5, /device:TPU:1, one launch (start us, length us, event | category | flops | bytes accessed | tf_op | source)
XLA Modules:
  0.0 97.1 jit_solution(441866196590979770)
XLA Ops:
  0.0 2.5 %pack.1 = bf16[16,16,1536]{2,1,0:T(8,128)(2,1)} custom-call(f32[16,16384]{1,0:T(8,128)} %train_hbm.1, f32[16,2048]{1,0:T(8,128)} %query_hbm.1), custom_call_target="tpu_custom_call" | custom-call | tf_op jit(solution)/shard_map/pack/pallas_call | solution.py:69
  2.5 20.6 %all_to_all.15.arr_ref = bf16[16,16,1536]{2,1,0:T(8,128)(2,1)S(1)} all-to-all(bf16[16,16,1536]{2,1,0:T(8,128)(2,1)} %pack.1), channel_id=1, replica_groups=mesh['yl'=2,'z'=4,'c'=2,'x'=4,'yh'=2] {'yl','z','c'}, dimensions={0} | all-to-all | bytes 1572864 | tf_op jit(solution)/shard_map/all_to_all | solution.py:293
  23.2 2.3 %centre.1 = (bf16[1024,256]{1,0:T(8,128)(2,1)}, bf16[16,256,128]{2,1,0:T(8,128)(2,1)}) custom-call(s32[32]{0:T(128)S(1)} %copy-done, bf16[16,16,1536]{2,1,0:T(8,128)(2,1)S(1)} %all_to_all.15.arr_ref), custom_call_target="tpu_custom_call" | custom-call | tf_op jit(solution)/shard_map/centre/pallas_call | solution.py:111
  25.5 5.1 %all-to-all-start.1 = ((bf16[16,256,128]{2,1,0:T(8,128)(2,1)}), bf16[16,256,128]{2,1,0:T(8,128)(2,1)S(1)}, u32[]{:S(2)}, u32[]{:S(2)}) async-start(bf16[16,256,128]{2,1,0:T(8,128)(2,1)} %get-tuple-element.16), calls=%async_computation.1 | async-start | bytes 2097152 | tf_op jit(solution)/shard_map/all_to_all | solution.py:302
  30.6 0.1 iota_multiply_fusion
  30.7 1.2 %collective-permute-start = (bf16[1024,256]{1,0:T(8,128)(2,1)}, bf16[1024,256]{1,0:T(8,128)(2,1)S(1)}, u32[]{:S(2)}, u32[]{:S(2)}) collective-permute-start(bf16[1024,256]{1,0:T(8,128)(2,1)} %get-tuple-element.15.own), channel_id=1, source_target_pairs={{0,2},{2,4},{4,6},{6,0},{1,3},{3,5},{5,7},{7,1},{8,10},{10,12},{12... | collective-permute-start | bytes 1572872 | tf_op jit(solution)/shard_map/ppermute | solution.py:283
  31.9 1.5 %collective-permute-start.1 = (bf16[1024,256]{1,0:T(8,128)(2,1)}, bf16[1024,256]{1,0:T(8,128)(2,1)S(1)}, u32[]{:S(2)}, u32[]{:S(2)}) collective-permute-start(bf16[1024,256]{1,0:T(8,128)(2,1)} %get-tuple-element.15.own), channel_id=1, source_target_pairs={{0,6},{2,0},{4,2},{6,4},{1,7},{3,1},{5,3},{7,5},{8,14},{10,8},{12,... | collective-permute-start | bytes 1572872 | tf_op jit(solution)/shard_map/ppermute | solution.py:283
  33.5 0.1 add.119
  33.6 12.6 %all-to-all-done.1.q_ref = bf16[16,256,128]{2,1,0:T(8,128)(2,1)S(1)} async-done(((bf16[16,256,128]{2,1,0:T(8,128)(2,1)}), bf16[16,256,128]{2,1,0:T(8,128)(2,1)S(1)}, u32[]{:S(2)}, u32[]{:S(2)}) %all-to-all-start.1) | async-done | bytes 1048608 | tf_op jit(solution)/shard_map/all_to_all | solution.py:302
  46.2 1.4 %collective-permute-start.4 = (bf16[16,256,128]{2,1,0:T(8,128)(2,1)S(1)}, bf16[16,256,128]{2,1,0:T(8,128)(2,1)S(1)}, u32[]{:S(2)}, u32[]{:S(2)}) collective-permute-start(bf16[16,256,128]{2,1,0:T(8,128)(2,1)S(1)} %all-to-all-done.1.q_ref), channel_id=1, source_target_pairs={{0,8},{8,0},{1,9},{9,1},{2,10},{10,2},{3,11},{11,3},{4,12},{12,4},... | collective-permute-start | bytes 3145736 | tf_op jit(solution)/shard_map/ppermute | solution.py:283
  47.6 0.1 copy.9
  47.7 0.2 reduce-window.8
  47.8 0.1 reduce.ends_ref
  48.0 1.3 %collective-permute-start.2 = (bf16[512,256]{1,0:T(8,128)(2,1)S(1)}, bf16[512,256]{1,0:T(8,128)(2,1)}, u32[]{:S(2)}, u32[]{:S(2)}) collective-permute-start(bf16[512,256]{1,0:T(8,128)(2,1)S(1)} %slice.8), channel_id=1, source_target_pairs={{0,2},{2,4},{4,6},{6,0},{1,3},{3,5},{5,7},{7,1},{8,10},{10,12},{12... | collective-permute-start | bytes 786440 | tf_op jit(solution)/shard_map/ppermute | solution.py:283
  49.3 0.7 slice.9
  50.0 1.5 %collective-permute-start.3 = (bf16[512,256]{1,0:T(8,128)(2,1)}, bf16[512,256]{1,0:T(8,128)(2,1)}, u32[]{:S(2)}, u32[]{:S(2)}) collective-permute-start(bf16[512,256]{1,0:T(8,128)(2,1)} %slice.9), channel_id=1, source_target_pairs={{0,6},{2,0},{4,2},{6,4},{1,7},{3,1},{5,3},{7,5},{8,14},{10,8},{12,... | collective-permute-start | bytes 786440 | tf_op jit(solution)/shard_map/ppermute | solution.py:283
  51.5 0.2 convert_reduce_fusion.1
  51.7 0.1 add.118.bases_ref
  51.8 5.5 %collective-permute-done.2 = bf16[512,256]{1,0:T(8,128)(2,1)} collective-permute-done((bf16[512,256]{1,0:T(8,128)(2,1)S(1)}, bf16[512,256]{1,0:T(8,128)(2,1)}, u32[]{:S(2)}, u32[]{:S(2)}) %collective-permute-start.2) | collective-permute-done | bytes 262176 | tf_op jit(solution)/shard_map/ppermute | solution.py:283
  57.2 0.7 collective-permute-done.3
  57.9 1.1 %pad_maximum_fusion.far = bf16[1024,256]{1,0:T(8,128)(2,1)S(1)} fusion(bf16[512,256]{1,0:T(8,128)(2,1)} %collective-permute-done.3, bf16[512,256]{1,0:T(8,128)(2,1)} %collective-permute-done.2), kind=kLoop, calls=%fused_computation.1 | loop fusion | flops 1048576 | bytes 1048576 | tf_op jit(solution)/shard_map/concatenate | solution.py:300
  59.0 9.0 %pool.2 = (f32[64,2048]{1,0:T(8,128)S(1)}, f32[64,2048]{1,0:T(8,128)S(1)}, f32[1,2048]{1,0:T(1,128)S(1)}, bf16[4096,256]{1,0:T(8,128)(2,1)S(1)}, bf16[4096,256]{1,0:T(8,128)(2,1)S(1)}) custom-call(s32[1]{0:T(128)} %bitcast.core_ref, s32[16]{0:T(128)S(1)} %add.118.bases_ref, s32[128]{0:T(128)S(1)} %sub.3.starts_ref, s32[128]{0:T(128)S(1)} %reduce.ends_ref, ...), custom_call_target="tpu_custom_call" | custom-call | flops 4294967296 | bytes 5242880 | tf_op jit(solution)/shard_map/pool/pallas_call | solution.py:221
  67.9 0.2 collective-permute-start.6
  68.2 8.0 %pool.3 = (f32[64,2048]{1,0:T(8,128)S(1)}, f32[64,2048]{1,0:T(8,128)S(1)}, f32[1,2048]{1,0:T(1,128)S(1)}) custom-call(s32[1]{0:T(128)} %bitcast.core_ref, s32[16]{0:T(128)S(1)} %add.118.bases_ref, s32[128]{0:T(128)S(1)} %sub.3.starts_ref, s32[128]{0:T(128)S(1)} %reduce.ends_ref, s32[16]{0:T(128)S(1)} %get-tuple-element.27.first_ref, ...), custom_call_target="tpu_custom_call" | custom-call | flops 4294967296 | bytes 5242880 | tf_op jit(solution)/shard_map/pool/pallas_call | solution.py:221
  76.1 0.1 collective-permute-start.5
  76.2 1.9 %collective-permute-done.5.got_a = f32[64,2048]{1,0:T(8,128)S(1)} collective-permute-done((f32[64,2048]{1,0:T(8,128)S(1)}, f32[64,2048]{1,0:T(8,128)S(1)}, u32[]{:S(2)}, u32[]{:S(2)}) %collective-permute-start.5) | collective-permute-done | bytes 524320 | tf_op jit(solution)/shard_map/ppermute | solution.py:283
  78.1 0.1 combine.1
  78.3 0.9 convert_element_type.13
  79.1 7.6 %all-to-all-start.2 = ((f16[16,8,2048]{2,1,0:T(8,128)(2,1)}), f16[16,8,2048]{2,1,0:T(8,128)(2,1)S(1)}, u32[]{:S(2)}, u32[]{:S(2)}) async-start(f16[16,8,2048]{2,1,0:T(8,128)(2,1)} %convert_element_type.13), calls=%async_computation.2 | async-start | bytes 1048576 | tf_op jit(solution)/shard_map/all_to_all | solution.py:321
  86.8 0.1 copy.10.len_ref
  86.9 9.4 %all-to-all-done.2 = f16[16,8,2048]{2,1,0:T(8,128)(2,1)S(1)} async-done(((f16[16,8,2048]{2,1,0:T(8,128)(2,1)}), f16[16,8,2048]{2,1,0:T(8,128)(2,1)S(1)}, u32[]{:S(2)}, u32[]{:S(2)}) %all-to-all-start.2) | async-done | bytes 524320 | tf_op jit(solution)/shard_map/all_to_all | solution.py:321
  96.4 0.7 finish.1
  (16 shorter events, 0.3 us)
Async XLA Ops:
  0.0 23.2 %copy-start = (s32[32]{0:T(128)S(1)}, s32[32]{0:T(128)}, u32[]{:S(2)}) copy-start(s32[32]{0:T(128)} %slots_ref.1) | copy-start | bytes 388
  2.5 45.0 %copy-start.1 = (s32[128]{0:T(128)S(1)}, s32[128]{0:T(128)}, u32[]{:S(2)}) copy-start(s32[128]{0:T(128)} %param.7) | copy-start | bytes 1540
  25.5 20.7 %all-to-all-start.1 = ((bf16[16,256,128]{2,1,0:T(8,128)(2,1)}), bf16[16,256,128]{2,1,0:T(8,128)(2,1)S(1)}, u32[]{:S(2)}, u32[]{:S(2)}) async-start(bf16[16,256,128]{2,1,0:T(8,128)(2,1)} %get-tuple-element.16), calls=%async_computation.1 | async-start | bytes 2097152 | tf_op jit(solution)/shard_map/all_to_all | solution.py:302
  30.7 17.2 %collective-permute-start = (bf16[1024,256]{1,0:T(8,128)(2,1)}, bf16[1024,256]{1,0:T(8,128)(2,1)S(1)}, u32[]{:S(2)}, u32[]{:S(2)}) collective-permute-start(bf16[1024,256]{1,0:T(8,128)(2,1)} %get-tuple-element.15.own), channel_id=1, source_target_pairs={{0,2},{2,4},{4,6},{6,0},{1,3},{3,5},{5,7},{7,1},{8,10},{10,12},{12... | collective-permute-start | bytes 1572872 | tf_op jit(solution)/shard_map/ppermute | solution.py:283
  31.9 17.3 %collective-permute-start.1 = (bf16[1024,256]{1,0:T(8,128)(2,1)}, bf16[1024,256]{1,0:T(8,128)(2,1)S(1)}, u32[]{:S(2)}, u32[]{:S(2)}) collective-permute-start(bf16[1024,256]{1,0:T(8,128)(2,1)} %get-tuple-element.15.own), channel_id=1, source_target_pairs={{0,6},{2,0},{4,2},{6,4},{1,7},{3,1},{5,3},{7,5},{8,14},{10,8},{12,... | collective-permute-start | bytes 1572872 | tf_op jit(solution)/shard_map/ppermute | solution.py:283
  46.2 22.0 %collective-permute-start.4 = (bf16[16,256,128]{2,1,0:T(8,128)(2,1)S(1)}, bf16[16,256,128]{2,1,0:T(8,128)(2,1)S(1)}, u32[]{:S(2)}, u32[]{:S(2)}) collective-permute-start(bf16[16,256,128]{2,1,0:T(8,128)(2,1)S(1)} %all-to-all-done.1.q_ref), channel_id=1, source_target_pairs={{0,8},{8,0},{1,9},{9,1},{2,10},{10,2},{3,11},{11,3},{4,12},{12,4},... | collective-permute-start | bytes 3145736 | tf_op jit(solution)/shard_map/ppermute | solution.py:283
  48.0 9.2 %collective-permute-start.2 = (bf16[512,256]{1,0:T(8,128)(2,1)S(1)}, bf16[512,256]{1,0:T(8,128)(2,1)}, u32[]{:S(2)}, u32[]{:S(2)}) collective-permute-start(bf16[512,256]{1,0:T(8,128)(2,1)S(1)} %slice.8), channel_id=1, source_target_pairs={{0,2},{2,4},{4,6},{6,0},{1,3},{3,5},{5,7},{7,1},{8,10},{10,12},{12... | collective-permute-start | bytes 786440 | tf_op jit(solution)/shard_map/ppermute | solution.py:283
  50.0 7.9 %collective-permute-start.3 = (bf16[512,256]{1,0:T(8,128)(2,1)}, bf16[512,256]{1,0:T(8,128)(2,1)}, u32[]{:S(2)}, u32[]{:S(2)}) collective-permute-start(bf16[512,256]{1,0:T(8,128)(2,1)} %slice.9), channel_id=1, source_target_pairs={{0,6},{2,0},{4,2},{6,4},{1,7},{3,1},{5,3},{7,5},{8,14},{10,8},{12,... | collective-permute-start | bytes 786440 | tf_op jit(solution)/shard_map/ppermute | solution.py:283
  67.9 8.3 %collective-permute-start.6 = (f32[64,2048]{1,0:T(8,128)S(1)}, f32[64,2048]{1,0:T(8,128)S(1)}, u32[]{:S(2)}, u32[]{:S(2)}) collective-permute-start(f32[64,2048]{1,0:T(8,128)S(1)} %get-tuple-element.23), channel_id=1, source_target_pairs={{0,8},{8,0},{1,9},{9,1},{2,10},{10,2},{3,11},{11,3},{4,12},{12,4},... | collective-permute-start | bytes 1572872 | tf_op jit(solution)/shard_map/ppermute | solution.py:283
  76.1 2.0 %collective-permute-start.5 = (f32[64,2048]{1,0:T(8,128)S(1)}, f32[64,2048]{1,0:T(8,128)S(1)}, u32[]{:S(2)}, u32[]{:S(2)}) collective-permute-start(f32[64,2048]{1,0:T(8,128)S(1)} %get-tuple-element.20), channel_id=1, source_target_pairs={{0,8},{8,0},{1,9},{9,1},{2,10},{10,2},{3,11},{11,3},{4,12},{12,4},... | collective-permute-start | bytes 1572872 | tf_op jit(solution)/shard_map/ppermute | solution.py:283
  79.1 17.2 %all-to-all-start.2 = ((f16[16,8,2048]{2,1,0:T(8,128)(2,1)}), f16[16,8,2048]{2,1,0:T(8,128)(2,1)S(1)}, u32[]{:S(2)}, u32[]{:S(2)}) async-start(f16[16,8,2048]{2,1,0:T(8,128)(2,1)} %convert_element_type.13), calls=%async_computation.2 | async-start | bytes 1048576 | tf_op jit(solution)/shard_map/all_to_all | solution.py:321

commit v6 on v5

--- a/solution.py
+++ b/solution.py
@@ -15,6 +15,8 @@
 RUN = 1024
 QPIECE = 128
 TILE = 256
+SUB = 128
+PASSES = TILE // (SUB // 2)
 NBLK = 512
 BODY = 1024
 PACK_MIB = 62
@@ -38,16 +40,18 @@
 
 
 def pack_body(train_hbm, query_hbm, out_ref, train_ref, query_ref, sem):
-    copies = [
-        pltpu.make_async_copy(query_hbm, query_ref, sem.at[0]),
-        pltpu.make_async_copy(train_hbm, train_ref, sem.at[1]),
-    ]
+    width = train_ref.shape[1] // 4
+    copies = [pltpu.make_async_copy(query_hbm, query_ref, sem.at[4])]
+    for i in range(4):
+        cols = pl.ds(i * width, width)
+        copies.append(pltpu.make_async_copy(train_hbm.at[:, cols], train_ref.at[:, cols], sem.at[i]))
     for copy in copies:
         copy.start()
-    for copy in copies:
-        copy.wait()
+    copies[0].wait()
     rows = train_ref.shape[0]
     for i in range(16):
+        if i % 4 == 0:
+            copies[1 + i // 4].wait()
         block = train_ref[:, i * RUN : (i + 1) * RUN]
         mean = jnp.sum(block, axis=0, keepdims=True) / rows
         out_ref[i, :, :RUN] = (block - mean).astype(bf16)
@@ -74,7 +78,7 @@
         scratch_shapes=[
             pltpu.VMEM(train.shape, f32),
             pltpu.VMEM(query.shape, f32),
-            pltpu.SemaphoreType.DMA((2,)),
+            pltpu.SemaphoreType.DMA((5,)),
         ],
         compiler_params=params(PACK_MIB),
         name="pack",
@@ -137,23 +141,24 @@
 
 def pool_first_body(core_ref, bases_ref, starts_ref, ends_ref, first_ref, main_ref, last_ref,
                     own, left, right, far, q_ref,
-                    send_ref, keep_ref, weight_ref, tok, main_tok, qs, acc):
+                    send_ref, keep_ref, weight_ref, tok, main_tok, qs, acc, *lists):
     i = 0
     for ref in (own, left, right, far):
-        for r in range(0, RUN, TILE):
-            block = ref[r : r + TILE, :]
+        for r in range(0, RUN, SUB):
+            block = ref[r : r + SUB, :]
             k = main_ref[i]
-            tok[i * TILE : (i + 1) * TILE, :] = block
-            main_tok[i * TILE : (i + 1) * TILE, :] = rows_kept(
+            tok[i * SUB : (i + 1) * SUB, :] = block
+            main_tok[i * SUB : (i + 1) * SUB, :] = rows_kept(
                 block, starts_ref[k] - bases_ref[i], ends_ref[k] - bases_ref[i]
             )
             i += 1
     pool_columns(core_ref, bases_ref, starts_ref, ends_ref, first_ref, main_ref, last_ref,
-                 tok, main_tok, q_ref, send_ref, keep_ref, weight_ref, qs, acc)
+                 tok, main_tok, q_ref, send_ref, keep_ref, weight_ref, qs, acc, *lists)
 
 
 def pool_columns(core_ref, bases_ref, starts_ref, ends_ref, first_ref, main_ref, last_ref,
-                 tok, main_tok, q_ref, send_ref, keep_ref, weight_ref, qs, acc):
+                 tok, main_tok, q_ref, send_ref, keep_ref, weight_ref, qs, acc,
+                 picked, sub_list, doc_list):
     core = core_ref[0]
     for i in range(16):
         o = (i % 2 * 8 + i // 2) * QPIECE
@@ -169,42 +174,58 @@
         keep = jnp.where(owner % 2 == core, 1, 0)
         return keep * (DOCS // 2) + owner // 2 * DOC_OWN + k % DOC_OWN
 
-    def add_sums(lhs, k):
-        row = row_of(k)
+    def add_sums(lhs, docs):
+        rows = [row_of(k) for k in docs]
+        size = lhs.shape[0] // len(rows)
         for b in range(NQ_HALF // NBLK):
             where = slice(b * NBLK, (b + 1) * NBLK)
             s = jnp.dot(lhs, qs[:, where], preferred_element_type=f32)
-            acc[pl.ds(row, 1), where] += jnp.sum(s * jnp.abs(s), axis=0, keepdims=True)
-
-    tiles = BODY // TILE
+            p = s * jnp.abs(s)
+            for j, row in enumerate(rows):
+                acc[pl.ds(row, 1), where] += jnp.sum(
+                    p[j * size : (j + 1) * size], axis=0, keepdims=True
+                )
 
     @pl.loop(0, NT_HERE // BODY)
     def _(block):
-        for j in range(tiles):
-            i = block * tiles + j
-            add_sums(main_tok[pl.ds(pl.multiple_of(i * TILE, TILE), TILE), :], main_ref[i])
-
-    @pl.loop(0, NT_HERE // TILE)
-    def _(i):
-        @pl.when(first_ref[i] != last_ref[i])
-        def _():
-            base = bases_ref[i]
-            main = main_ref[i]
-
-            def one_doc(k, _):
-                @pl.when(k != main)
-                def _():
-                    half = TILE // 2
-                    o = jnp.where(k > main, half, 0)
-                    rows = pl.multiple_of(i * TILE + o, half)
-                    lhs = rows_kept(
-                        tok[pl.ds(rows, half), :], starts_ref[k] - base - o, ends_ref[k] - base - o
-                    )
-                    add_sums(lhs, k)
-
-                return 0
-
-            lax.fori_loop(first_ref[i], last_ref[i] + 1, one_doc, 0)
+        for j in range(BODY // TILE):
+            i = block * (BODY // TILE) + j
+            lhs = main_tok[pl.ds(pl.multiple_of(i * TILE, TILE), TILE), :]
+            add_sums(lhs, [main_ref[i * (TILE // SUB) + h] for h in range(TILE // SUB)])
+
+    def list_docs(i, n):
+        def list_doc(k, n):
+            other = k != main_ref[i]
+
+            @pl.when(other)
+            def _():
+                sub_list[n] = i
+                doc_list[n] = k
+
+            return n + other.astype(jnp.int32)
+
+        return lax.fori_loop(first_ref[i], last_ref[i] + 1, list_doc, n)
+
+    extra = lax.fori_loop(0, NT_HERE // SUB, list_docs, 0)
+    half = SUB // 2
+
+    @pl.loop(0, (extra + PASSES - 1) // PASSES)
+    def _(g):
+        docs = []
+        for j in range(PASSES):
+            e = g * PASSES + j
+            at = jnp.minimum(e, extra - 1)
+            i = sub_list[at]
+            k = doc_list[at]
+            o = jnp.where(k > main_ref[i], half, 0)
+            base = bases_ref[i] + o
+            end = jnp.where(e < extra, ends_ref[k] - base, 0)
+            rows = pl.multiple_of(i * SUB + o, half)
+            picked[j * half : (j + 1) * half, :] = rows_kept(
+                tok[pl.ds(rows, half), :], starts_ref[k] - base, end
+            )
+            docs.append(k)
+        add_sums(picked[...], docs)
 
     send_ref[...] = acc[: DOCS // 2, :]
     keep_ref[...] = acc[DOCS // 2 :, :]
@@ -226,6 +247,9 @@
         scratch_shapes=[
             pltpu.VMEM((DRAWS, NQ_HALF), bf16),
             pltpu.VMEM((DOCS, NQ_HALF), f32),
+            pltpu.VMEM((TILE, DRAWS), bf16),
+            pltpu.SMEM((DOCS,), jnp.int32),
+            pltpu.SMEM((DOCS,), jnp.int32),
         ],
         compiler_params=params(20),
         cost_estimate=pl.CostEstimate(
@@ -306,8 +330,8 @@
     doc_starts = doc_ends - doc_lengths
     xs = jnp.stack([x, (x + 3) % 4, (x + 1) % 4, (x + 2) % 4])
     run_bases = (xs * 2 + yh) * (16 * RUN) + t * RUN
-    bases = (run_bases[:, None] + jnp.arange(RUN // TILE, dtype=jnp.int32) * TILE).reshape(-1)
-    spots = jnp.stack([bases, bases + TILE // 2, bases + (TILE - 1)])
+    bases = (run_bases[:, None] + jnp.arange(RUN // SUB, dtype=jnp.int32) * SUB).reshape(-1)
+    spots = jnp.stack([bases, bases + SUB // 2, bases + (SUB - 1)])
     first, main, last = jnp.sum(
         doc_ends[None, None, :] <= spots[:, :, None], axis=2, dtype=jnp.int32
     )

time: 98.7 us -> 97.1 us (0.984)
    all_to_all x1, starting transfers between devices: 7.63 us -> 5.95 us  [step(): lax.all_to_all(sums.astype(jnp.float16), ('yl', 'z', 'yh'), split_axis=0,...]
where the time goes in v6:
time: 97.1 us; the launch traced here: 95.7 us
  waiting for transfers between devices  30.3 us (31%)
  Pallas kernels  21.6 us (22%)
  blocking collectives  20.6 us (21%)
  starting transfers between devices  19.1 us (20%)
  other arithmetic  2.74 us (3%)
  local copies, waits for them, and re-layouts  1.12 us (1%)
    all_to_all x1, blocking collectives, step(): lax.all_to_all(packed, ('yl', 'z', 'c'), split_axis=0, concat_axis=0, til...  20.6 us
    pallas_call x2, Pallas kernels, pool(): pl.pallas_call(pool_first_body if is_first else pool_columns, in_specs=[s...  16.2 us
    all_to_all x1, waiting for transfers between devices, step(): lax.all_to_all(copies, ('yl', 'z', 'yh'), split_axis=0, concat_axis=0, ti...  12.6 us
    all_to_all x1, waiting for transfers between devices, step(): lax.all_to_all(sums.astype(jnp.float16), ('yl', 'z', 'yh'), split_axis=0,...  9.7 us
    ppermute x7, starting transfers between devices, shift(): lax.ppermute(value, axis, [(i, (i + by) % size) for i in range(size)])  8.04 us
    ppermute x7, waiting for transfers between devices, shift(): lax.ppermute(value, axis, [(i, (i + by) % size) for i in range(size)])  8.02 us
    all_to_all x1, starting transfers between devices, step(): lax.all_to_all(sums.astype(jnp.float16), ('yl', 'z', 'yh'), split_axis=0,...  5.95 us
    all_to_all x1, starting transfers between devices, step(): lax.all_to_all(copies, ('yl', 'z', 'yh'), split_axis=0, concat_axis=0, ti...  5.13 us
  transfers between devices with their start and end apart: 9, of which 5 were waited for; matrix products, arithmetic and copies ran while one was open for 3% of the time, Pallas kernels for 17%

profile of v6, /device:TPU:1, one launch (start us, length us, event | category | flops | bytes accessed | tf_op | source)
XLA Modules:
  0.0 95.7 jit_solution(3666123946118399661)
XLA Ops:
  0.0 2.3 %pack.1 = bf16[16,16,1536]{2,1,0:T(8,128)(2,1)} custom-call(f32[16,16384]{1,0:T(8,128)} %train_hbm.1, f32[16,2048]{1,0:T(8,128)} %query_hbm.1), custom_call_target="tpu_custom_call" | custom-call | tf_op jit(solution)/shard_map/pack/pallas_call | solution.py:73
  2.3 20.6 %all_to_all.15.arr_ref = bf16[16,16,1536]{2,1,0:T(8,128)(2,1)S(1)} all-to-all(bf16[16,16,1536]{2,1,0:T(8,128)(2,1)} %pack.1), channel_id=1, replica_groups=mesh['yl'=2,'z'=4,'c'=2,'x'=4,'yh'=2] {'yl','z','c'}, dimensions={0} | all-to-all | bytes 1572864 | tf_op jit(solution)/shard_map/all_to_all | solution.py:317
  23.0 2.3 %centre.1 = (bf16[1024,256]{1,0:T(8,128)(2,1)}, bf16[16,256,128]{2,1,0:T(8,128)(2,1)}) custom-call(s32[32]{0:T(128)S(1)} %copy-done, bf16[16,16,1536]{2,1,0:T(8,128)(2,1)S(1)} %all_to_all.15.arr_ref), custom_call_target="tpu_custom_call" | custom-call | tf_op jit(solution)/shard_map/centre/pallas_call | solution.py:115
  25.3 5.1 %all-to-all-start.1 = ((bf16[16,256,128]{2,1,0:T(8,128)(2,1)}), bf16[16,256,128]{2,1,0:T(8,128)(2,1)S(1)}, u32[]{:S(2)}, u32[]{:S(2)}) async-start(bf16[16,256,128]{2,1,0:T(8,128)(2,1)} %get-tuple-element.16), calls=%async_computation.1 | async-start | bytes 2097152 | tf_op jit(solution)/shard_map/all_to_all | solution.py:326
  30.5 0.1 multiply_add_fusion
  30.5 1.2 %collective-permute-start = (bf16[1024,256]{1,0:T(8,128)(2,1)}, bf16[1024,256]{1,0:T(8,128)(2,1)S(1)}, u32[]{:S(2)}, u32[]{:S(2)}) collective-permute-start(bf16[1024,256]{1,0:T(8,128)(2,1)} %get-tuple-element.15.own), channel_id=1, source_target_pairs={{0,2},{2,4},{4,6},{6,0},{1,3},{3,5},{5,7},{7,1},{8,10},{10,12},{12... | collective-permute-start | bytes 1572872 | tf_op jit(solution)/shard_map/ppermute | solution.py:307
  31.8 1.5 %collective-permute-start.1 = (bf16[1024,256]{1,0:T(8,128)(2,1)}, bf16[1024,256]{1,0:T(8,128)(2,1)S(1)}, u32[]{:S(2)}, u32[]{:S(2)}) collective-permute-start(bf16[1024,256]{1,0:T(8,128)(2,1)} %get-tuple-element.15.own), channel_id=1, source_target_pairs={{0,6},{2,0},{4,2},{6,4},{1,7},{3,1},{5,3},{7,5},{8,14},{10,8},{12,... | collective-permute-start | bytes 1572872 | tf_op jit(solution)/shard_map/ppermute | solution.py:307
  33.3 0.1 add.125
  33.4 12.6 %all-to-all-done.1.q_ref = bf16[16,256,128]{2,1,0:T(8,128)(2,1)S(1)} async-done(((bf16[16,256,128]{2,1,0:T(8,128)(2,1)}), bf16[16,256,128]{2,1,0:T(8,128)(2,1)S(1)}, u32[]{:S(2)}, u32[]{:S(2)}) %all-to-all-start.1) | async-done | bytes 1048608 | tf_op jit(solution)/shard_map/all_to_all | solution.py:326
  46.0 1.4 %collective-permute-start.4 = (bf16[16,256,128]{2,1,0:T(8,128)(2,1)S(1)}, bf16[16,256,128]{2,1,0:T(8,128)(2,1)S(1)}, u32[]{:S(2)}, u32[]{:S(2)}) collective-permute-start(bf16[16,256,128]{2,1,0:T(8,128)(2,1)S(1)} %all-to-all-done.1.q_ref), channel_id=1, source_target_pairs={{0,8},{8,0},{1,9},{9,1},{2,10},{10,2},{3,11},{11,3},{4,12},{12,4},... | collective-permute-start | bytes 3145736 | tf_op jit(solution)/shard_map/ppermute | solution.py:307
  47.4 0.1 copy.9
  47.5 0.2 reduce-window.8
  47.6 0.1 reduce.ends_ref
  47.8 1.3 %collective-permute-start.2 = (bf16[512,256]{1,0:T(8,128)(2,1)S(1)}, bf16[512,256]{1,0:T(8,128)(2,1)}, u32[]{:S(2)}, u32[]{:S(2)}) collective-permute-start(bf16[512,256]{1,0:T(8,128)(2,1)S(1)} %slice.8), channel_id=1, source_target_pairs={{0,2},{2,4},{4,6},{6,0},{1,3},{3,5},{5,7},{7,1},{8,10},{10,12},{12... | collective-permute-start | bytes 786440 | tf_op jit(solution)/shard_map/ppermute | solution.py:307
  49.1 0.7 slice.9
  49.8 1.5 %collective-permute-start.3 = (bf16[512,256]{1,0:T(8,128)(2,1)}, bf16[512,256]{1,0:T(8,128)(2,1)}, u32[]{:S(2)}, u32[]{:S(2)}) collective-permute-start(bf16[512,256]{1,0:T(8,128)(2,1)} %slice.9), channel_id=1, source_target_pairs={{0,6},{2,0},{4,2},{6,4},{1,7},{3,1},{5,3},{7,5},{8,14},{10,8},{12,... | collective-permute-start | bytes 786440 | tf_op jit(solution)/shard_map/ppermute | solution.py:307
  51.3 0.2 convert_reduce_fusion.1
  51.5 0.1 add.124.bases_ref
  51.6 5.5 %collective-permute-done.2 = bf16[512,256]{1,0:T(8,128)(2,1)} collective-permute-done((bf16[512,256]{1,0:T(8,128)(2,1)S(1)}, bf16[512,256]{1,0:T(8,128)(2,1)}, u32[]{:S(2)}, u32[]{:S(2)}) %collective-permute-start.2) | collective-permute-done | bytes 262176 | tf_op jit(solution)/shard_map/ppermute | solution.py:307
  57.0 0.7 collective-permute-done.3
  57.7 1.1 %pad_maximum_fusion.far = bf16[1024,256]{1,0:T(8,128)(2,1)S(1)} fusion(bf16[512,256]{1,0:T(8,128)(2,1)} %collective-permute-done.3, bf16[512,256]{1,0:T(8,128)(2,1)} %collective-permute-done.2), kind=kLoop, calls=%fused_computation.1 | loop fusion | flops 1048576 | bytes 1048576 | tf_op jit(solution)/shard_map/concatenate | solution.py:324
  58.8 8.6 %pool.2 = (f32[64,2048]{1,0:T(8,128)S(1)}, f32[64,2048]{1,0:T(8,128)S(1)}, f32[1,2048]{1,0:T(1,128)S(1)}, bf16[4096,256]{1,0:T(8,128)(2,1)S(1)}, bf16[4096,256]{1,0:T(8,128)(2,1)S(1)}) custom-call(s32[1]{0:T(128)} %bitcast.core_ref, s32[32]{0:T(128)S(1)} %add.124.bases_ref, s32[128]{0:T(128)S(1)} %sub.3.starts_ref, s32[128]{0:T(128)S(1)} %reduce.ends_ref, ...), custom_call_target="tpu_custom_call" | custom-call | flops 4294967296 | bytes 5242880 | tf_op jit(solution)/shard_map/pool/pallas_call | solution.py:242
  67.4 1.2 %collective-permute-start.6 = (f32[64,2048]{1,0:T(8,128)S(1)}, f32[64,2048]{1,0:T(8,128)S(1)}, u32[]{:S(2)}, u32[]{:S(2)}) collective-permute-start(f32[64,2048]{1,0:T(8,128)S(1)} %get-tuple-element.23), channel_id=1, source_target_pairs={{0,8},{8,0},{1,9},{9,1},{2,10},{10,2},{3,11},{11,3},{4,12},{12,4},... | collective-permute-start | bytes 1572872 | tf_op jit(solution)/shard_map/ppermute | solution.py:307
  68.6 7.6 %pool.3 = (f32[64,2048]{1,0:T(8,128)S(1)}, f32[64,2048]{1,0:T(8,128)S(1)}, f32[1,2048]{1,0:T(1,128)S(1)}) custom-call(s32[1]{0:T(128)} %bitcast.core_ref, s32[32]{0:T(128)S(1)} %add.124.bases_ref, s32[128]{0:T(128)S(1)} %sub.3.starts_ref, s32[128]{0:T(128)S(1)} %reduce.ends_ref, s32[32]{0:T(128)S(1)} %get-tuple-element.27.first_ref, ...), custom_call_target="tpu_custom_call" | custom-call | flops 4294967296 | bytes 5242880 | tf_op jit(solution)/shard_map/pool/pallas_call | solution.py:242
  76.1 0.1 collective-permute-start.5
  76.2 1.9 %collective-permute-done.5.got_a = f32[64,2048]{1,0:T(8,128)S(1)} collective-permute-done((f32[64,2048]{1,0:T(8,128)S(1)}, f32[64,2048]{1,0:T(8,128)S(1)}, u32[]{:S(2)}, u32[]{:S(2)}) %collective-permute-start.5) | collective-permute-done | bytes 524320 | tf_op jit(solution)/shard_map/ppermute | solution.py:307
  78.1 0.1 combine.1
  78.3 0.9 convert_element_type.13
  79.1 6.0 %all-to-all-start.2 = ((f16[16,8,2048]{2,1,0:T(8,128)(2,1)}), f16[16,8,2048]{2,1,0:T(8,128)(2,1)S(1)}, u32[]{:S(2)}, u32[]{:S(2)}) async-start(f16[16,8,2048]{2,1,0:T(8,128)(2,1)} %convert_element_type.13), calls=%async_computation.2 | async-start | bytes 1048576 | tf_op jit(solution)/shard_map/all_to_all | solution.py:345
  85.2 0.1 copy.10.len_ref
  85.3 9.7 %all-to-all-done.2 = f16[16,8,2048]{2,1,0:T(8,128)(2,1)S(1)} async-done(((f16[16,8,2048]{2,1,0:T(8,128)(2,1)}), f16[16,8,2048]{2,1,0:T(8,128)(2,1)S(1)}, u32[]{:S(2)}, u32[]{:S(2)}) %all-to-all-start.2) | async-done | bytes 524320 | tf_op jit(solution)/shard_map/all_to_all | solution.py:345
  95.0 0.7 finish.1
  (17 shorter events, 0.3 us)
Async XLA Ops:
  0.0 23.0 %copy-start = (s32[32]{0:T(128)S(1)}, s32[32]{0:T(128)}, u32[]{:S(2)}) copy-start(s32[32]{0:T(128)} %slots_ref.1) | copy-start | bytes 388
  2.3 45.1 %copy-start.1 = (s32[128]{0:T(128)S(1)}, s32[128]{0:T(128)}, u32[]{:S(2)}) copy-start(s32[128]{0:T(128)} %param.7) | copy-start | bytes 1540
  25.3 20.7 %all-to-all-start.1 = ((bf16[16,256,128]{2,1,0:T(8,128)(2,1)}), bf16[16,256,128]{2,1,0:T(8,128)(2,1)S(1)}, u32[]{:S(2)}, u32[]{:S(2)}) async-start(bf16[16,256,128]{2,1,0:T(8,128)(2,1)} %get-tuple-element.16), calls=%async_computation.1 | async-start | bytes 2097152 | tf_op jit(solution)/shard_map/all_to_all | solution.py:326
  30.5 17.2 %collective-permute-start = (bf16[1024,256]{1,0:T(8,128)(2,1)}, bf16[1024,256]{1,0:T(8,128)(2,1)S(1)}, u32[]{:S(2)}, u32[]{:S(2)}) collective-permute-start(bf16[1024,256]{1,0:T(8,128)(2,1)} %get-tuple-element.15.own), channel_id=1, source_target_pairs={{0,2},{2,4},{4,6},{6,0},{1,3},{3,5},{5,7},{7,1},{8,10},{10,12},{12... | collective-permute-start | bytes 1572872 | tf_op jit(solution)/shard_map/ppermute | solution.py:307
  31.8 17.3 %collective-permute-start.1 = (bf16[1024,256]{1,0:T(8,128)(2,1)}, bf16[1024,256]{1,0:T(8,128)(2,1)S(1)}, u32[]{:S(2)}, u32[]{:S(2)}) collective-permute-start(bf16[1024,256]{1,0:T(8,128)(2,1)} %get-tuple-element.15.own), channel_id=1, source_target_pairs={{0,6},{2,0},{4,2},{6,4},{1,7},{3,1},{5,3},{7,5},{8,14},{10,8},{12,... | collective-permute-start | bytes 1572872 | tf_op jit(solution)/shard_map/ppermute | solution.py:307
  46.0 22.6 %collective-permute-start.4 = (bf16[16,256,128]{2,1,0:T(8,128)(2,1)S(1)}, bf16[16,256,128]{2,1,0:T(8,128)(2,1)S(1)}, u32[]{:S(2)}, u32[]{:S(2)}) collective-permute-start(bf16[16,256,128]{2,1,0:T(8,128)(2,1)S(1)} %all-to-all-done.1.q_ref), channel_id=1, source_target_pairs={{0,8},{8,0},{1,9},{9,1},{2,10},{10,2},{3,11},{11,3},{4,12},{12,4},... | collective-permute-start | bytes 3145736 | tf_op jit(solution)/shard_map/ppermute | solution.py:307
  47.8 9.2 %collective-permute-start.2 = (bf16[512,256]{1,0:T(8,128)(2,1)S(1)}, bf16[512,256]{1,0:T(8,128)(2,1)}, u32[]{:S(2)}, u32[]{:S(2)}) collective-permute-start(bf16[512,256]{1,0:T(8,128)(2,1)S(1)} %slice.8), channel_id=1, source_target_pairs={{0,2},{2,4},{4,6},{6,0},{1,3},{3,5},{5,7},{7,1},{8,10},{10,12},{12... | collective-permute-start | bytes 786440 | tf_op jit(solution)/shard_map/ppermute | solution.py:307
  49.8 7.9 %collective-permute-start.3 = (bf16[512,256]{1,0:T(8,128)(2,1)}, bf16[512,256]{1,0:T(8,128)(2,1)}, u32[]{:S(2)}, u32[]{:S(2)}) collective-permute-start(bf16[512,256]{1,0:T(8,128)(2,1)} %slice.9), channel_id=1, source_target_pairs={{0,6},{2,0},{4,2},{6,4},{1,7},{3,1},{5,3},{7,5},{8,14},{10,8},{12,... | collective-permute-start | bytes 786440 | tf_op jit(solution)/shard_map/ppermute | solution.py:307
  67.4 8.8 %collective-permute-start.6 = (f32[64,2048]{1,0:T(8,128)S(1)}, f32[64,2048]{1,0:T(8,128)S(1)}, u32[]{:S(2)}, u32[]{:S(2)}) collective-permute-start(f32[64,2048]{1,0:T(8,128)S(1)} %get-tuple-element.23), channel_id=1, source_target_pairs={{0,8},{8,0},{1,9},{9,1},{2,10},{10,2},{3,11},{11,3},{4,12},{12,4},... | collective-permute-start | bytes 1572872 | tf_op jit(solution)/shard_map/ppermute | solution.py:307
  76.1 2.0 %collective-permute-start.5 = (f32[64,2048]{1,0:T(8,128)S(1)}, f32[64,2048]{1,0:T(8,128)S(1)}, u32[]{:S(2)}, u32[]{:S(2)}) collective-permute-start(f32[64,2048]{1,0:T(8,128)S(1)} %get-tuple-element.20), channel_id=1, source_target_pairs={{0,8},{8,0},{1,9},{9,1},{2,10},{10,2},{3,11},{11,3},{4,12},{12,4},... | collective-permute-start | bytes 1572872 | tf_op jit(solution)/shard_map/ppermute | solution.py:307
  79.1 15.8 %all-to-all-start.2 = ((f16[16,8,2048]{2,1,0:T(8,128)(2,1)}), f16[16,8,2048]{2,1,0:T(8,128)(2,1)S(1)}, u32[]{:S(2)}, u32[]{:S(2)}) async-start(f16[16,8,2048]{2,1,0:T(8,128)(2,1)} %convert_element_type.13), calls=%async_computation.2 | async-start | bytes 1048576 | tf_op jit(solution)/shard_map/all_to_all | solution.py:345

commit v7 on v6

--- a/solution.py
+++ b/solution.py
@@ -18,7 +18,7 @@
 SUB = 128
 PASSES = TILE // (SUB // 2)
 NBLK = 512
-BODY = 1024
+BODY = 2048
 PACK_MIB = 62
 NQ_HALF = 2048
 PIECE = RUN + 256 + 2 * QPIECE
@@ -39,7 +39,7 @@
     return hi, mid, rest - mid
 
 
-def pack_body(train_hbm, query_hbm, out_ref, train_ref, query_ref, sem):
+def pack_body(train_hbm, query_hbm, out_hbm, train_ref, query_ref, out_ref, sem, out_sem):
     width = train_ref.shape[1] // 4
     copies = [pltpu.make_async_copy(query_hbm, query_ref, sem.at[4])]
     for i in range(4):
@@ -47,11 +47,17 @@
         copies.append(pltpu.make_async_copy(train_hbm.at[:, cols], train_ref.at[:, cols], sem.at[i]))
     for copy in copies:
         copy.start()
+    out_copies = []
+    for i in range(4):
+        part = pl.ds(i * 4, 4)
+        out_copies.append(pltpu.make_async_copy(out_ref.at[part], out_hbm.at[part], out_sem.at[i]))
     copies[0].wait()
     rows = train_ref.shape[0]
     for i in range(16):
         if i % 4 == 0:
             copies[1 + i // 4].wait()
+        if i % 4 == 1 and i > 4:
+            out_copies[i // 4 - 1].start()
         block = train_ref[:, i * RUN : (i + 1) * RUN]
         mean = jnp.sum(block, axis=0, keepdims=True) / rows
         out_ref[i, :, :RUN] = (block - mean).astype(bf16)
@@ -67,25 +73,30 @@
         hi, mid, _ = terms(block - mean)
         out_ref[i, :, o + 256 : o + 384] = hi.astype(bf16)
         out_ref[i, :, o + 384 : o + 512] = mid.astype(bf16)
+    out_copies[3].start()
+    for copy in out_copies:
+        copy.wait()
 
 
 def pack(train, query):
     return pl.pallas_call(
         pack_body,
         in_specs=[pl.BlockSpec(memory_space=pltpu.HBM)] * 2,
-        out_specs=pl.BlockSpec(memory_space=pltpu.VMEM),
+        out_specs=pl.BlockSpec(memory_space=pltpu.HBM),
         out_shape=jax.ShapeDtypeStruct((16, train.shape[0], PIECE), bf16),
         scratch_shapes=[
             pltpu.VMEM(train.shape, f32),
             pltpu.VMEM(query.shape, f32),
+            pltpu.VMEM((16, train.shape[0], PIECE), bf16),
             pltpu.SemaphoreType.DMA((5,)),
+            pltpu.SemaphoreType.DMA((4,)),
         ],
         compiler_params=params(PACK_MIB),
         name="pack",
     )(train, query)
 
 
-def centre_body(slots_ref, arr_ref, u_ref, q_ref, qc_ref, qp_ref, mean_ref):
+def centre_body(slots_ref, arr_ref, u_ref, q_out, qc_ref, qp_ref, mean_ref, q_ref, sem):
     def part(o):
         return arr_ref[:, :, o : o + 128].astype(f32)
 
@@ -97,9 +108,7 @@
     qc_ref[...] = qc.reshape(CHAINS, PER_CHAIN, QPIECE)
     for s in range(CHAINS):
         qp_ref[s] = qc_ref[slots_ref[s]]
-    paired = qp_ref[...].reshape(DRAWS, QPIECE).astype(bf16)
-    for i in range(16):
-        q_ref[i] = paired
+    q_ref[...] = qp_ref[...].reshape(DRAWS, QPIECE).astype(bf16)
 
     upper = part(RUN)
     mean_ref[...] = (low[:, :8] + upper[:, 8:]) + upper[:, :8]
@@ -109,6 +118,14 @@
         c = (part(j * 128) + offset).reshape(DRAWS, 128).astype(bf16).astype(f32)
         scale = lax.rsqrt(jnp.sum(c * c, axis=0, keepdims=True) / (DRAWS - 1) + EPS)
         u_ref[j * 128 : (j + 1) * 128, :] = (c * scale).T.astype(bf16)
+        if j == 0:
+            copies = [
+                pltpu.make_async_copy(q_ref, q_out.at[i], sem.at[i]) for i in range(16)
+            ]
+            for copy in copies:
+                copy.start()
+    for copy in copies:
+        copy.wait()
 
 
 def centre(slots, arr):
@@ -122,11 +139,16 @@
             jax.ShapeDtypeStruct((RUN, DRAWS), bf16),
             jax.ShapeDtypeStruct((16, DRAWS, QPIECE), bf16),
         ),
-        out_specs=[pl.BlockSpec(memory_space=pltpu.VMEM)] * 2,
+        out_specs=[
+            pl.BlockSpec(memory_space=pltpu.VMEM),
+            pl.BlockSpec(memory_space=pltpu.HBM),
+        ],
         scratch_shapes=[
             pltpu.VMEM((CHAINS, PER_CHAIN, QPIECE), f32),
             pltpu.VMEM((CHAINS, PER_CHAIN, QPIECE), f32),
             pltpu.VMEM((16, 8, 128), f32),
+            pltpu.VMEM((DRAWS, QPIECE), bf16),
+            pltpu.SemaphoreType.DMA((16,)),
         ],
         compiler_params=params(16),
         name="centre",

time: 97.1 us -> 97 us (level)
  transfers between devices with their start and end apart: 9 -> 9, of which waited for: 5 -> 5; matrix products, arithmetic and copies ran while one was open for 3% -> 3% of each run, Pallas kernels for 17% -> 16%
where the time goes in v7:
time: 97 us; the launch traced here: 95.6 us
  waiting for transfers between devices  30.3 us (31%)
  Pallas kernels  21.5 us (22%)
  blocking collectives  20.6 us (21%)
  starting transfers between devices  19.2 us (20%)
  other arithmetic  2.74 us (3%)
  local copies, waits for them, and re-layouts  1.12 us (1%)
    all_to_all x1, blocking collectives, step(): lax.all_to_all(packed, ('yl', 'z', 'c'), split_axis=0, concat_axis=0, til...  20.6 us
    pallas_call x2, Pallas kernels, pool(): pl.pallas_call(pool_first_body if is_first else pool_columns, in_specs=[s...  15.5 us
    all_to_all x1, waiting for transfers between devices, step(): lax.all_to_all(copies, ('yl', 'z', 'yh'), split_axis=0, concat_axis=0, ti...  12.6 us
    all_to_all x1, waiting for transfers between devices, step(): lax.all_to_all(sums.astype(jnp.float16), ('yl', 'z', 'yh'), split_axis=0,...  9.7 us
    ppermute x7, starting transfers between devices, shift(): lax.ppermute(value, axis, [(i, (i + by) % size) for i in range(size)])  8.08 us
    ppermute x7, waiting for transfers between devices, shift(): lax.ppermute(value, axis, [(i, (i + by) % size) for i in range(size)])  8.02 us
    all_to_all x1, starting transfers between devices, step(): lax.all_to_all(sums.astype(jnp.float16), ('yl', 'z', 'yh'), split_axis=0,...  5.95 us
    all_to_all x1, starting transfers between devices, step(): lax.all_to_all(copies, ('yl', 'z', 'yh'), split_axis=0, concat_axis=0, ti...  5.14 us
  transfers between devices with their start and end apart: 9, of which 5 were waited for; matrix products, arithmetic and copies ran while one was open for 3% of the time, Pallas kernels for 16%

profile of v7, /device:TPU:1, one launch (start us, length us, event | category | flops | bytes accessed | tf_op | source)
XLA Modules:
  0.0 95.6 jit_solution(16028878965171913011)
XLA Ops:
  0.0 2.1 %pack.1 = bf16[16,16,1536]{2,1,0:T(8,128)(2,1)} custom-call(f32[16,16384]{1,0:T(8,128)} %train_hbm.1, f32[16,2048]{1,0:T(8,128)} %query_hbm.1), custom_call_target="tpu_custom_call" | custom-call | tf_op jit(solution)/shard_map/pack/pallas_call | solution.py:82
  2.2 20.6 %all_to_all.15.arr_ref = bf16[16,16,1536]{2,1,0:T(8,128)(2,1)S(1)} all-to-all(bf16[16,16,1536]{2,1,0:T(8,128)(2,1)} %pack.1), channel_id=1, replica_groups=mesh['yl'=2,'z'=4,'c'=2,'x'=4,'yh'=2] {'yl','z','c'}, dimensions={0} | all-to-all | bytes 1572864 | tf_op jit(solution)/shard_map/all_to_all | solution.py:339
  22.8 3.0 %centre.1 = (bf16[1024,256]{1,0:T(8,128)(2,1)}, bf16[16,256,128]{2,1,0:T(8,128)(2,1)}) custom-call(s32[32]{0:T(128)S(1)} %copy-done, bf16[16,16,1536]{2,1,0:T(8,128)(2,1)S(1)} %all_to_all.15.arr_ref), custom_call_target="tpu_custom_call" | custom-call | tf_op jit(solution)/shard_map/centre/pallas_call | solution.py:132
  25.8 5.1 %all-to-all-start.1 = ((bf16[16,256,128]{2,1,0:T(8,128)(2,1)}), bf16[16,256,128]{2,1,0:T(8,128)(2,1)S(1)}, u32[]{:S(2)}, u32[]{:S(2)}) async-start(bf16[16,256,128]{2,1,0:T(8,128)(2,1)} %get-tuple-element.16), calls=%async_computation.1 | async-start | bytes 2097152 | tf_op jit(solution)/shard_map/all_to_all | solution.py:348
  31.0 0.1 multiply_add_fusion
  31.1 1.2 %collective-permute-start = (bf16[1024,256]{1,0:T(8,128)(2,1)}, bf16[1024,256]{1,0:T(8,128)(2,1)S(1)}, u32[]{:S(2)}, u32[]{:S(2)}) collective-permute-start(bf16[1024,256]{1,0:T(8,128)(2,1)} %get-tuple-element.15.own), channel_id=1, source_target_pairs={{0,2},{2,4},{4,6},{6,0},{1,3},{3,5},{5,7},{7,1},{8,10},{10,12},{12... | collective-permute-start | bytes 1572872 | tf_op jit(solution)/shard_map/ppermute | solution.py:329
  32.3 1.5 %collective-permute-start.1 = (bf16[1024,256]{1,0:T(8,128)(2,1)}, bf16[1024,256]{1,0:T(8,128)(2,1)S(1)}, u32[]{:S(2)}, u32[]{:S(2)}) collective-permute-start(bf16[1024,256]{1,0:T(8,128)(2,1)} %get-tuple-element.15.own), channel_id=1, source_target_pairs={{0,6},{2,0},{4,2},{6,4},{1,7},{3,1},{5,3},{7,5},{8,14},{10,8},{12,... | collective-permute-start | bytes 1572872 | tf_op jit(solution)/shard_map/ppermute | solution.py:329
  33.9 0.1 add.125
  33.9 12.6 %all-to-all-done.1.q_ref = bf16[16,256,128]{2,1,0:T(8,128)(2,1)S(1)} async-done(((bf16[16,256,128]{2,1,0:T(8,128)(2,1)}), bf16[16,256,128]{2,1,0:T(8,128)(2,1)S(1)}, u32[]{:S(2)}, u32[]{:S(2)}) %all-to-all-start.1) | async-done | bytes 1048608 | tf_op jit(solution)/shard_map/all_to_all | solution.py:348
  46.5 1.4 %collective-permute-start.4 = (bf16[16,256,128]{2,1,0:T(8,128)(2,1)S(1)}, bf16[16,256,128]{2,1,0:T(8,128)(2,1)S(1)}, u32[]{:S(2)}, u32[]{:S(2)}) collective-permute-start(bf16[16,256,128]{2,1,0:T(8,128)(2,1)S(1)} %all-to-all-done.1.q_ref), channel_id=1, source_target_pairs={{0,8},{8,0},{1,9},{9,1},{2,10},{10,2},{3,11},{11,3},{4,12},{12,4},... | collective-permute-start | bytes 3145736 | tf_op jit(solution)/shard_map/ppermute | solution.py:329
  47.9 0.1 copy.9
  48.0 0.2 reduce-window.8
  48.2 0.1 reduce.ends_ref
  48.4 1.3 %collective-permute-start.2 = (bf16[512,256]{1,0:T(8,128)(2,1)S(1)}, bf16[512,256]{1,0:T(8,128)(2,1)}, u32[]{:S(2)}, u32[]{:S(2)}) collective-permute-start(bf16[512,256]{1,0:T(8,128)(2,1)S(1)} %slice.8), channel_id=1, source_target_pairs={{0,2},{2,4},{4,6},{6,0},{1,3},{3,5},{5,7},{7,1},{8,10},{10,12},{12... | collective-permute-start | bytes 786440 | tf_op jit(solution)/shard_map/ppermute | solution.py:329
  49.7 0.7 slice.9
  50.4 1.5 %collective-permute-start.3 = (bf16[512,256]{1,0:T(8,128)(2,1)}, bf16[512,256]{1,0:T(8,128)(2,1)}, u32[]{:S(2)}, u32[]{:S(2)}) collective-permute-start(bf16[512,256]{1,0:T(8,128)(2,1)} %slice.9), channel_id=1, source_target_pairs={{0,6},{2,0},{4,2},{6,4},{1,7},{3,1},{5,3},{7,5},{8,14},{10,8},{12,... | collective-permute-start | bytes 786440 | tf_op jit(solution)/shard_map/ppermute | solution.py:329
  51.8 0.2 convert_reduce_fusion.1
  52.0 0.1 add.124.bases_ref
  52.1 5.5 %collective-permute-done.2 = bf16[512,256]{1,0:T(8,128)(2,1)} collective-permute-done((bf16[512,256]{1,0:T(8,128)(2,1)S(1)}, bf16[512,256]{1,0:T(8,128)(2,1)}, u32[]{:S(2)}, u32[]{:S(2)}) %collective-permute-start.2) | collective-permute-done | bytes 262176 | tf_op jit(solution)/shard_map/ppermute | solution.py:329
  57.6 0.7 collective-permute-done.3
  58.3 1.1 %pad_maximum_fusion.far = bf16[1024,256]{1,0:T(8,128)(2,1)S(1)} fusion(bf16[512,256]{1,0:T(8,128)(2,1)} %collective-permute-done.3, bf16[512,256]{1,0:T(8,128)(2,1)} %collective-permute-done.2), kind=kLoop, calls=%fused_computation.1 | loop fusion | flops 1048576 | bytes 1048576 | tf_op jit(solution)/shard_map/concatenate | solution.py:346
  59.3 8.2 %pool.2 = (f32[64,2048]{1,0:T(8,128)S(1)}, f32[64,2048]{1,0:T(8,128)S(1)}, f32[1,2048]{1,0:T(1,128)S(1)}, bf16[4096,256]{1,0:T(8,128)(2,1)S(1)}, bf16[4096,256]{1,0:T(8,128)(2,1)S(1)}) custom-call(s32[1]{0:T(128)} %bitcast.core_ref, s32[32]{0:T(128)S(1)} %add.124.bases_ref, s32[128]{0:T(128)S(1)} %sub.3.starts_ref, s32[128]{0:T(128)S(1)} %reduce.ends_ref, ...), custom_call_target="tpu_custom_call" | custom-call | flops 4294967296 | bytes 5242880 | tf_op jit(solution)/shard_map/pool/pallas_call | solution.py:264
  67.6 1.2 %collective-permute-start.6 = (f32[64,2048]{1,0:T(8,128)S(1)}, f32[64,2048]{1,0:T(8,128)S(1)}, u32[]{:S(2)}, u32[]{:S(2)}) collective-permute-start(f32[64,2048]{1,0:T(8,128)S(1)} %get-tuple-element.23), channel_id=1, source_target_pairs={{0,8},{8,0},{1,9},{9,1},{2,10},{10,2},{3,11},{11,3},{4,12},{12,4},... | collective-permute-start | bytes 1572872 | tf_op jit(solution)/shard_map/ppermute | solution.py:329
  68.8 7.2 %pool.3 = (f32[64,2048]{1,0:T(8,128)S(1)}, f32[64,2048]{1,0:T(8,128)S(1)}, f32[1,2048]{1,0:T(1,128)S(1)}) custom-call(s32[1]{0:T(128)} %bitcast.core_ref, s32[32]{0:T(128)S(1)} %add.124.bases_ref, s32[128]{0:T(128)S(1)} %sub.3.starts_ref, s32[128]{0:T(128)S(1)} %reduce.ends_ref, s32[32]{0:T(128)S(1)} %get-tuple-element.27.first_ref, ...), custom_call_target="tpu_custom_call" | custom-call | flops 4294967296 | bytes 5242880 | tf_op jit(solution)/shard_map/pool/pallas_call | solution.py:264
  76.0 0.1 collective-permute-start.5
  76.1 1.9 %collective-permute-done.5.got_a = f32[64,2048]{1,0:T(8,128)S(1)} collective-permute-done((f32[64,2048]{1,0:T(8,128)S(1)}, f32[64,2048]{1,0:T(8,128)S(1)}, u32[]{:S(2)}, u32[]{:S(2)}) %collective-permute-start.5) | collective-permute-done | bytes 524320 | tf_op jit(solution)/shard_map/ppermute | solution.py:329
  78.0 0.1 combine.1
  78.1 0.9 convert_element_type.13
  79.0 6.0 %all-to-all-start.2 = ((f16[16,8,2048]{2,1,0:T(8,128)(2,1)}), f16[16,8,2048]{2,1,0:T(8,128)(2,1)S(1)}, u32[]{:S(2)}, u32[]{:S(2)}) async-start(f16[16,8,2048]{2,1,0:T(8,128)(2,1)} %convert_element_type.13), calls=%async_computation.2 | async-start | bytes 1048576 | tf_op jit(solution)/shard_map/all_to_all | solution.py:367
  85.0 0.1 copy.10.len_ref
  85.1 9.7 %all-to-all-done.2 = f16[16,8,2048]{2,1,0:T(8,128)(2,1)S(1)} async-done(((f16[16,8,2048]{2,1,0:T(8,128)(2,1)}), f16[16,8,2048]{2,1,0:T(8,128)(2,1)S(1)}, u32[]{:S(2)}, u32[]{:S(2)}) %all-to-all-start.2) | async-done | bytes 524320 | tf_op jit(solution)/shard_map/all_to_all | solution.py:367
  94.9 0.7 finish.1
  (17 shorter events, 0.3 us)
Async XLA Ops:
  0.0 22.8 %copy-start = (s32[32]{0:T(128)S(1)}, s32[32]{0:T(128)}, u32[]{:S(2)}) copy-start(s32[32]{0:T(128)} %slots_ref.1) | copy-start | bytes 388
  2.2 45.8 %copy-start.1 = (s32[128]{0:T(128)S(1)}, s32[128]{0:T(128)}, u32[]{:S(2)}) copy-start(s32[128]{0:T(128)} %param.7) | copy-start | bytes 1540
  25.8 20.7 %all-to-all-start.1 = ((bf16[16,256,128]{2,1,0:T(8,128)(2,1)}), bf16[16,256,128]{2,1,0:T(8,128)(2,1)S(1)}, u32[]{:S(2)}, u32[]{:S(2)}) async-start(bf16[16,256,128]{2,1,0:T(8,128)(2,1)} %get-tuple-element.16), calls=%async_computation.1 | async-start | bytes 2097152 | tf_op jit(solution)/shard_map/all_to_all | solution.py:348
  31.1 17.2 %collective-permute-start = (bf16[1024,256]{1,0:T(8,128)(2,1)}, bf16[1024,256]{1,0:T(8,128)(2,1)S(1)}, u32[]{:S(2)}, u32[]{:S(2)}) collective-permute-start(bf16[1024,256]{1,0:T(8,128)(2,1)} %get-tuple-element.15.own), channel_id=1, source_target_pairs={{0,2},{2,4},{4,6},{6,0},{1,3},{3,5},{5,7},{7,1},{8,10},{10,12},{12... | collective-permute-start | bytes 1572872 | tf_op jit(solution)/shard_map/ppermute | solution.py:329
  32.3 17.3 %collective-permute-start.1 = (bf16[1024,256]{1,0:T(8,128)(2,1)}, bf16[1024,256]{1,0:T(8,128)(2,1)S(1)}, u32[]{:S(2)}, u32[]{:S(2)}) collective-permute-start(bf16[1024,256]{1,0:T(8,128)(2,1)} %get-tuple-element.15.own), channel_id=1, source_target_pairs={{0,6},{2,0},{4,2},{6,4},{1,7},{3,1},{5,3},{7,5},{8,14},{10,8},{12,... | collective-permute-start | bytes 1572872 | tf_op jit(solution)/shard_map/ppermute | solution.py:329
  46.5 22.2 %collective-permute-start.4 = (bf16[16,256,128]{2,1,0:T(8,128)(2,1)S(1)}, bf16[16,256,128]{2,1,0:T(8,128)(2,1)S(1)}, u32[]{:S(2)}, u32[]{:S(2)}) collective-permute-start(bf16[16,256,128]{2,1,0:T(8,128)(2,1)S(1)} %all-to-all-done.1.q_ref), channel_id=1, source_target_pairs={{0,8},{8,0},{1,9},{9,1},{2,10},{10,2},{3,11},{11,3},{4,12},{12,4},... | collective-permute-start | bytes 3145736 | tf_op jit(solution)/shard_map/ppermute | solution.py:329
  48.4 9.2 %collective-permute-start.2 = (bf16[512,256]{1,0:T(8,128)(2,1)S(1)}, bf16[512,256]{1,0:T(8,128)(2,1)}, u32[]{:S(2)}, u32[]{:S(2)}) collective-permute-start(bf16[512,256]{1,0:T(8,128)(2,1)S(1)} %slice.8), channel_id=1, source_target_pairs={{0,2},{2,4},{4,6},{6,0},{1,3},{3,5},{5,7},{7,1},{8,10},{10,12},{12... | collective-permute-start | bytes 786440 | tf_op jit(solution)/shard_map/ppermute | solution.py:329
  50.4 7.9 %collective-permute-start.3 = (bf16[512,256]{1,0:T(8,128)(2,1)}, bf16[512,256]{1,0:T(8,128)(2,1)}, u32[]{:S(2)}, u32[]{:S(2)}) collective-permute-start(bf16[512,256]{1,0:T(8,128)(2,1)} %slice.9), channel_id=1, source_target_pairs={{0,6},{2,0},{4,2},{6,4},{1,7},{3,1},{5,3},{7,5},{8,14},{10,8},{12,... | collective-permute-start | bytes 786440 | tf_op jit(solution)/shard_map/ppermute | solution.py:329
  67.6 8.5 %collective-permute-start.6 = (f32[64,2048]{1,0:T(8,128)S(1)}, f32[64,2048]{1,0:T(8,128)S(1)}, u32[]{:S(2)}, u32[]{:S(2)}) collective-permute-start(f32[64,2048]{1,0:T(8,128)S(1)} %get-tuple-element.23), channel_id=1, source_target_pairs={{0,8},{8,0},{1,9},{9,1},{2,10},{10,2},{3,11},{11,3},{4,12},{12,4},... | collective-permute-start | bytes 1572872 | tf_op jit(solution)/shard_map/ppermute | solution.py:329
  76.0 2.0 %collective-permute-start.5 = (f32[64,2048]{1,0:T(8,128)S(1)}, f32[64,2048]{1,0:T(8,128)S(1)}, u32[]{:S(2)}, u32[]{:S(2)}) collective-permute-start(f32[64,2048]{1,0:T(8,128)S(1)} %get-tuple-element.20), channel_id=1, source_target_pairs={{0,8},{8,0},{1,9},{9,1},{2,10},{10,2},{3,11},{11,3},{4,12},{12,4},... | collective-permute-start | bytes 1572872 | tf_op jit(solution)/shard_map/ppermute | solution.py:329
  79.0 15.8 %all-to-all-start.2 = ((f16[16,8,2048]{2,1,0:T(8,128)(2,1)}), f16[16,8,2048]{2,1,0:T(8,128)(2,1)S(1)}, u32[]{:S(2)}, u32[]{:S(2)}) async-start(f16[16,8,2048]{2,1,0:T(8,128)(2,1)} %convert_element_type.13), calls=%async_computation.2 | async-start | bytes 1048576 | tf_op jit(solution)/shard_map/all_to_all | solution.py:367

commit v8 on v7

--- a/solution.py
+++ b/solution.py
@@ -161,6 +161,40 @@
     return jnp.where(inside, block.astype(f32), 0.0).astype(bf16)
 
 
+def docs_body(runs_ref, len_ref, bases_ref, starts_ref, ends_ref, first_ref, main_ref, last_ref):
+    lengths = len_ref[...].astype(f32)
+    row = lax.broadcasted_iota(jnp.int32, (DOCS, DOCS), 0)
+    col = lax.broadcasted_iota(jnp.int32, (DOCS, DOCS), 1)
+    column = jnp.sum(jnp.where(row == col, lengths, 0.0), axis=1, keepdims=True)
+    ends_column = jnp.sum(jnp.where(col <= row, lengths, 0.0), axis=1, keepdims=True)
+    ends = jnp.sum(jnp.where(row <= col, column, 0.0), axis=0, keepdims=True)
+    ends_ref[...] = ends.astype(jnp.int32)
+    starts_ref[...] = (ends - lengths).astype(jnp.int32)
+    group = lax.broadcasted_iota(jnp.int32, (1, NT_HERE // SUB), 1)
+    per_run = RUN // SUB
+    base = group % per_run * SUB
+    for i in range(4):
+        base = base + jnp.where(group // per_run == i, runs_ref[i], 0)
+    bases_ref[...] = base
+    for ref, o in ((first_ref, 0), (main_ref, SUB // 2), (last_ref, SUB - 1)):
+        before = ends_column <= (base + o).astype(f32)
+        ref[...] = jnp.sum(jnp.where(before, 1.0, 0.0), axis=0, keepdims=True).astype(jnp.int32)
+
+
+def docs_tables(runs, lengths):
+    vmem = pl.BlockSpec(memory_space=pltpu.VMEM)
+    groups = jax.ShapeDtypeStruct((1, NT_HERE // SUB), jnp.int32)
+    table = jax.ShapeDtypeStruct((1, DOCS), jnp.int32)
+    return pl.pallas_call(
+        docs_body,
+        in_specs=[pl.BlockSpec(memory_space=pltpu.SMEM), vmem],
+        out_specs=[vmem] * 6,
+        out_shape=[groups, table, table, groups, groups, groups],
+        compiler_params=params(16),
+        name="docs",
+    )(runs, lengths)
+
+
 def pool_first_body(core_ref, bases_ref, starts_ref, ends_ref, first_ref, main_ref, last_ref,
                     own, left, right, far, q_ref,
                     send_ref, keep_ref, weight_ref, tok, main_tok, qs, acc, *lists):
@@ -168,10 +202,10 @@
     for ref in (own, left, right, far):
         for r in range(0, RUN, SUB):
             block = ref[r : r + SUB, :]
-            k = main_ref[i]
+            k = main_ref[0, i]
             tok[i * SUB : (i + 1) * SUB, :] = block
             main_tok[i * SUB : (i + 1) * SUB, :] = rows_kept(
-                block, starts_ref[k] - bases_ref[i], ends_ref[k] - bases_ref[i]
+                block, starts_ref[0, k] - bases_ref[0, i], ends_ref[0, k] - bases_ref[0, i]
             )
             i += 1
     pool_columns(core_ref, bases_ref, starts_ref, ends_ref, first_ref, main_ref, last_ref,
@@ -213,11 +247,11 @@
         for j in range(BODY // TILE):
             i = block * (BODY // TILE) + j
             lhs = main_tok[pl.ds(pl.multiple_of(i * TILE, TILE), TILE), :]
-            add_sums(lhs, [main_ref[i * (TILE // SUB) + h] for h in range(TILE // SUB)])
+            add_sums(lhs, [main_ref[0, i * (TILE // SUB) + h] for h in range(TILE // SUB)])
 
     def list_docs(i, n):
         def list_doc(k, n):
-            other = k != main_ref[i]
+            other = k != main_ref[0, i]
 
             @pl.when(other)
             def _():
@@ -226,7 +260,7 @@
 
             return n + other.astype(jnp.int32)
 
-        return lax.fori_loop(first_ref[i], last_ref[i] + 1, list_doc, n)
+        return lax.fori_loop(first_ref[0, i], last_ref[0, i] + 1, list_doc, n)
 
     extra = lax.fori_loop(0, NT_HERE // SUB, list_docs, 0)
     half = SUB // 2
@@ -239,12 +273,12 @@
             at = jnp.minimum(e, extra - 1)
             i = sub_list[at]
             k = doc_list[at]
-            o = jnp.where(k > main_ref[i], half, 0)
-            base = bases_ref[i] + o
-            end = jnp.where(e < extra, ends_ref[k] - base, 0)
+            o = jnp.where(k > main_ref[0, i], half, 0)
+            base = bases_ref[0, i] + o
+            end = jnp.where(e < extra, ends_ref[0, k] - base, 0)
             rows = pl.multiple_of(i * SUB + o, half)
             picked[j * half : (j + 1) * half, :] = rows_kept(
-                tok[pl.ds(rows, half), :], starts_ref[k] - base, end
+                tok[pl.ds(rows, half), :], starts_ref[0, k] - base, end
             )
             docs.append(k)
         add_sums(picked[...], docs)
@@ -348,15 +382,10 @@
     qa = lax.all_to_all(copies, ("yl", "z", "yh"), split_axis=0, concat_axis=0, tiled=True)
     qb = shift(qa, "c", 1)
 
-    doc_ends = jnp.cumsum(doc_lengths)
-    doc_starts = doc_ends - doc_lengths
     xs = jnp.stack([x, (x + 3) % 4, (x + 1) % 4, (x + 2) % 4])
-    run_bases = (xs * 2 + yh) * (16 * RUN) + t * RUN
-    bases = (run_bases[:, None] + jnp.arange(RUN // SUB, dtype=jnp.int32) * SUB).reshape(-1)
-    spots = jnp.stack([bases, bases + SUB // 2, bases + (SUB - 1)])
-    first, main, last = jnp.sum(
-        doc_ends[None, None, :] <= spots[:, :, None], axis=2, dtype=jnp.int32
-    )
+    runs = (xs * 2 + yh) * (16 * RUN) + t * RUN
+    tables = docs_tables(runs, doc_lengths.reshape(1, DOCS))
+    bases, doc_starts, doc_ends, first, main, last = tables
 
     where = (core.reshape(1), bases, doc_starts, doc_ends, first, main, last)
     send_a, keep_a, weight_a, tok, main_tok = pool(where, (own, left, right, far), qa)

time: 97 us -> 96.4 us (level)
  transfers between devices with their start and end apart: 9 -> 9, of which waited for: 5 -> 5; matrix products, arithmetic and copies ran while one was open for 3% -> 2% of each run, Pallas kernels for 16% -> 17%
where the time goes in v8:
time: 96.4 us; the launch traced here: 95.1 us
  waiting for transfers between devices  30.1 us (31%)
  Pallas kernels  22 us (23%)
  blocking collectives  20.6 us (21%)
  starting transfers between devices  19.2 us (20%)
  other arithmetic  2.16 us (2%)
    all_to_all x1, blocking collectives, step(): lax.all_to_all(packed, ('yl', 'z', 'c'), split_axis=0, concat_axis=0, til...  20.6 us
    pallas_call x2, Pallas kernels, pool(): pl.pallas_call(pool_first_body if is_first else pool_columns, in_specs=[s...  15.3 us
    all_to_all x1, waiting for transfers between devices, step(): lax.all_to_all(copies, ('yl', 'z', 'yh'), split_axis=0, concat_axis=0, ti...  12.8 us
    all_to_all x1, waiting for transfers between devices, step(): lax.all_to_all(sums.astype(jnp.float16), ('yl', 'z', 'yh'), split_axis=0,...  9.7 us
    ppermute x7, starting transfers between devices, shift(): lax.ppermute(value, axis, [(i, (i + by) % size) for i in range(size)])  8.13 us
    ppermute x7, waiting for transfers between devices, shift(): lax.ppermute(value, axis, [(i, (i + by) % size) for i in range(size)])  7.58 us
    all_to_all x1, starting transfers between devices, step(): lax.all_to_all(sums.astype(jnp.float16), ('yl', 'z', 'yh'), split_axis=0,...  5.94 us
    all_to_all x1, starting transfers between devices, step(): lax.all_to_all(copies, ('yl', 'z', 'yh'), split_axis=0, concat_axis=0, ti...  5.14 us
  transfers between devices with their start and end apart: 9, of which 5 were waited for; matrix products, arithmetic and copies ran while one was open for 2% of the time, Pallas kernels for 17%

profile of v8, /device:TPU:1, one launch (start us, length us, event | category | flops | bytes accessed | tf_op | source)
XLA Modules:
  0.0 95.1 jit_solution(2592110494404426491)
XLA Ops:
  0.0 2.2 %pack.1 = bf16[16,16,1536]{2,1,0:T(8,128)(2,1)} custom-call(f32[16,16384]{1,0:T(8,128)} %train_hbm.1, f32[16,2048]{1,0:T(8,128)} %query_hbm.1), custom_call_target="tpu_custom_call" | custom-call | tf_op jit(solution)/shard_map/pack/pallas_call | solution.py:82
  2.2 20.6 %all_to_all.15.arr_ref = bf16[16,16,1536]{2,1,0:T(8,128)(2,1)S(1)} all-to-all(bf16[16,16,1536]{2,1,0:T(8,128)(2,1)} %pack.1), channel_id=1, replica_groups=mesh['yl'=2,'z'=4,'c'=2,'x'=4,'yh'=2] {'yl','z','c'}, dimensions={0} | all-to-all | bytes 1572864 | tf_op jit(solution)/shard_map/all_to_all | solution.py:373
  22.8 3.0 %centre.1 = (bf16[1024,256]{1,0:T(8,128)(2,1)}, bf16[16,256,128]{2,1,0:T(8,128)(2,1)}) custom-call(s32[32]{0:T(128)S(1)} %copy-done, bf16[16,16,1536]{2,1,0:T(8,128)(2,1)S(1)} %all_to_all.15.arr_ref), custom_call_target="tpu_custom_call" | custom-call | tf_op jit(solution)/shard_map/centre/pallas_call | solution.py:132
  25.9 5.1 %all-to-all-start.1 = ((bf16[16,256,128]{2,1,0:T(8,128)(2,1)}), bf16[16,256,128]{2,1,0:T(8,128)(2,1)S(1)}, u32[]{:S(2)}, u32[]{:S(2)}) async-start(bf16[16,256,128]{2,1,0:T(8,128)(2,1)} %get-tuple-element.28), calls=%async_computation.1 | async-start | bytes 2097152 | tf_op jit(solution)/shard_map/all_to_all | solution.py:382
  31.0 1.3 %collective-permute-start = (bf16[1024,256]{1,0:T(8,128)(2,1)}, bf16[1024,256]{1,0:T(8,128)(2,1)S(1)}, u32[]{:S(2)}, u32[]{:S(2)}) collective-permute-start(bf16[1024,256]{1,0:T(8,128)(2,1)} %get-tuple-element.27.own), channel_id=1, source_target_pairs={{0,2},{2,4},{4,6},{6,0},{1,3},{3,5},{5,7},{7,1},{8,10},{10,12},{12... | collective-permute-start | bytes 1572872 | tf_op jit(solution)/shard_map/ppermute | solution.py:363
  32.3 1.5 %collective-permute-start.1 = (bf16[1024,256]{1,0:T(8,128)(2,1)}, bf16[1024,256]{1,0:T(8,128)(2,1)S(1)}, u32[]{:S(2)}, u32[]{:S(2)}) collective-permute-start(bf16[1024,256]{1,0:T(8,128)(2,1)} %get-tuple-element.27.own), channel_id=1, source_target_pairs={{0,6},{2,0},{4,2},{6,4},{1,7},{3,1},{5,3},{7,5},{8,14},{10,8},{12,... | collective-permute-start | bytes 1572872 | tf_op jit(solution)/shard_map/ppermute | solution.py:363
  33.8 12.8 %all-to-all-done.1.q_ref = bf16[16,256,128]{2,1,0:T(8,128)(2,1)S(1)} async-done(((bf16[16,256,128]{2,1,0:T(8,128)(2,1)}), bf16[16,256,128]{2,1,0:T(8,128)(2,1)S(1)}, u32[]{:S(2)}, u32[]{:S(2)}) %all-to-all-start.1) | async-done | bytes 1048608 | tf_op jit(solution)/shard_map/all_to_all | solution.py:382
  46.6 1.4 %collective-permute-start.4 = (bf16[16,256,128]{2,1,0:T(8,128)(2,1)S(1)}, bf16[16,256,128]{2,1,0:T(8,128)(2,1)S(1)}, u32[]{:S(2)}, u32[]{:S(2)}) collective-permute-start(bf16[16,256,128]{2,1,0:T(8,128)(2,1)S(1)} %all-to-all-done.1.q_ref), channel_id=1, source_target_pairs={{0,8},{8,0},{1,9},{9,1},{2,10},{10,2},{3,11},{11,3},{4,12},{12,4},... | collective-permute-start | bytes 3145736 | tf_op jit(solution)/shard_map/ppermute | solution.py:363
  48.0 0.0 collective-permute-done.left
  48.0 1.3 %collective-permute-start.2 = (bf16[512,256]{1,0:T(8,128)(2,1)S(1)}, bf16[512,256]{1,0:T(8,128)(2,1)}, u32[]{:S(2)}, u32[]{:S(2)}) collective-permute-start(bf16[512,256]{1,0:T(8,128)(2,1)S(1)} %slice.8), channel_id=1, source_target_pairs={{0,2},{2,4},{4,6},{6,0},{1,3},{3,5},{5,7},{7,1},{8,10},{10,12},{12... | collective-permute-start | bytes 786440 | tf_op jit(solution)/shard_map/ppermute | solution.py:363
  49.3 0.0 collective-permute-done.1.right
  49.3 0.7 slice.9
  50.0 1.5 %collective-permute-start.3 = (bf16[512,256]{1,0:T(8,128)(2,1)}, bf16[512,256]{1,0:T(8,128)(2,1)}, u32[]{:S(2)}, u32[]{:S(2)}) collective-permute-start(bf16[512,256]{1,0:T(8,128)(2,1)} %slice.9), channel_id=1, source_target_pairs={{0,6},{2,0},{4,2},{6,4},{1,7},{3,1},{5,3},{7,5},{8,14},{10,8},{12,... | collective-permute-start | bytes 786440 | tf_op jit(solution)/shard_map/ppermute | solution.py:363
  51.5 0.1 multiply_add_fusion.runs_ref
  51.6 0.7 docs.1
  52.2 5.0 %collective-permute-done.2 = bf16[512,256]{1,0:T(8,128)(2,1)} collective-permute-done((bf16[512,256]{1,0:T(8,128)(2,1)S(1)}, bf16[512,256]{1,0:T(8,128)(2,1)}, u32[]{:S(2)}, u32[]{:S(2)}) %collective-permute-start.2) | collective-permute-done | bytes 262176 | tf_op jit(solution)/shard_map/ppermute | solution.py:363
  57.2 0.7 collective-permute-done.3
  57.9 1.1 %pad_maximum_fusion.far = bf16[1024,256]{1,0:T(8,128)(2,1)S(1)} fusion(bf16[512,256]{1,0:T(8,128)(2,1)} %collective-permute-done.3, bf16[512,256]{1,0:T(8,128)(2,1)} %collective-permute-done.2), kind=kLoop, calls=%fused_computation.1 | loop fusion | flops 1048576 | bytes 1048576 | tf_op jit(solution)/shard_map/concatenate | solution.py:380
  59.0 8.1 %pool.2 = (f32[64,2048]{1,0:T(8,128)S(1)}, f32[64,2048]{1,0:T(8,128)S(1)}, f32[1,2048]{1,0:T(1,128)S(1)}, bf16[4096,256]{1,0:T(8,128)(2,1)S(1)}, bf16[4096,256]{1,0:T(8,128)(2,1)S(1)}) custom-call(s32[1]{0:T(128)} %bitcast.core_ref, s32[1,32]{1,0:T(1,128)S(1)} %get-tuple-element.21.bases_ref, s32[1,128]{1,0:T(1,128)S(1)} %get-tuple-element.22.starts_ref, ...), custom_call_target="tpu_custom_call" | custom-call | flops 4294967296 | bytes 5242880 | tf_op jit(solution)/shard_map/pool/pallas_call | solution.py:298
  67.1 1.2 %collective-permute-start.6 = (f32[64,2048]{1,0:T(8,128)S(1)}, f32[64,2048]{1,0:T(8,128)S(1)}, u32[]{:S(2)}, u32[]{:S(2)}) collective-permute-start(f32[64,2048]{1,0:T(8,128)S(1)} %get-tuple-element.35), channel_id=1, source_target_pairs={{0,8},{8,0},{1,9},{9,1},{2,10},{10,2},{3,11},{11,3},{4,12},{12,4},... | collective-permute-start | bytes 1572872 | tf_op jit(solution)/shard_map/ppermute | solution.py:363
  68.3 0.0 collective-permute-done.4.q_ref
  68.3 7.1 %pool.3 = (f32[64,2048]{1,0:T(8,128)S(1)}, f32[64,2048]{1,0:T(8,128)S(1)}, f32[1,2048]{1,0:T(1,128)S(1)}) custom-call(s32[1]{0:T(128)} %bitcast.core_ref, s32[1,32]{1,0:T(1,128)S(1)} %get-tuple-element.21.bases_ref, s32[1,128]{1,0:T(1,128)S(1)} %get-tuple-element.22.starts_ref, s32[1,128]{1,0:T(1,128)S(1)} %get-tuple-element.23.ends_ref, ...), custom_call_target="tpu_custom_call" | custom-call | flops 4294967296 | bytes 5242880 | tf_op jit(solution)/shard_map/pool/pallas_call | solution.py:298
  75.4 0.1 collective-permute-start.5
  75.5 1.9 %collective-permute-done.5.got_a = f32[64,2048]{1,0:T(8,128)S(1)} collective-permute-done((f32[64,2048]{1,0:T(8,128)S(1)}, f32[64,2048]{1,0:T(8,128)S(1)}, u32[]{:S(2)}, u32[]{:S(2)}) %collective-permute-start.5) | collective-permute-done | bytes 524320 | tf_op jit(solution)/shard_map/ppermute | solution.py:363
  77.4 0.2 combine.1
  77.6 0.9 convert_element_type.9
  78.5 5.9 %all-to-all-start.2 = ((f16[16,8,2048]{2,1,0:T(8,128)(2,1)}), f16[16,8,2048]{2,1,0:T(8,128)(2,1)S(1)}, u32[]{:S(2)}, u32[]{:S(2)}) async-start(f16[16,8,2048]{2,1,0:T(8,128)(2,1)} %convert_element_type.9), calls=%async_computation.2 | async-start | bytes 1048576 | tf_op jit(solution)/shard_map/all_to_all | solution.py:396
  84.4 0.1 convert_bitcast_fusion
  84.5 0.1 copy.5.len_ref
  84.6 9.7 %all-to-all-done.2 = f16[16,8,2048]{2,1,0:T(8,128)(2,1)S(1)} async-done(((f16[16,8,2048]{2,1,0:T(8,128)(2,1)}), f16[16,8,2048]{2,1,0:T(8,128)(2,1)S(1)}, u32[]{:S(2)}, u32[]{:S(2)}) %all-to-all-start.2) | async-done | bytes 524320 | tf_op jit(solution)/shard_map/all_to_all | solution.py:396
  94.3 0.1 convert_reduce_fusion.total_ref
  94.3 0.7 finish.1
  (6 shorter events, 0.0 us)
Async XLA Ops:
  0.0 22.8 %copy-start = (s32[32]{0:T(128)S(1)}, s32[32]{0:T(128)}, u32[]{:S(2)}) copy-start(s32[32]{0:T(128)} %slots_ref.1) | copy-start | bytes 388
  22.8 28.7 %copy-start.1 = (s32[128]{0:T(128)S(1)}, s32[128]{0:T(128)}, u32[]{:S(2)}) copy-start(s32[128]{0:T(128)} %param.7) | copy-start | bytes 1540
  25.9 20.7 %all-to-all-start.1 = ((bf16[16,256,128]{2,1,0:T(8,128)(2,1)}), bf16[16,256,128]{2,1,0:T(8,128)(2,1)S(1)}, u32[]{:S(2)}, u32[]{:S(2)}) async-start(bf16[16,256,128]{2,1,0:T(8,128)(2,1)} %get-tuple-element.28), calls=%async_computation.1 | async-start | bytes 2097152 | tf_op jit(solution)/shard_map/all_to_all | solution.py:382
  31.0 17.0 %collective-permute-start = (bf16[1024,256]{1,0:T(8,128)(2,1)}, bf16[1024,256]{1,0:T(8,128)(2,1)S(1)}, u32[]{:S(2)}, u32[]{:S(2)}) collective-permute-start(bf16[1024,256]{1,0:T(8,128)(2,1)} %get-tuple-element.27.own), channel_id=1, source_target_pairs={{0,2},{2,4},{4,6},{6,0},{1,3},{3,5},{5,7},{7,1},{8,10},{10,12},{12... | collective-permute-start | bytes 1572872 | tf_op jit(solution)/shard_map/ppermute | solution.py:363
  32.3 17.0 %collective-permute-start.1 = (bf16[1024,256]{1,0:T(8,128)(2,1)}, bf16[1024,256]{1,0:T(8,128)(2,1)S(1)}, u32[]{:S(2)}, u32[]{:S(2)}) collective-permute-start(bf16[1024,256]{1,0:T(8,128)(2,1)} %get-tuple-element.27.own), channel_id=1, source_target_pairs={{0,6},{2,0},{4,2},{6,4},{1,7},{3,1},{5,3},{7,5},{8,14},{10,8},{12,... | collective-permute-start | bytes 1572872 | tf_op jit(solution)/shard_map/ppermute | solution.py:363
  46.6 21.7 %collective-permute-start.4 = (bf16[16,256,128]{2,1,0:T(8,128)(2,1)S(1)}, bf16[16,256,128]{2,1,0:T(8,128)(2,1)S(1)}, u32[]{:S(2)}, u32[]{:S(2)}) collective-permute-start(bf16[16,256,128]{2,1,0:T(8,128)(2,1)S(1)} %all-to-all-done.1.q_ref), channel_id=1, source_target_pairs={{0,8},{8,0},{1,9},{9,1},{2,10},{10,2},{3,11},{11,3},{4,12},{12,4},... | collective-permute-start | bytes 3145736 | tf_op jit(solution)/shard_map/ppermute | solution.py:363
  48.0 9.2 %collective-permute-start.2 = (bf16[512,256]{1,0:T(8,128)(2,1)S(1)}, bf16[512,256]{1,0:T(8,128)(2,1)}, u32[]{:S(2)}, u32[]{:S(2)}) collective-permute-start(bf16[512,256]{1,0:T(8,128)(2,1)S(1)} %slice.8), channel_id=1, source_target_pairs={{0,2},{2,4},{4,6},{6,0},{1,3},{3,5},{5,7},{7,1},{8,10},{10,12},{12... | collective-permute-start | bytes 786440 | tf_op jit(solution)/shard_map/ppermute | solution.py:363
  50.0 7.9 %collective-permute-start.3 = (bf16[512,256]{1,0:T(8,128)(2,1)}, bf16[512,256]{1,0:T(8,128)(2,1)}, u32[]{:S(2)}, u32[]{:S(2)}) collective-permute-start(bf16[512,256]{1,0:T(8,128)(2,1)} %slice.9), channel_id=1, source_target_pairs={{0,6},{2,0},{4,2},{6,4},{1,7},{3,1},{5,3},{7,5},{8,14},{10,8},{12,... | collective-permute-start | bytes 786440 | tf_op jit(solution)/shard_map/ppermute | solution.py:363
  67.1 8.4 %collective-permute-start.6 = (f32[64,2048]{1,0:T(8,128)S(1)}, f32[64,2048]{1,0:T(8,128)S(1)}, u32[]{:S(2)}, u32[]{:S(2)}) collective-permute-start(f32[64,2048]{1,0:T(8,128)S(1)} %get-tuple-element.35), channel_id=1, source_target_pairs={{0,8},{8,0},{1,9},{9,1},{2,10},{10,2},{3,11},{11,3},{4,12},{12,4},... | collective-permute-start | bytes 1572872 | tf_op jit(solution)/shard_map/ppermute | solution.py:363
  75.4 2.0 %collective-permute-start.5 = (f32[64,2048]{1,0:T(8,128)S(1)}, f32[64,2048]{1,0:T(8,128)S(1)}, u32[]{:S(2)}, u32[]{:S(2)}) collective-permute-start(f32[64,2048]{1,0:T(8,128)S(1)} %get-tuple-element.32), channel_id=1, source_target_pairs={{0,8},{8,0},{1,9},{9,1},{2,10},{10,2},{3,11},{11,3},{4,12},{12,4},... | collective-permute-start | bytes 1572872 | tf_op jit(solution)/shard_map/ppermute | solution.py:363
  78.5 15.8 %all-to-all-start.2 = ((f16[16,8,2048]{2,1,0:T(8,128)(2,1)}), f16[16,8,2048]{2,1,0:T(8,128)(2,1)S(1)}, u32[]{:S(2)}, u32[]{:S(2)}) async-start(f16[16,8,2048]{2,1,0:T(8,128)(2,1)} %convert_element_type.9), calls=%async_computation.2 | async-start | bytes 1048576 | tf_op jit(solution)/shard_map/all_to_all | solution.py:396

commit v9 on v8

--- a/solution.py
+++ b/solution.py
@@ -161,6 +161,27 @@
     return jnp.where(inside, block.astype(f32), 0.0).astype(bf16)
 
 
+def weights_body(qa_ref, qb_ref, weight_a, weight_b):
+    for q_ref, weight_ref in ((qa_ref, weight_a), (qb_ref, weight_b)):
+        for i in range(16):
+            o = (i % 2 * 8 + i // 2) * QPIECE
+            wide = q_ref[i].astype(f32)
+            scale = lax.rsqrt(jnp.sum(wide * wide, axis=0, keepdims=True) / (DRAWS - 1) + EPS)
+            weight_ref[:, o : o + QPIECE] = (scale / (DRAWS - 1)) * (scale / (DRAWS - 1))
+
+
+def weights(qa, qb):
+    vmem = pl.BlockSpec(memory_space=pltpu.VMEM)
+    return pl.pallas_call(
+        weights_body,
+        in_specs=[vmem] * 2,
+        out_shape=[jax.ShapeDtypeStruct((1, NQ_HALF), f32)] * 2,
+        out_specs=[vmem] * 2,
+        compiler_params=params(16),
+        name="weights",
+    )(qa, qb)
+
+
 def docs_body(runs_ref, len_ref, bases_ref, starts_ref, ends_ref, first_ref, main_ref, last_ref):
     lengths = len_ref[...].astype(f32)
     row = lax.broadcasted_iota(jnp.int32, (DOCS, DOCS), 0)
@@ -197,7 +218,7 @@
 
 def pool_first_body(core_ref, bases_ref, starts_ref, ends_ref, first_ref, main_ref, last_ref,
                     own, left, right, far, q_ref,
-                    send_ref, keep_ref, weight_ref, tok, main_tok, qs, acc, *lists):
+                    send_ref, keep_ref, tok, main_tok, qs, acc, *lists):
     i = 0
     for ref in (own, left, right, far):
         for r in range(0, RUN, SUB):
@@ -209,20 +230,16 @@
             )
             i += 1
     pool_columns(core_ref, bases_ref, starts_ref, ends_ref, first_ref, main_ref, last_ref,
-                 tok, main_tok, q_ref, send_ref, keep_ref, weight_ref, qs, acc, *lists)
+                 tok, main_tok, q_ref, send_ref, keep_ref, qs, acc, *lists)
 
 
 def pool_columns(core_ref, bases_ref, starts_ref, ends_ref, first_ref, main_ref, last_ref,
-                 tok, main_tok, q_ref, send_ref, keep_ref, weight_ref, qs, acc,
+                 tok, main_tok, q_ref, send_ref, keep_ref, qs, acc,
                  picked, sub_list, doc_list):
     core = core_ref[0]
     for i in range(16):
         o = (i % 2 * 8 + i // 2) * QPIECE
-        block = q_ref[i]
-        qs[:, o : o + QPIECE] = block
-        wide = block.astype(f32)
-        scale = lax.rsqrt(jnp.sum(wide * wide, axis=0, keepdims=True) / (DRAWS - 1) + EPS)
-        weight_ref[:, o : o + QPIECE] = (scale / (DRAWS - 1)) * (scale / (DRAWS - 1))
+        qs[:, o : o + QPIECE] = q_ref[i]
     acc[...] = jnp.zeros_like(acc)
 
     def row_of(k):
@@ -291,7 +308,7 @@
     smem = pl.BlockSpec(memory_space=pltpu.SMEM)
     vmem = pl.BlockSpec(memory_space=pltpu.VMEM)
     sums = jax.ShapeDtypeStruct((DOCS // 2, NQ_HALF), f32)
-    shapes = [sums, sums, jax.ShapeDtypeStruct((1, NQ_HALF), f32)]
+    shapes = [sums, sums]
     is_first = len(tokens) == 4
     if is_first:
         shapes += [jax.ShapeDtypeStruct((NT_HERE, DRAWS), bf16)] * 2
@@ -388,10 +405,11 @@
     bases, doc_starts, doc_ends, first, main, last = tables
 
     where = (core.reshape(1), bases, doc_starts, doc_ends, first, main, last)
-    send_a, keep_a, weight_a, tok, main_tok = pool(where, (own, left, right, far), qa)
+    send_a, keep_a, tok, main_tok = pool(where, (own, left, right, far), qa)
     cross_a = shift(send_a, "c", 1)
-    send_b, keep_b, weight_b = pool(where, (tok, main_tok), qb)
+    send_b, keep_b = pool(where, (tok, main_tok), qb)
     cross_b = shift(send_b, "c", 1)
+    weight_a, weight_b = weights(qa, qb)
     sums = combine(keep_a, cross_b, weight_a, keep_b, cross_a, weight_b)
     pieces = lax.all_to_all(
         sums.astype(jnp.float16), ("yl", "z", "yh"), split_axis=0, concat_axis=0, tiled=True

time: 96.4 us -> 96.2 us (level)
  no operation moved by 1% of the time
where the time goes in v9:
time: 96.2 us; the launch traced here: 94.8 us
  waiting for transfers between devices  29.6 us (31%)
  Pallas kernels  22.2 us (23%)
  blocking collectives  20.6 us (21%)
  starting transfers between devices  19.2 us (20%)
  other arithmetic  2.16 us (2%)
    all_to_all x1, blocking collectives, step(): lax.all_to_all(packed, ('yl', 'z', 'c'), split_axis=0, concat_axis=0, til...  20.6 us
    pallas_call x2, Pallas kernels, pool(): pl.pallas_call(pool_first_body if is_first else pool_columns, in_specs=[s...  15.1 us
    all_to_all x1, waiting for transfers between devices, step(): lax.all_to_all(copies, ('yl', 'z', 'yh'), split_axis=0, concat_axis=0, ti...  12.8 us
    all_to_all x1, waiting for transfers between devices, step(): lax.all_to_all(sums.astype(jnp.float16), ('yl', 'z', 'yh'), split_axis=0,...  9.7 us
    ppermute x7, starting transfers between devices, shift(): lax.ppermute(value, axis, [(i, (i + by) % size) for i in range(size)])  8.14 us
    ppermute x7, waiting for transfers between devices, shift(): lax.ppermute(value, axis, [(i, (i + by) % size) for i in range(size)])  7.11 us
    all_to_all x1, starting transfers between devices, step(): lax.all_to_all(sums.astype(jnp.float16), ('yl', 'z', 'yh'), split_axis=0,...  5.94 us
    all_to_all x1, starting transfers between devices, step(): lax.all_to_all(copies, ('yl', 'z', 'yh'), split_axis=0, concat_axis=0, ti...  5.14 us
  transfers between devices with their start and end apart: 9, of which 5 were waited for; matrix products, arithmetic and copies ran while one was open for 2% of the time, Pallas kernels for 17%

profile of v9, /device:TPU:1, one launch (start us, length us, event | category | flops | bytes accessed | tf_op | source)
XLA Modules:
  0.0 94.8 jit_solution(3955992995973444975)
XLA Ops:
  0.0 2.1 %pack.1 = bf16[16,16,1536]{2,1,0:T(8,128)(2,1)} custom-call(f32[16,16384]{1,0:T(8,128)} %train_hbm.1, f32[16,2048]{1,0:T(8,128)} %query_hbm.1), custom_call_target="tpu_custom_call" | custom-call | tf_op jit(solution)/shard_map/pack/pallas_call | solution.py:82
  2.2 20.6 %all_to_all.15.arr_ref = bf16[16,16,1536]{2,1,0:T(8,128)(2,1)S(1)} all-to-all(bf16[16,16,1536]{2,1,0:T(8,128)(2,1)} %pack.1), channel_id=1, replica_groups=mesh['yl'=2,'z'=4,'c'=2,'x'=4,'yh'=2] {'yl','z','c'}, dimensions={0} | all-to-all | bytes 1572864 | tf_op jit(solution)/shard_map/all_to_all | solution.py:390
  22.8 3.0 %centre.1 = (bf16[1024,256]{1,0:T(8,128)(2,1)}, bf16[16,256,128]{2,1,0:T(8,128)(2,1)}) custom-call(s32[32]{0:T(128)S(1)} %copy-done, bf16[16,16,1536]{2,1,0:T(8,128)(2,1)S(1)} %all_to_all.15.arr_ref), custom_call_target="tpu_custom_call" | custom-call | tf_op jit(solution)/shard_map/centre/pallas_call | solution.py:132
  25.8 5.1 %all-to-all-start.1 = ((bf16[16,256,128]{2,1,0:T(8,128)(2,1)}), bf16[16,256,128]{2,1,0:T(8,128)(2,1)S(1)}, u32[]{:S(2)}, u32[]{:S(2)}) async-start(bf16[16,256,128]{2,1,0:T(8,128)(2,1)} %get-tuple-element.28), calls=%async_computation.1 | async-start | bytes 2097152 | tf_op jit(solution)/shard_map/all_to_all | solution.py:399
  31.0 1.3 %collective-permute-start = (bf16[1024,256]{1,0:T(8,128)(2,1)}, bf16[1024,256]{1,0:T(8,128)(2,1)S(1)}, u32[]{:S(2)}, u32[]{:S(2)}) collective-permute-start(bf16[1024,256]{1,0:T(8,128)(2,1)} %get-tuple-element.27.own), channel_id=1, source_target_pairs={{0,2},{2,4},{4,6},{6,0},{1,3},{3,5},{5,7},{7,1},{8,10},{10,12},{12... | collective-permute-start | bytes 1572872 | tf_op jit(solution)/shard_map/ppermute | solution.py:380
  32.3 1.5 %collective-permute-start.1 = (bf16[1024,256]{1,0:T(8,128)(2,1)}, bf16[1024,256]{1,0:T(8,128)(2,1)S(1)}, u32[]{:S(2)}, u32[]{:S(2)}) collective-permute-start(bf16[1024,256]{1,0:T(8,128)(2,1)} %get-tuple-element.27.own), channel_id=1, source_target_pairs={{0,6},{2,0},{4,2},{6,4},{1,7},{3,1},{5,3},{7,5},{8,14},{10,8},{12,... | collective-permute-start | bytes 1572872 | tf_op jit(solution)/shard_map/ppermute | solution.py:380
  33.7 12.8 %all-to-all-done.1.q_ref.qa_ref = bf16[16,256,128]{2,1,0:T(8,128)(2,1)S(1)} async-done(((bf16[16,256,128]{2,1,0:T(8,128)(2,1)}), bf16[16,256,128]{2,1,0:T(8,128)(2,1)S(1)}, u32[]{:S(2)}, u32[]{:S(2)}) %all-to-all-start.1) | async-done | bytes 1048608 | tf_op jit(solution)/shard_map/all_to_all | solution.py:399
  46.6 1.4 %collective-permute-start.4 = (bf16[16,256,128]{2,1,0:T(8,128)(2,1)S(1)}, bf16[16,256,128]{2,1,0:T(8,128)(2,1)S(1)}, u32[]{:S(2)}, u32[]{:S(2)}) collective-permute-start(bf16[16,256,128]{2,1,0:T(8,128)(2,1)S(1)} %all-to-all-done.1.q_ref.qa_ref), channel_id=1, source_target_pairs={{0,8},{8,0},{1,9},{9,1},{2,10},{10,2},{3,11},{11,3},{4,12},{12,4},... | collective-permute-start | bytes 3145736 | tf_op jit(solution)/shard_map/ppermute | solution.py:380
  47.9 0.0 collective-permute-done.left
  48.0 1.3 %collective-permute-start.2 = (bf16[512,256]{1,0:T(8,128)(2,1)S(1)}, bf16[512,256]{1,0:T(8,128)(2,1)}, u32[]{:S(2)}, u32[]{:S(2)}) collective-permute-start(bf16[512,256]{1,0:T(8,128)(2,1)S(1)} %slice.8), channel_id=1, source_target_pairs={{0,2},{2,4},{4,6},{6,0},{1,3},{3,5},{5,7},{7,1},{8,10},{10,12},{12... | collective-permute-start | bytes 786440 | tf_op jit(solution)/shard_map/ppermute | solution.py:380
  49.3 0.7 slice.9
  50.0 1.5 %collective-permute-start.3 = (bf16[512,256]{1,0:T(8,128)(2,1)}, bf16[512,256]{1,0:T(8,128)(2,1)}, u32[]{:S(2)}, u32[]{:S(2)}) collective-permute-start(bf16[512,256]{1,0:T(8,128)(2,1)} %slice.9), channel_id=1, source_target_pairs={{0,6},{2,0},{4,2},{6,4},{1,7},{3,1},{5,3},{7,5},{8,14},{10,8},{12,... | collective-permute-start | bytes 786440 | tf_op jit(solution)/shard_map/ppermute | solution.py:380
  51.5 0.1 multiply_add_fusion.runs_ref
  51.5 0.7 docs.1
  52.2 5.0 %collective-permute-done.2 = bf16[512,256]{1,0:T(8,128)(2,1)} collective-permute-done((bf16[512,256]{1,0:T(8,128)(2,1)S(1)}, bf16[512,256]{1,0:T(8,128)(2,1)}, u32[]{:S(2)}, u32[]{:S(2)}) %collective-permute-start.2) | collective-permute-done | bytes 262176 | tf_op jit(solution)/shard_map/ppermute | solution.py:380
  57.2 0.7 collective-permute-done.3
  57.9 1.1 %pad_maximum_fusion.far = bf16[1024,256]{1,0:T(8,128)(2,1)S(1)} fusion(bf16[512,256]{1,0:T(8,128)(2,1)} %collective-permute-done.3, bf16[512,256]{1,0:T(8,128)(2,1)} %collective-permute-done.2), kind=kLoop, calls=%fused_computation.1 | loop fusion | flops 1048576 | bytes 1048576 | tf_op jit(solution)/shard_map/concatenate | solution.py:397
  59.0 8.0 %pool.2 = (f32[64,2048]{1,0:T(8,128)S(1)}, f32[64,2048]{1,0:T(8,128)S(1)}, bf16[4096,256]{1,0:T(8,128)(2,1)S(1)}, bf16[4096,256]{1,0:T(8,128)(2,1)S(1)}) custom-call(s32[1]{0:T(128)} %bitcast.core_ref, s32[1,32]{1,0:T(1,128)S(1)} %get-tuple-element.21.bases_ref, s32[1,128]{1,0:T(1,128)S(1)} %get-tuple-element.22.starts_ref, ...), custom_call_target="tpu_custom_call" | custom-call | flops 4294967296 | bytes 5242880 | tf_op jit(solution)/shard_map/pool/pallas_call | solution.py:315
  67.0 1.2 %collective-permute-start.6 = (f32[64,2048]{1,0:T(8,128)S(1)}, f32[64,2048]{1,0:T(8,128)S(1)}, u32[]{:S(2)}, u32[]{:S(2)}) collective-permute-start(f32[64,2048]{1,0:T(8,128)S(1)} %get-tuple-element.35), channel_id=1, source_target_pairs={{0,8},{8,0},{1,9},{9,1},{2,10},{10,2},{3,11},{11,3},{4,12},{12,4},... | collective-permute-start | bytes 1572872 | tf_op jit(solution)/shard_map/ppermute | solution.py:380
  68.2 0.0 collective-permute-done.4.q_ref.qb_ref
  68.2 7.0 %pool.3 = (f32[64,2048]{1,0:T(8,128)S(1)}, f32[64,2048]{1,0:T(8,128)S(1)}) custom-call(s32[1]{0:T(128)} %bitcast.core_ref, s32[1,32]{1,0:T(1,128)S(1)} %get-tuple-element.21.bases_ref, s32[1,128]{1,0:T(1,128)S(1)} %get-tuple-element.22.starts_ref, s32[1,128]{1,0:T(1,128)S(1)} %get-tuple-element.23.ends_ref, s32[1,32]{1,0:T(1,128)S(1)} %get-tuple-element.24.first_ref, ...), custom_call_target="tpu_custom_call" | custom-call | flops 4294967296 | bytes 5242880 | tf_op jit(solution)/shard_map/pool/pallas_call | solution.py:315
  75.2 0.1 collective-permute-start.5
  75.3 0.5 weights.1
  75.8 1.4 %collective-permute-done.5.got_a = f32[64,2048]{1,0:T(8,128)S(1)} collective-permute-done((f32[64,2048]{1,0:T(8,128)S(1)}, f32[64,2048]{1,0:T(8,128)S(1)}, u32[]{:S(2)}, u32[]{:S(2)}) %collective-permute-start.5) | collective-permute-done | bytes 524320 | tf_op jit(solution)/shard_map/ppermute | solution.py:380
  77.2 0.2 combine.1
  77.4 0.9 convert_element_type.9
  78.2 5.9 %all-to-all-start.2 = ((f16[16,8,2048]{2,1,0:T(8,128)(2,1)}), f16[16,8,2048]{2,1,0:T(8,128)(2,1)S(1)}, u32[]{:S(2)}, u32[]{:S(2)}) async-start(f16[16,8,2048]{2,1,0:T(8,128)(2,1)} %convert_element_type.9), calls=%async_computation.2 | async-start | bytes 1048576 | tf_op jit(solution)/shard_map/all_to_all | solution.py:414
  84.2 0.1 convert_bitcast_fusion
  84.3 0.1 copy.5.len_ref
  84.3 9.7 %all-to-all-done.2 = f16[16,8,2048]{2,1,0:T(8,128)(2,1)S(1)} async-done(((f16[16,8,2048]{2,1,0:T(8,128)(2,1)}), f16[16,8,2048]{2,1,0:T(8,128)(2,1)S(1)}, u32[]{:S(2)}, u32[]{:S(2)}) %all-to-all-start.2) | async-done | bytes 524320 | tf_op jit(solution)/shard_map/all_to_all | solution.py:414
  94.0 0.1 convert_reduce_fusion.total_ref
  94.1 0.7 finish.1
  (7 shorter events, 0.0 us)
Async XLA Ops:
  0.0 22.8 %copy-start = (s32[32]{0:T(128)S(1)}, s32[32]{0:T(128)}, u32[]{:S(2)}) copy-start(s32[32]{0:T(128)} %slots_ref.1) | copy-start | bytes 388
  22.8 28.7 %copy-start.1 = (s32[128]{0:T(128)S(1)}, s32[128]{0:T(128)}, u32[]{:S(2)}) copy-start(s32[128]{0:T(128)} %param.7) | copy-start | bytes 1540
  25.8 20.7 %all-to-all-start.1 = ((bf16[16,256,128]{2,1,0:T(8,128)(2,1)}), bf16[16,256,128]{2,1,0:T(8,128)(2,1)S(1)}, u32[]{:S(2)}, u32[]{:S(2)}) async-start(bf16[16,256,128]{2,1,0:T(8,128)(2,1)} %get-tuple-element.28), calls=%async_computation.1 | async-start | bytes 2097152 | tf_op jit(solution)/shard_map/all_to_all | solution.py:399
  31.0 17.0 %collective-permute-start = (bf16[1024,256]{1,0:T(8,128)(2,1)}, bf16[1024,256]{1,0:T(8,128)(2,1)S(1)}, u32[]{:S(2)}, u32[]{:S(2)}) collective-permute-start(bf16[1024,256]{1,0:T(8,128)(2,1)} %get-tuple-element.27.own), channel_id=1, source_target_pairs={{0,2},{2,4},{4,6},{6,0},{1,3},{3,5},{5,7},{7,1},{8,10},{10,12},{12... | collective-permute-start | bytes 1572872 | tf_op jit(solution)/shard_map/ppermute | solution.py:380
  32.3 17.0 %collective-permute-start.1 = (bf16[1024,256]{1,0:T(8,128)(2,1)}, bf16[1024,256]{1,0:T(8,128)(2,1)S(1)}, u32[]{:S(2)}, u32[]{:S(2)}) collective-permute-start(bf16[1024,256]{1,0:T(8,128)(2,1)} %get-tuple-element.27.own), channel_id=1, source_target_pairs={{0,6},{2,0},{4,2},{6,4},{1,7},{3,1},{5,3},{7,5},{8,14},{10,8},{12,... | collective-permute-start | bytes 1572872 | tf_op jit(solution)/shard_map/ppermute | solution.py:380
  46.6 21.6 %collective-permute-start.4 = (bf16[16,256,128]{2,1,0:T(8,128)(2,1)S(1)}, bf16[16,256,128]{2,1,0:T(8,128)(2,1)S(1)}, u32[]{:S(2)}, u32[]{:S(2)}) collective-permute-start(bf16[16,256,128]{2,1,0:T(8,128)(2,1)S(1)} %all-to-all-done.1.q_ref.qa_ref), channel_id=1, source_target_pairs={{0,8},{8,0},{1,9},{9,1},{2,10},{10,2},{3,11},{11,3},{4,12},{12,4},... | collective-permute-start | bytes 3145736 | tf_op jit(solution)/shard_map/ppermute | solution.py:380
  48.0 9.2 %collective-permute-start.2 = (bf16[512,256]{1,0:T(8,128)(2,1)S(1)}, bf16[512,256]{1,0:T(8,128)(2,1)}, u32[]{:S(2)}, u32[]{:S(2)}) collective-permute-start(bf16[512,256]{1,0:T(8,128)(2,1)S(1)} %slice.8), channel_id=1, source_target_pairs={{0,2},{2,4},{4,6},{6,0},{1,3},{3,5},{5,7},{7,1},{8,10},{10,12},{12... | collective-permute-start | bytes 786440 | tf_op jit(solution)/shard_map/ppermute | solution.py:380
  50.0 7.9 %collective-permute-start.3 = (bf16[512,256]{1,0:T(8,128)(2,1)}, bf16[512,256]{1,0:T(8,128)(2,1)}, u32[]{:S(2)}, u32[]{:S(2)}) collective-permute-start(bf16[512,256]{1,0:T(8,128)(2,1)} %slice.9), channel_id=1, source_target_pairs={{0,6},{2,0},{4,2},{6,4},{1,7},{3,1},{5,3},{7,5},{8,14},{10,8},{12,... | collective-permute-start | bytes 786440 | tf_op jit(solution)/shard_map/ppermute | solution.py:380
  67.0 8.8 %collective-permute-start.6 = (f32[64,2048]{1,0:T(8,128)S(1)}, f32[64,2048]{1,0:T(8,128)S(1)}, u32[]{:S(2)}, u32[]{:S(2)}) collective-permute-start(f32[64,2048]{1,0:T(8,128)S(1)} %get-tuple-element.35), channel_id=1, source_target_pairs={{0,8},{8,0},{1,9},{9,1},{2,10},{10,2},{3,11},{11,3},{4,12},{12,4},... | collective-permute-start | bytes 1572872 | tf_op jit(solution)/shard_map/ppermute | solution.py:380
  75.2 2.0 %collective-permute-start.5 = (f32[64,2048]{1,0:T(8,128)S(1)}, f32[64,2048]{1,0:T(8,128)S(1)}, u32[]{:S(2)}, u32[]{:S(2)}) collective-permute-start(f32[64,2048]{1,0:T(8,128)S(1)} %get-tuple-element.32), channel_id=1, source_target_pairs={{0,8},{8,0},{1,9},{9,1},{2,10},{10,2},{3,11},{11,3},{4,12},{12,4},... | collective-permute-start | bytes 1572872 | tf_op jit(solution)/shard_map/ppermute | solution.py:380
  78.2 15.8 %all-to-all-start.2 = ((f16[16,8,2048]{2,1,0:T(8,128)(2,1)}), f16[16,8,2048]{2,1,0:T(8,128)(2,1)S(1)}, u32[]{:S(2)}, u32[]{:S(2)}) async-start(f16[16,8,2048]{2,1,0:T(8,128)(2,1)} %convert_element_type.9), calls=%async_computation.2 | async-start | bytes 1048576 | tf_op jit(solution)/shard_map/all_to_all | solution.py:414

commit v10 on v9

--- a/solution.py
+++ b/solution.py
@@ -182,6 +182,23 @@
     )(qa, qb)
 
 
+def touch_body(lo_ref, hi_ref, out_ref):
+    out_ref[...] = (lo_ref[:8, :].astype(f32) + hi_ref[:8, :].astype(f32))[:1, :128]
+
+
+def touch(lo, hi):
+    rows = pl.BlockSpec((16, DRAWS), lambda i: (0, 0))
+    return pl.pallas_call(
+        touch_body,
+        grid=(1,),
+        in_specs=[rows] * 2,
+        out_specs=pl.BlockSpec((1, 128), lambda i: (0, 0)),
+        out_shape=jax.ShapeDtypeStruct((1, 128), f32),
+        compiler_params=params(4),
+        name="touch",
+    )(lo, hi)
+
+
 def docs_body(runs_ref, len_ref, bases_ref, starts_ref, ends_ref, first_ref, main_ref, last_ref):
     lengths = len_ref[...].astype(f32)
     row = lax.broadcasted_iota(jnp.int32, (DOCS, DOCS), 0)
@@ -216,12 +233,12 @@
     )(runs, lengths)
 
 
-def pool_first_body(core_ref, bases_ref, starts_ref, ends_ref, first_ref, main_ref, last_ref,
-                    own, left, right, far, q_ref,
+def pool_first_body(seen_ref, core_ref, bases_ref, starts_ref, ends_ref, first_ref, main_ref, last_ref,
+                    own, left, right, far_lo, far_hi, q_ref,
                     send_ref, keep_ref, tok, main_tok, qs, acc, *lists):
     i = 0
-    for ref in (own, left, right, far):
-        for r in range(0, RUN, SUB):
+    for ref in (own, left, right, far_lo, far_hi):
+        for r in range(0, ref.shape[0], SUB):
             block = ref[r : r + SUB, :]
             k = main_ref[0, i]
             tok[i * SUB : (i + 1) * SUB, :] = block
@@ -229,11 +246,11 @@
                 block, starts_ref[0, k] - bases_ref[0, i], ends_ref[0, k] - bases_ref[0, i]
             )
             i += 1
-    pool_columns(core_ref, bases_ref, starts_ref, ends_ref, first_ref, main_ref, last_ref,
+    pool_columns(seen_ref, core_ref, bases_ref, starts_ref, ends_ref, first_ref, main_ref, last_ref,
                  tok, main_tok, q_ref, send_ref, keep_ref, qs, acc, *lists)
 
 
-def pool_columns(core_ref, bases_ref, starts_ref, ends_ref, first_ref, main_ref, last_ref,
+def pool_columns(seen_ref, core_ref, bases_ref, starts_ref, ends_ref, first_ref, main_ref, last_ref,
                  tok, main_tok, q_ref, send_ref, keep_ref, qs, acc,
                  picked, sub_list, doc_list):
     core = core_ref[0]
@@ -309,7 +326,7 @@
     vmem = pl.BlockSpec(memory_space=pltpu.VMEM)
     sums = jax.ShapeDtypeStruct((DOCS // 2, NQ_HALF), f32)
     shapes = [sums, sums]
-    is_first = len(tokens) == 4
+    is_first = len(tokens) == 5
     if is_first:
         shapes += [jax.ShapeDtypeStruct((NT_HERE, DRAWS), bf16)] * 2
     return pl.pallas_call(
@@ -394,7 +411,7 @@
     right = shift(own, "x", -1)
     far_lo = shift(left[: RUN // 2], "x", 1)
     far_hi = shift(right[RUN // 2 :], "x", -1)
-    far = jnp.concatenate([far_lo, far_hi])
+    arrived_both = touch(far_lo, far_hi)
 
     qa = lax.all_to_all(copies, ("yl", "z", "yh"), split_axis=0, concat_axis=0, tiled=True)
     qb = shift(qa, "c", 1)
@@ -404,8 +421,8 @@
     tables = docs_tables(runs, doc_lengths.reshape(1, DOCS))
     bases, doc_starts, doc_ends, first, main, last = tables
 
-    where = (core.reshape(1), bases, doc_starts, doc_ends, first, main, last)
-    send_a, keep_a, tok, main_tok = pool(where, (own, left, right, far), qa)
+    where = (arrived_both, core.reshape(1), bases, doc_starts, doc_ends, first, main, last)
+    send_a, keep_a, tok, main_tok = pool(where, (own, left, right, far_lo, far_hi), qa)
     cross_a = shift(send_a, "c", 1)
     send_b, keep_b = pool(where, (tok, main_tok), qb)
     cross_b = shift(send_b, "c", 1)

time: 96.2 us -> 95.9 us (level)
  other arithmetic: 2.16 us -> 1.09 us
    concatenate x1 -> x0, other arithmetic: 1.06 us -> none  [step(): far = jnp.concatenate([far_lo, far_hi])]
where the time goes in v10:
time: 95.9 us; the launch traced here: 94.6 us
  waiting for transfers between devices  29.5 us (31%)
  Pallas kernels  22.2 us (23%)
  blocking collectives  20.6 us (21%)
  starting transfers between devices  19.2 us (20%)
  local copies, waits for them, and re-layouts  1.78 us (2%)
  other arithmetic  1.09 us (1%)
    all_to_all x1, blocking collectives, step(): lax.all_to_all(packed, ('yl', 'z', 'c'), split_axis=0, concat_axis=0, til...  20.6 us
    pallas_call x2, Pallas kernels, pool(): pl.pallas_call(pool_first_body if is_first else pool_columns, in_specs=[s...  15 us
    all_to_all x1, waiting for transfers between devices, step(): lax.all_to_all(copies, ('yl', 'z', 'yh'), split_axis=0, concat_axis=0, ti...  12.8 us
    all_to_all x1, waiting for transfers between devices, step(): lax.all_to_all(sums.astype(jnp.float16), ('yl', 'z', 'yh'), split_axis=0,...  9.7 us
    ppermute x7, starting transfers between devices, shift(): lax.ppermute(value, axis, [(i, (i + by) % size) for i in range(size)])  8.14 us
    ppermute x7, waiting for transfers between devices, shift(): lax.ppermute(value, axis, [(i, (i + by) % size) for i in range(size)])  7 us
    all_to_all x1, starting transfers between devices, step(): lax.all_to_all(sums.astype(jnp.float16), ('yl', 'z', 'yh'), split_axis=0,...  5.94 us
    all_to_all x1, starting transfers between devices, step(): lax.all_to_all(copies, ('yl', 'z', 'yh'), split_axis=0, concat_axis=0, ti...  5.14 us
  transfers between devices with their start and end apart: 9, of which 5 were waited for; matrix products, arithmetic and copies ran while one was open for 2% of the time, Pallas kernels for 17%

profile of v10, /device:TPU:1, one launch (start us, length us, event | category | flops | bytes accessed | tf_op | source)
XLA Modules:
  0.0 94.6 jit_solution(9694933550243394972)
XLA Ops:
  0.0 2.1 %pack.1 = bf16[16,16,1536]{2,1,0:T(8,128)(2,1)} custom-call(f32[16,16384]{1,0:T(8,128)} %train_hbm.1, f32[16,2048]{1,0:T(8,128)} %query_hbm.1), custom_call_target="tpu_custom_call" | custom-call | tf_op jit(solution)/shard_map/pack/pallas_call | solution.py:82
  2.2 20.6 %all_to_all.15.arr_ref = bf16[16,16,1536]{2,1,0:T(8,128)(2,1)S(1)} all-to-all(bf16[16,16,1536]{2,1,0:T(8,128)(2,1)} %pack.1), channel_id=1, replica_groups=mesh['yl'=2,'z'=4,'c'=2,'x'=4,'yh'=2] {'yl','z','c'}, dimensions={0} | all-to-all | bytes 1572864 | tf_op jit(solution)/shard_map/all_to_all | solution.py:407
  22.8 3.0 %centre.1 = (bf16[1024,256]{1,0:T(8,128)(2,1)}, bf16[16,256,128]{2,1,0:T(8,128)(2,1)}) custom-call(s32[32]{0:T(128)S(1)} %copy-done, bf16[16,16,1536]{2,1,0:T(8,128)(2,1)S(1)} %all_to_all.15.arr_ref), custom_call_target="tpu_custom_call" | custom-call | tf_op jit(solution)/shard_map/centre/pallas_call | solution.py:132
  25.8 5.1 %all-to-all-start.1 = ((bf16[16,256,128]{2,1,0:T(8,128)(2,1)}), bf16[16,256,128]{2,1,0:T(8,128)(2,1)S(1)}, u32[]{:S(2)}, u32[]{:S(2)}) async-start(bf16[16,256,128]{2,1,0:T(8,128)(2,1)} %get-tuple-element.28), calls=%async_computation.1 | async-start | bytes 2097152 | tf_op jit(solution)/shard_map/all_to_all | solution.py:416
  31.0 1.3 %collective-permute-start = (bf16[1024,256]{1,0:T(8,128)(2,1)}, bf16[1024,256]{1,0:T(8,128)(2,1)S(1)}, u32[]{:S(2)}, u32[]{:S(2)}) collective-permute-start(bf16[1024,256]{1,0:T(8,128)(2,1)} %get-tuple-element.21.own), channel_id=1, source_target_pairs={{0,2},{2,4},{4,6},{6,0},{1,3},{3,5},{5,7},{7,1},{8,10},{10,12},{12... | collective-permute-start | bytes 1572872 | tf_op jit(solution)/shard_map/ppermute | solution.py:397
  32.3 1.5 %collective-permute-start.2 = (bf16[1024,256]{1,0:T(8,128)(2,1)}, bf16[1024,256]{1,0:T(8,128)(2,1)}, u32[]{:S(2)}, u32[]{:S(2)}) collective-permute-start(bf16[1024,256]{1,0:T(8,128)(2,1)} %get-tuple-element.21.own), channel_id=1, source_target_pairs={{0,6},{2,0},{4,2},{6,4},{1,7},{3,1},{5,3},{7,5},{8,14},{10,8},{12,... | collective-permute-start | bytes 1572872 | tf_op jit(solution)/shard_map/ppermute | solution.py:397
  33.7 12.8 %all-to-all-done.1.q_ref.qa_ref = bf16[16,256,128]{2,1,0:T(8,128)(2,1)S(1)} async-done(((bf16[16,256,128]{2,1,0:T(8,128)(2,1)}), bf16[16,256,128]{2,1,0:T(8,128)(2,1)S(1)}, u32[]{:S(2)}, u32[]{:S(2)}) %all-to-all-start.1) | async-done | bytes 1048608 | tf_op jit(solution)/shard_map/all_to_all | solution.py:416
  46.6 1.4 %collective-permute-start.4 = (bf16[16,256,128]{2,1,0:T(8,128)(2,1)S(1)}, bf16[16,256,128]{2,1,0:T(8,128)(2,1)S(1)}, u32[]{:S(2)}, u32[]{:S(2)}) collective-permute-start(bf16[16,256,128]{2,1,0:T(8,128)(2,1)S(1)} %all-to-all-done.1.q_ref.qa_ref), channel_id=1, source_target_pairs={{0,8},{8,0},{1,9},{9,1},{2,10},{10,2},{3,11},{11,3},{4,12},{12,4},... | collective-permute-start | bytes 3145736 | tf_op jit(solution)/shard_map/ppermute | solution.py:397
  47.9 0.0 collective-permute-done.left
  48.0 1.3 %collective-permute-start.1 = (bf16[512,256]{1,0:T(8,128)(2,1)S(1)}, bf16[512,256]{1,0:T(8,128)(2,1)S(1)}, u32[]{:S(2)}, u32[]{:S(2)}) collective-permute-start(bf16[512,256]{1,0:T(8,128)(2,1)S(1)} %slice.8), channel_id=1, source_target_pairs={{0,2},{2,4},{4,6},{6,0},{1,3},{3,5},{5,7},{7,1},{8,10},{10,12},{12... | collective-permute-start | bytes 786440 | tf_op jit(solution)/shard_map/ppermute | solution.py:397
  49.3 0.0 collective-permute-done.2.right
  49.3 1.7 %slice.9 = bf16[512,256]{1,0:T(8,128)(2,1)} slice(bf16[1024,256]{1,0:T(8,128)(2,1)} %collective-permute-done.2.right), slice={[512:1024], [0:256]} | slice | bytes 524288 | tf_op jit(solution)/shard_map/slice | solution.py:413
  50.9 1.5 %collective-permute-start.3 = (bf16[512,256]{1,0:T(8,128)(2,1)}, bf16[512,256]{1,0:T(8,128)(2,1)S(1)}, u32[]{:S(2)}, u32[]{:S(2)}) collective-permute-start(bf16[512,256]{1,0:T(8,128)(2,1)} %slice.9), channel_id=1, source_target_pairs={{0,6},{2,0},{4,2},{6,4},{1,7},{3,1},{5,3},{7,5},{8,14},{10,8},{12,... | collective-permute-start | bytes 786440 | tf_op jit(solution)/shard_map/ppermute | solution.py:397
  52.4 0.1 multiply_add_fusion.runs_ref
  52.5 0.7 docs.1
  53.1 4.0 %collective-permute-done.1.lo_ref.far_lo = bf16[512,256]{1,0:T(8,128)(2,1)S(1)} collective-permute-done((bf16[512,256]{1,0:T(8,128)(2,1)S(1)}, bf16[512,256]{1,0:T(8,128)(2,1)S(1)}, u32[]{:S(2)}, u32[]{:S(2)}) %collective-permute-start.1) | collective-permute-done | bytes 262176 | tf_op jit(solution)/shard_map/ppermute | solution.py:397
  57.1 1.6 %collective-permute-done.3.hi_ref.far_hi = bf16[512,256]{1,0:T(8,128)(2,1)S(1)} collective-permute-done((bf16[512,256]{1,0:T(8,128)(2,1)}, bf16[512,256]{1,0:T(8,128)(2,1)S(1)}, u32[]{:S(2)}, u32[]{:S(2)}) %collective-permute-start.3) | collective-permute-done | bytes 262176 | tf_op jit(solution)/shard_map/ppermute | solution.py:397
  58.7 8.1 %pool.2 = (f32[64,2048]{1,0:T(8,128)S(1)}, f32[64,2048]{1,0:T(8,128)S(1)}, bf16[4096,256]{1,0:T(8,128)(2,1)S(1)}, bf16[4096,256]{1,0:T(8,128)(2,1)S(1)}) custom-call(f32[1,128]{1,0:T(1,128)S(1)} %touch.1.seen_ref, s32[1]{0:T(128)} %bitcast.core_ref, s32[1,32]{1,0:T(1,128)S(1)} %get-tuple-element.22.bases_ref, s32[1,128]{1,0:T(1,128)S(1)} %get-tuple-element.23.starts_ref, ...), custom_call_target="tpu_custom_call" | custom-call | flops 4294967296 | bytes 5242880 | tf_op jit(solution)/shard_map/pool/pallas_call | solution.py:332
  66.8 1.2 %collective-permute-start.6 = (f32[64,2048]{1,0:T(8,128)S(1)}, f32[64,2048]{1,0:T(8,128)S(1)}, u32[]{:S(2)}, u32[]{:S(2)}) collective-permute-start(f32[64,2048]{1,0:T(8,128)S(1)} %get-tuple-element.35), channel_id=1, source_target_pairs={{0,8},{8,0},{1,9},{9,1},{2,10},{10,2},{3,11},{11,3},{4,12},{12,4},... | collective-permute-start | bytes 1572872 | tf_op jit(solution)/shard_map/ppermute | solution.py:397
  68.0 0.0 collective-permute-done.4.q_ref.qb_ref
  68.0 6.9 %pool.3 = (f32[64,2048]{1,0:T(8,128)S(1)}, f32[64,2048]{1,0:T(8,128)S(1)}) custom-call(f32[1,128]{1,0:T(1,128)S(1)} %touch.1.seen_ref, s32[1]{0:T(128)} %bitcast.core_ref, s32[1,32]{1,0:T(1,128)S(1)} %get-tuple-element.22.bases_ref, s32[1,128]{1,0:T(1,128)S(1)} %get-tuple-element.23.starts_ref, s32[1,128]{1,0:T(1,128)S(1)} %get-tuple-element.24.ends_ref, ...), custom_call_target="tpu_custom_call" | custom-call | flops 4294967296 | bytes 5242880 | tf_op jit(solution)/shard_map/pool/pallas_call | solution.py:332
  75.0 0.1 collective-permute-start.5
  75.1 0.5 weights.1
  75.5 1.4 %collective-permute-done.5.got_a = f32[64,2048]{1,0:T(8,128)S(1)} collective-permute-done((f32[64,2048]{1,0:T(8,128)S(1)}, f32[64,2048]{1,0:T(8,128)S(1)}, u32[]{:S(2)}, u32[]{:S(2)}) %collective-permute-start.5) | collective-permute-done | bytes 524320 | tf_op jit(solution)/shard_map/ppermute | solution.py:397
  77.0 0.1 combine.1
  77.1 0.9 convert_element_type.9
  77.9 5.9 %all-to-all-start.2 = ((f16[16,8,2048]{2,1,0:T(8,128)(2,1)}), f16[16,8,2048]{2,1,0:T(8,128)(2,1)S(1)}, u32[]{:S(2)}, u32[]{:S(2)}) async-start(f16[16,8,2048]{2,1,0:T(8,128)(2,1)} %convert_element_type.9), calls=%async_computation.2 | async-start | bytes 1048576 | tf_op jit(solution)/shard_map/all_to_all | solution.py:431
  83.9 0.1 convert_bitcast_fusion
  84.0 0.1 copy.5.len_ref
  84.1 9.7 %all-to-all-done.2 = f16[16,8,2048]{2,1,0:T(8,128)(2,1)S(1)} async-done(((f16[16,8,2048]{2,1,0:T(8,128)(2,1)}), f16[16,8,2048]{2,1,0:T(8,128)(2,1)S(1)}, u32[]{:S(2)}, u32[]{:S(2)}) %all-to-all-start.2) | async-done | bytes 524320 | tf_op jit(solution)/shard_map/all_to_all | solution.py:431
  93.8 0.1 convert_reduce_fusion.total_ref
  93.8 0.7 finish.1
  (7 shorter events, 0.0 us)
Async XLA Ops:
  0.0 22.8 %copy-start = (s32[32]{0:T(128)S(1)}, s32[32]{0:T(128)}, u32[]{:S(2)}) copy-start(s32[32]{0:T(128)} %slots_ref.1) | copy-start | bytes 388
  22.8 29.7 %copy-start.1 = (s32[128]{0:T(128)S(1)}, s32[128]{0:T(128)}, u32[]{:S(2)}) copy-start(s32[128]{0:T(128)} %param.7) | copy-start | bytes 1540
  25.8 20.7 %all-to-all-start.1 = ((bf16[16,256,128]{2,1,0:T(8,128)(2,1)}), bf16[16,256,128]{2,1,0:T(8,128)(2,1)S(1)}, u32[]{:S(2)}, u32[]{:S(2)}) async-start(bf16[16,256,128]{2,1,0:T(8,128)(2,1)} %get-tuple-element.28), calls=%async_computation.1 | async-start | bytes 2097152 | tf_op jit(solution)/shard_map/all_to_all | solution.py:416
  31.0 17.0 %collective-permute-start = (bf16[1024,256]{1,0:T(8,128)(2,1)}, bf16[1024,256]{1,0:T(8,128)(2,1)S(1)}, u32[]{:S(2)}, u32[]{:S(2)}) collective-permute-start(bf16[1024,256]{1,0:T(8,128)(2,1)} %get-tuple-element.21.own), channel_id=1, source_target_pairs={{0,2},{2,4},{4,6},{6,0},{1,3},{3,5},{5,7},{7,1},{8,10},{10,12},{12... | collective-permute-start | bytes 1572872 | tf_op jit(solution)/shard_map/ppermute | solution.py:397
  32.3 17.0 %collective-permute-start.2 = (bf16[1024,256]{1,0:T(8,128)(2,1)}, bf16[1024,256]{1,0:T(8,128)(2,1)}, u32[]{:S(2)}, u32[]{:S(2)}) collective-permute-start(bf16[1024,256]{1,0:T(8,128)(2,1)} %get-tuple-element.21.own), channel_id=1, source_target_pairs={{0,6},{2,0},{4,2},{6,4},{1,7},{3,1},{5,3},{7,5},{8,14},{10,8},{12,... | collective-permute-start | bytes 1572872 | tf_op jit(solution)/shard_map/ppermute | solution.py:397
  46.6 21.5 %collective-permute-start.4 = (bf16[16,256,128]{2,1,0:T(8,128)(2,1)S(1)}, bf16[16,256,128]{2,1,0:T(8,128)(2,1)S(1)}, u32[]{:S(2)}, u32[]{:S(2)}) collective-permute-start(bf16[16,256,128]{2,1,0:T(8,128)(2,1)S(1)} %all-to-all-done.1.q_ref.qa_ref), channel_id=1, source_target_pairs={{0,8},{8,0},{1,9},{9,1},{2,10},{10,2},{3,11},{11,3},{4,12},{12,4},... | collective-permute-start | bytes 3145736 | tf_op jit(solution)/shard_map/ppermute | solution.py:397
  48.0 9.1 %collective-permute-start.1 = (bf16[512,256]{1,0:T(8,128)(2,1)S(1)}, bf16[512,256]{1,0:T(8,128)(2,1)S(1)}, u32[]{:S(2)}, u32[]{:S(2)}) collective-permute-start(bf16[512,256]{1,0:T(8,128)(2,1)S(1)} %slice.8), channel_id=1, source_target_pairs={{0,2},{2,4},{4,6},{6,0},{1,3},{3,5},{5,7},{7,1},{8,10},{10,12},{12... | collective-permute-start | bytes 786440 | tf_op jit(solution)/shard_map/ppermute | solution.py:397
  50.9 7.8 %collective-permute-start.3 = (bf16[512,256]{1,0:T(8,128)(2,1)}, bf16[512,256]{1,0:T(8,128)(2,1)S(1)}, u32[]{:S(2)}, u32[]{:S(2)}) collective-permute-start(bf16[512,256]{1,0:T(8,128)(2,1)} %slice.9), channel_id=1, source_target_pairs={{0,6},{2,0},{4,2},{6,4},{1,7},{3,1},{5,3},{7,5},{8,14},{10,8},{12,... | collective-permute-start | bytes 786440 | tf_op jit(solution)/shard_map/ppermute | solution.py:397
  66.8 8.7 %collective-permute-start.6 = (f32[64,2048]{1,0:T(8,128)S(1)}, f32[64,2048]{1,0:T(8,128)S(1)}, u32[]{:S(2)}, u32[]{:S(2)}) collective-permute-start(f32[64,2048]{1,0:T(8,128)S(1)} %get-tuple-element.35), channel_id=1, source_target_pairs={{0,8},{8,0},{1,9},{9,1},{2,10},{10,2},{3,11},{11,3},{4,12},{12,4},... | collective-permute-start | bytes 1572872 | tf_op jit(solution)/shard_map/ppermute | solution.py:397
  75.0 2.0 %collective-permute-start.5 = (f32[64,2048]{1,0:T(8,128)S(1)}, f32[64,2048]{1,0:T(8,128)S(1)}, u32[]{:S(2)}, u32[]{:S(2)}) collective-permute-start(f32[64,2048]{1,0:T(8,128)S(1)} %get-tuple-element.32), channel_id=1, source_target_pairs={{0,8},{8,0},{1,9},{9,1},{2,10},{10,2},{3,11},{11,3},{4,12},{12,4},... | collective-permute-start | bytes 1572872 | tf_op jit(solution)/shard_map/ppermute | solution.py:397
  77.9 15.8 %all-to-all-start.2 = ((f16[16,8,2048]{2,1,0:T(8,128)(2,1)}), f16[16,8,2048]{2,1,0:T(8,128)(2,1)S(1)}, u32[]{:S(2)}, u32[]{:S(2)}) async-start(f16[16,8,2048]{2,1,0:T(8,128)(2,1)} %convert_element_type.9), calls=%async_computation.2 | async-start | bytes 1048576 | tf_op jit(solution)/shard_map/all_to_all | solution.py:431
